TPU v7x, 8 devices: a whole 2x2x1 slice. The times are simulated.
8 devices in a mesh: ep: 2 (over z, y), dp: 4 (over x, core).
Axes of the slice: x: 2, y: 2, z: 1, core: 2. Of those that a mesh axis runs over, the one named last changes fastest.
Arguments:
- tokens: bfloat16 [4096, 512], P(('dp', 'ep'))
- dy_out: bfloat16 [4096, 512], P(('dp', 'ep'))
- dense_w1: bfloat16 [512, 512], replicated
- route_idx1: int32 [4096, 8], P(('dp', 'ep'))
- route_gate1: float32 [4096, 8], P(('dp', 'ep'))
- w_gate1: bfloat16 [128, 512, 192], P('ep')
- w_up1: bfloat16 [128, 512, 192], P('ep')
- w_down1: bfloat16 [128, 192, 512], P('ep')
- dense_w2: bfloat16 [512, 512], replicated
- route_idx2: int32 [4096, 8], P(('dp', 'ep'))
- route_gate2: float32 [4096, 8], P(('dp', 'ep'))
- w_gate2: bfloat16 [128, 512, 192], P('ep')
- w_up2: bfloat16 [128, 512, 192], P('ep')
- w_down2: bfloat16 [128, 192, 512], P('ep')
Outputs:
- output 1: bfloat16 [4096, 512], P(('dp', 'ep'))
- output 2: bfloat16 [512, 512], P(('dp', 'ep'))
- output 3: bfloat16 [128, 512, 192], P('ep', 'dp')
- output 4: bfloat16 [128, 512, 192], P('ep', 'dp')
- output 5: bfloat16 [128, 192, 512], P('ep', None, 'dp')
- output 6: bfloat16 [512, 512], P(('dp', 'ep'))
- output 7: bfloat16 [128, 512, 192], P('ep', 'dp')
- output 8: bfloat16 [128, 512, 192], P('ep', 'dp')
- output 9: bfloat16 [128, 192, 512], P('ep', None, 'dp')
All inputs are finite; a program needn't handle non-finite values.
Results may differ from a plain program's by a relative error of at most 0.02.
Values are sent between devices in bfloat16 or wider.
A program may use at most 1 GiB of HBM per device.

v0:
```python
import jax
import jax.numpy as jnp
from jax import lax
from jax.sharding import PartitionSpec as P


def copy_rows(route_idx, n_exp, capacity):
    flat_exp = route_idx.reshape(-1)
    n_copies = flat_exp.shape[0]
    order = jnp.argsort(flat_exp, stable=True).astype(jnp.int32)
    sorted_exp = jnp.take(flat_exp, order)
    counts = jnp.zeros((n_exp,), jnp.int32).at[flat_exp].add(1)
    starts = jnp.cumsum(counts, dtype=jnp.int32) - counts
    dest_row = sorted_exp * capacity + jnp.arange(n_copies, dtype=jnp.int32) - jnp.take(starts, sorted_exp)
    return jnp.zeros((n_copies,), jnp.int32).at[order].set(dest_row).reshape(route_idx.shape)


def row_fill(flat_pos, values, n_rows, empty):
    return jnp.full((n_rows,), empty, values.dtype).at[flat_pos.reshape(-1)].set(values.reshape(-1))


def dispatch(x_loc, dense_w, route_idx, n_exp):
    n_tok, top_k = route_idx.shape
    capacity = 2 * n_tok * top_k // n_exp
    mixed = (x_loc.astype(jnp.float32) + jnp.dot(x_loc, dense_w, preferred_element_type=jnp.float32)).astype(jnp.bfloat16)
    flat_pos = copy_rows(route_idx, n_exp, capacity)
    tok_ids = jnp.broadcast_to(jnp.arange(n_tok, dtype=jnp.int32)[:, None], (n_tok, top_k))
    row_tok = row_fill(flat_pos, tok_ids, n_exp * capacity, n_tok)
    send = jnp.take(mixed, row_tok, axis=0, mode='fill', fill_value=0).reshape(n_exp, capacity, -1)
    recv = lax.all_to_all(send, 'ep', 0, 1, tiled=True)
    return mixed, flat_pos, row_tok, recv


def expert_hidden(recv, w_gate, w_up):
    a_pre = jnp.einsum('ecd,edf->ecf', recv, w_gate, preferred_element_type=jnp.float32)
    b_pre = jnp.einsum('ecd,edf->ecf', recv, w_up, preferred_element_type=jnp.float32)
    hidden = (jax.nn.silu(a_pre) * b_pre).astype(jnp.bfloat16)
    return a_pre, b_pre, hidden


def combine(mixed, hidden, w_down, flat_pos, route_gate):
    expert_out = jnp.einsum('ecf,efd->ecd', hidden, w_down, preferred_element_type=jnp.float32).astype(jnp.bfloat16)
    returned = lax.all_to_all(expert_out, 'ep', 1, 0, tiled=True)
    returned = returned.reshape(-1, returned.shape[-1])
    picked = jnp.take(returned, flat_pos, axis=0)
    return (mixed.astype(jnp.float32) + jnp.sum(route_gate[:, :, None] * picked, axis=1)).astype(jnp.bfloat16)


def layer_backward(grad_y, x_loc, dense_w, route_gate, w_gate, w_up, w_down, n_exp, flat_pos, row_tok, recv, a_pre, b_pre, hidden):
    n_rows = row_tok.shape[0]
    capacity = n_rows // n_exp
    row_gate = row_fill(flat_pos, route_gate, n_rows, 0.0)
    grad_send = (jnp.take(grad_y, row_tok, axis=0, mode='fill', fill_value=0) * row_gate[:, None]).astype(jnp.bfloat16)
    grad_out = lax.all_to_all(grad_send.reshape(n_exp, capacity, -1), 'ep', 0, 1, tiled=True)
    grad_hidden = jnp.einsum('ecd,efd->ecf', grad_out, w_down, preferred_element_type=jnp.float32).astype(jnp.bfloat16)
    grad_down = jnp.einsum('ecf,ecd->efd', hidden, grad_out, preferred_element_type=jnp.float32)
    sigma_a = jax.nn.sigmoid(a_pre)
    hidden_wide = grad_hidden.astype(jnp.float32)
    grad_a = (hidden_wide * b_pre * sigma_a * (1.0 + a_pre * (1.0 - sigma_a))).astype(jnp.bfloat16)
    grad_b = (hidden_wide * a_pre * sigma_a).astype(jnp.bfloat16)
    grad_gate = jnp.einsum('ecd,ecf->edf', recv, grad_a, preferred_element_type=jnp.float32)
    grad_up = jnp.einsum('ecd,ecf->edf', recv, grad_b, preferred_element_type=jnp.float32)
    grad_recv = (jnp.einsum('ecf,edf->ecd', grad_a, w_gate, preferred_element_type=jnp.float32)
                 + jnp.einsum('ecf,edf->ecd', grad_b, w_up, preferred_element_type=jnp.float32)).astype(jnp.bfloat16)
    grad_back = lax.all_to_all(grad_recv, 'ep', 1, 0, tiled=True)
    grad_back = grad_back.reshape(-1, grad_back.shape[-1])
    grad_picked = jnp.take(grad_back, flat_pos, axis=0)
    grad_mixed = (grad_y.astype(jnp.float32) + jnp.sum(grad_picked, axis=1, dtype=jnp.float32)).astype(jnp.bfloat16)
    grad_dense = jnp.einsum('td,te->de', x_loc, grad_mixed, preferred_element_type=jnp.float32)
    grad_x = (grad_mixed.astype(jnp.float32) + jnp.einsum('te,de->td', grad_mixed, dense_w, preferred_element_type=jnp.float32)).astype(jnp.bfloat16)
    return grad_x, (grad_dense, grad_gate, grad_up, grad_down)


def reduce_grads(partials):
    grad_dense, grad_gate, grad_up, grad_down = [piece.astype(jnp.bfloat16) for piece in partials]
    return (lax.psum_scatter(grad_dense, ('dp', 'ep'), scatter_dimension=0, tiled=True),
            lax.psum_scatter(grad_gate, 'dp', scatter_dimension=1, tiled=True),
            lax.psum_scatter(grad_up, 'dp', scatter_dimension=1, tiled=True),
            lax.psum_scatter(grad_down, 'dp', scatter_dimension=2, tiled=True))


def solution(mesh):
    ep_size = mesh.shape['ep']
    tok_spec = P(('dp', 'ep'), None)
    exp_spec = P('ep', None, None)
    layer_specs = (P(None, None), tok_spec, tok_spec, exp_spec, exp_spec, exp_spec)
    grad_specs = (P(('dp', 'ep'), None), P('ep', 'dp', None), P('ep', 'dp', None), P('ep', None, 'dp'))

    def local_step(tokens, dy_out, dense_w1, route_idx1, route_gate1, w_gate1, w_up1, w_down1, dense_w2, route_idx2, route_gate2, w_gate2, w_up2, w_down2):
        n_exp = w_gate1.shape[0] * ep_size
        mixed_one, place_one, rowtok_one, recv_one = dispatch(tokens, dense_w1, route_idx1, n_exp)
        a_one, b_one, hid_one = expert_hidden(recv_one, w_gate1, w_up1)
        mid_tok = combine(mixed_one, hid_one, w_down1, place_one, route_gate1)
        mixed_two, place_two, rowtok_two, recv_two = dispatch(mid_tok, dense_w2, route_idx2, n_exp)
        a_two, b_two, hid_two = expert_hidden(recv_two, w_gate2, w_up2)
        grad_mid, parts_two = layer_backward(dy_out, mid_tok, dense_w2, route_gate2, w_gate2, w_up2, w_down2, n_exp, place_two, rowtok_two, recv_two, a_two, b_two, hid_two)
        grads_two = reduce_grads(parts_two)
        grad_tok, parts_one = layer_backward(grad_mid, tokens, dense_w1, route_gate1, w_gate1, w_up1, w_down1, n_exp, place_one, rowtok_one, recv_one, a_one, b_one, hid_one)
        grads_one = reduce_grads(parts_one)
        return (grad_tok,) + grads_one + grads_two

    return jax.shard_map(local_step, mesh=mesh, in_specs=(tok_spec, tok_spec) + layer_specs + layer_specs,
                         out_specs=(tok_spec,) + grad_specs + grad_specs, check_vma=False)
```

profile of v0, /device:TPU:0, one launch (start us, length us, event | category | flops | bytes accessed | tf_op | source)
XLA Modules:
  0.0 1713.7 jit_solution(14790647576330511391)
XLA Ops:
  37.3 28.8 %scatter_custom_fusion.4 = s32[128]{0:T(128)S(1)} fusion(s32[4096]{0:T(1024)S(1)} %bitcast.140, s32[4096]{0:T(1024)S(1)} %broadcast.84, s32[]{:T(128)} %constant.42.clone.1), kind=kCustom, calls=%fused_computation.113 | custom fusion | flops 4096 | bytes 516 | tf_op jit(solution)/shard_map/scatter-add | solution.py:12
  66.5 24.7 %gather_fusion.4 = s32[4096]{0:T(1024)S(1)} fusion(s32[128]{0:T(128)S(1)} %sub.20, s32[4096]{0:T(1024)S(1)} %fusion.26), kind=kCustom, calls=%fused_computation.5.clone | custom fusion | bytes 49152 | tf_op jit(solution)/shard_map/jit(_take)/gather | solution.py:14
  123.1 33.6 %gather_fusion.5 = bf16[8192,512]{1,0:T(8,128)(2,1)} fusion(bf16[512,512]{1,0:T(8,128)(2,1)S(1)} %fusion.11, s32[8192]{0:T(1024)S(1)} %fusion.17), kind=kCustom, calls=%fused_computation.6.clone | custom fusion | bytes 16809984 | tf_op jit(solution)/shard_map/jit(_take)/gather | solution.py:29
  171.6 93.5 %all-to-all-done.1 = bf16[128,64,512]{2,1,0:T(8,128)(2,1)} async-done(((bf16[128,64,512]{2,1,0:T(8,128)(2,1)}), bf16[128,64,512]{2,1,0:T(8,128)(2,1)}, u32[]{:S(2)}, u32[]{:S(2)}) %all-to-all-start.1) | async-done | bytes 8388640 | tf_op jit(solution)/shard_map/all_to_all | solution.py:30
  330.2 29.0 %scatter_custom_fusion = s32[128]{0:T(128)S(1)} fusion(s32[4096]{0:T(1024)S(1)} %bitcast.141, s32[4096]{0:T(1024)S(1)} %broadcast.84, s32[]{:T(128)} %constant.42.clone.1), kind=kCustom, calls=%fused_computation.115 | custom fusion | flops 4096 | bytes 516 | tf_op jit(solution)/shard_map/scatter-add | solution.py:12
  388.8 24.7 %gather_fusion.1 = s32[4096]{0:T(1024)S(1)} fusion(s32[128]{0:T(128)S(1)} %sub.18, s32[4096]{0:T(1024)S(1)} %fusion.27), kind=kCustom, calls=%fused_computation.1.clone | custom fusion | bytes 49152 | tf_op jit(solution)/shard_map/jit(_take)/gather | solution.py:14
  460.8 33.6 %gather_fusion.2 = bf16[8192,512]{1,0:T(8,128)(2,1)} fusion(bf16[512,512]{1,0:T(8,128)(2,1)S(1)} %copy-done.1, s32[8192]{0:T(1024)S(1)} %fusion.16), kind=kCustom, calls=%fused_computation.2.clone | custom fusion | bytes 16809984 | tf_op jit(solution)/shard_map/jit(_take)/gather | solution.py:53
  553.5 33.6 %gather_fusion.7 = bf16[8192,512]{1,0:T(8,128)(2,1)} fusion(bf16[512,512]{1,0:T(8,128)(2,1)S(1)} %fusion.12, s32[8192]{0:T(1024)S(1)} %fusion.16), kind=kCustom, calls=%fused_computation.7.clone | custom fusion | bytes 16809984 | tf_op jit(solution)/shard_map/jit(_take)/gather | solution.py:29
  630.8 71.1 %all-to-all-done.3 = bf16[128,64,512]{2,1,0:T(8,128)(2,1)} async-done(((bf16[128,64,512]{2,1,0:T(8,128)(2,1)}), bf16[128,64,512]{2,1,0:T(8,128)(2,1)}, u32[]{:S(2)}, u32[]{:S(2)}) %all-to-all-start.3) | async-done | bytes 8388640 | tf_op jit(solution)/shard_map/all_to_all | solution.py:30
  749.8 24.1 %copy.79 = bf16[64,192,512]{1,0,2:T(8,128)(2,1)} copy(bf16[64,192,512]{2,1,0:T(8,128)(2,1)} %convolution_convert_fusion.4) | data formatting | bytes 25165824
  773.9 24.8 %reshape.433 = bf16[512,12288]{1,0:T(8,128)(2,1)} reshape(bf16[512,64,192]{2,1,0:T(8,128)(2,1)} %bitcast.119) | data formatting | bytes 25165824
  810.3 24.1 %copy.77 = bf16[64,512,192]{2,0,1:T(8,128)(2,1)} copy(bf16[64,512,192]{1,2,0:T(8,128)(2,1)} %convolution_convert_fusion) | data formatting | bytes 25165824
  834.4 24.7 %reshape.431 = bf16[512,12288]{1,0:T(8,128)(2,1)} reshape(bf16[512,64,192]{2,1,0:T(8,128)(2,1)} %bitcast.120) | data formatting | bytes 25165824
  871.5 24.1 %copy.75 = bf16[64,512,192]{2,0,1:T(8,128)(2,1)} copy(bf16[64,512,192]{1,2,0:T(8,128)(2,1)} %convolution_convert_fusion.1) | data formatting | bytes 25165824
  895.6 24.7 %reshape.429 = bf16[512,12288]{1,0:T(8,128)(2,1)} reshape(bf16[512,64,192]{2,1,0:T(8,128)(2,1)} %bitcast.121) | data formatting | bytes 25165824
  986.5 73.8 %all-to-all-done.4 = bf16[64,128,512]{2,0,1:T(8,128)(2,1)} async-done(((bf16[64,128,512]{2,0,1:T(8,128)(2,1)}), bf16[64,128,512]{2,0,1:T(8,128)(2,1)}, u32[]{:S(2)}, u32[]{:S(2)}) %all-to-all-start.4) | async-done | bytes 8388640 | tf_op jit(solution)/shard_map/all_to_all | solution.py:65
  1099.8 33.6 %gather_fusion.9 = bf16[8192,512]{1,0:T(8,128)(2,1)} fusion(bf16[512,512]{1,0:T(8,128)(2,1)S(1)} %fusion.13, s32[8192]{0:T(1024)S(1)} %copy-done.20), kind=kCustom, calls=%fused_computation.8.clone | custom fusion | bytes 16809984 | tf_op jit(solution)/shard_map/jit(_take)/gather | solution.py:53
  1141.7 94.5 %all_to_all.117 = bf16[128,64,512]{2,1,0:T(8,128)(2,1)} all-to-all(bf16[128,64,512]{2,1,0:T(8,128)(2,1)S(1)} %bitcast.132), channel_id=1, replica_groups=mesh['ep'=2,'dp'=4] {'ep'}, dimensions={0} | all-to-all | bytes 16777216 | tf_op jit(solution)/shard_map/all_to_all | solution.py:54
  1280.1 24.8 %reshape.427 = bf16[512,12288]{1,0:T(8,128)(2,1)} reshape(bf16[512,64,192]{2,1,0:T(8,128)(2,1)} %bitcast.122) | data formatting | bytes 25165824
  1331.5 24.1 %copy.71 = bf16[64,512,192]{2,0,1:T(8,128)(2,1)} copy(bf16[64,512,192]{1,2,0:T(8,128)(2,1)} %convolution_convert_fusion.2) | data formatting | bytes 25165824
  1355.6 24.8 %reshape.425 = bf16[512,12288]{1,0:T(8,128)(2,1)} reshape(bf16[512,64,192]{2,1,0:T(8,128)(2,1)} %bitcast.123) | data formatting | bytes 25165824
  1392.7 24.3 %copy.69 = bf16[64,512,192]{2,0,1:T(8,128)(2,1)} copy(bf16[64,512,192]{1,2,0:T(8,128)(2,1)} %convolution_convert_fusion.3) | data formatting | bytes 25165824
  1416.9 24.8 %reshape.423 = bf16[512,12288]{1,0:T(8,128)(2,1)} reshape(bf16[512,64,192]{2,1,0:T(8,128)(2,1)} %bitcast.124) | data formatting | bytes 25165824
  1494.2 85.9 %all-to-all-done.6 = bf16[64,128,512]{2,0,1:T(8,128)(2,1)} async-done(((bf16[64,128,512]{2,0,1:T(8,128)(2,1)}), bf16[64,128,512]{2,0,1:T(8,128)(2,1)}, u32[]{:S(2)}, u32[]{:S(2)}) %all-to-all-start.6) | async-done | bytes 8388640 | tf_op jit(solution)/shard_map/all_to_all | solution.py:65
  (206 shorter events, 769.1 us)
Async XLA Ops:
  7.2 545.9 %copy-start = (bf16[512,512]{1,0:T(8,128)(2,1)S(1)}, bf16[512,512]{1,0:T(8,128)(2,1)}, u32[]{:S(2)}) copy-start(bf16[512,512]{1,0:T(8,128)(2,1)} %param.30) | copy-start | bytes 1572868
  66.5 56.1 %copy-start.17 = (bf16[512,512]{1,0:T(8,128)(2,1)S(1)}, bf16[512,512]{1,0:T(8,128)(2,1)}, u32[]{:S(2)}) copy-start(bf16[512,512]{1,0:T(8,128)(2,1)} %param.22) | copy-start | bytes 1572868
  66.5 56.1 %copy-start.29 = (bf16[512,512]{1,0:T(8,128)(2,1)S(1)}, bf16[512,512]{1,0:T(8,128)(2,1)}, u32[]{:S(2)}) copy-start(bf16[512,512]{1,0:T(8,128)(2,1)} %param.24) | copy-start | bytes 1572868
  122.6 34.1 %copy-start.23 = (pred[8192]{0:T(1024)(128)(4,1)}, pred[8192]{0:T(1024)(128)(4,1)S(1)}, u32[]{:S(2)}) copy-start(pred[8192]{0:T(1024)(128)(4,1)S(1)} %compare_and_fusion.2) | copy-start | bytes 24580
  122.6 34.0 %copy-start.19 = (s32[8192]{0:T(1024)}, s32[8192]{0:T(1024)S(1)}, u32[]{:S(2)}) copy-start(s32[8192]{0:T(1024)S(1)} %fusion.17) | copy-start | bytes 98308
  123.1 429.0 %copy-start.4 = (bf16[512,512]{1,0:T(8,128)(2,1)}, bf16[512,512]{1,0:T(8,128)(2,1)S(1)}, u32[]{:S(2)}) copy-start(bf16[512,512]{1,0:T(8,128)(2,1)S(1)} %fusion.11) | copy-start | bytes 1572868
  164.1 101.0 %all-to-all-start.1 = ((bf16[128,64,512]{2,1,0:T(8,128)(2,1)}), bf16[128,64,512]{2,1,0:T(8,128)(2,1)}, u32[]{:S(2)}, u32[]{:S(2)}) async-start(bf16[128,64,512]{2,1,0:T(8,128)(2,1)} %bitcast.131), calls=%async_computation.1 | async-start | bytes 16777216 | tf_op jit(solution)/shard_map/all_to_all | solution.py:30
  323.2 181.4 %all-to-all-start.2 = ((bf16[64,128,512]{2,0,1:T(8,128)(2,1)}), bf16[64,128,512]{2,0,1:T(8,128)(2,1)}, u32[]{:S(2)}, u32[]{:S(2)}) async-start(bf16[64,128,512]{2,0,1:T(8,128)(2,1)} %copy.57), calls=%async_computation.2 | async-start | bytes 16777216 | tf_op jit(solution)/shard_map/all_to_all | solution.py:43
  388.7 72.0 %copy-start.1 = (bf16[512,512]{1,0:T(8,128)(2,1)S(1)}, bf16[512,512]{1,0:T(8,128)(2,1)}, u32[]{:S(2)}) copy-start(bf16[512,512]{1,0:T(8,128)(2,1)} %param.23) | copy-start | bytes 1572868
  504.5 99.3 %all-to-all-start = ((bf16[128,64,512]{2,1,0:T(8,128)(2,1)}), bf16[128,64,512]{2,1,0:T(8,128)(2,1)}, u32[]{:S(2)}, u32[]{:S(2)}) async-start(bf16[128,64,512]{2,1,0:T(8,128)(2,1)} %bitcast.129), calls=%async_computation | async-start | bytes 16777216 | tf_op jit(solution)/shard_map/all_to_all | solution.py:54
  512.5 33.4 %copy-start.13 = (f32[512,8]{1,0:T(8,128)}, f32[512,8]{1,0:T(8,128)S(1)}, u32[]{:S(2)}) copy-start(f32[512,8]{1,0:T(8,128)S(1)} %copy.52) | copy-start | bytes 49156
  603.9 98.0 %all-to-all-start.3 = ((bf16[128,64,512]{2,1,0:T(8,128)(2,1)}), bf16[128,64,512]{2,1,0:T(8,128)(2,1)}, u32[]{:S(2)}, u32[]{:S(2)}) async-start(bf16[128,64,512]{2,1,0:T(8,128)(2,1)} %bitcast.130), calls=%async_computation.3 | async-start | bytes 16777216 | tf_op jit(solution)/shard_map/all_to_all | solution.py:30
  610.8 1011.3 %reduce-scatter.37.cloned.1.call-start = ((), (), s32[]{:S(2)}) async-start(), calls=%async_computation.22 | async-start | bytes 15728640
  798.7 837.4 %reduce-scatter.35.cloned.1.call-start = ((), (), s32[]{:S(2)}) async-start(), calls=%async_computation.21 | async-start | bytes 15728640
  859.1 791.0 %reduce-scatter.33.cloned.1.call-start = ((), (), s32[]{:S(2)}) async-start(), calls=%async_computation.20 | async-start | bytes 15728640
  962.8 97.4 %all-to-all-start.4 = ((bf16[64,128,512]{2,0,1:T(8,128)(2,1)}), bf16[64,128,512]{2,0,1:T(8,128)(2,1)}, u32[]{:S(2)}, u32[]{:S(2)}) async-start(bf16[64,128,512]{2,0,1:T(8,128)(2,1)} %copy.60), calls=%async_computation.4 | async-start | bytes 16777216 | tf_op jit(solution)/shard_map/all_to_all | solution.py:65
  969.9 694.3 %reduce-scatter.31.cloned.1.call-start = ((), (), s32[]{:S(2)}) async-start(), calls=%async_computation.19 | async-start | bytes 15728640
  1099.8 33.6 %copy-start.6 = (bf16[512,512]{1,0:T(8,128)(2,1)}, bf16[512,512]{1,0:T(8,128)(2,1)S(1)}, u32[]{:S(2)}) copy-start(bf16[512,512]{1,0:T(8,128)(2,1)S(1)} %fusion.13) | copy-start | bytes 1572868
  1099.8 33.6 %copy-start.24 = (pred[8192]{0:T(1024)(128)(4,1)S(1)}, pred[8192]{0:T(1024)(128)(4,1)}, u32[]{:S(2)}) copy-start(pred[8192]{0:T(1024)(128)(4,1)} %copy-done.23) | copy-start | bytes 24580
  1304.9 373.4 %reduce-scatter.29.cloned.1.call-start = ((), (), s32[]{:S(2)}) async-start(), calls=%async_computation.18 | async-start | bytes 15728640
  1380.4 312.0 %reduce-scatter.27.cloned.1.call-start = ((), (), s32[]{:S(2)}) async-start(), calls=%async_computation.17 | async-start | bytes 15728640
  1484.2 95.9 %all-to-all-start.6 = ((bf16[64,128,512]{2,0,1:T(8,128)(2,1)}), bf16[64,128,512]{2,0,1:T(8,128)(2,1)}, u32[]{:S(2)}, u32[]{:S(2)}) async-start(bf16[64,128,512]{2,0,1:T(8,128)(2,1)} %copy.64), calls=%async_computation.6 | async-start | bytes 16777216 | tf_op jit(solution)/shard_map/all_to_all | solution.py:65
  1491.3 215.1 %reduce-scatter.23.cloned.1.call-start = ((), (), s32[]{:S(2)}) async-start(), calls=%async_computation.15 | async-start | bytes 589824 | tf_op jit(solution)/shard_map/reduce_scatter | solution.py:76
  1494.0 212.5 %reduce-scatter.25.cloned.1.call-start = ((), (), s32[]{:S(2)}) async-start(), calls=%async_computation.16 | async-start | bytes 589824
  (20 other events, 258.0 us)
Sparse Core Ops, SparseCore 0:
  798.8 90.1 reduce-scatter.36
  891.6 90.5 reduce-scatter.34
  984.8 90.5 reduce-scatter.32
  1305.0 89.6 reduce-scatter.30
  1397.1 90.5 reduce-scatter.28
  1490.2 90.5 reduce-scatter.26
  1584.3 25.7 reduce-scatter.22
  1619.9 24.6 reduce-scatter.24
where the time goes:
time: 1730 us; the launch traced here: 1710 us
  local copies, waits for them, and re-layouts  872 us (50%)
  waiting for transfers between devices  334 us (19%)
  matrix products  235 us (14%)
  other arithmetic  119 us (7%)
  blocking collectives  94.5 us (5%)
  starting transfers between devices  43.6 us (3%)
    unnamed x89, local copies, waits for them, and re-layouts  382 us
    all_to_all x2, waiting for transfers between devices, dispatch(): recv = lax.all_to_all(send, 'ep', 0, 1, tiled=True)  165 us
    all_to_all x2, waiting for transfers between devices, layer_backward(): grad_back = lax.all_to_all(grad_recv, 'ep', 1, 0, tiled=True)  160 us
    all_to_all x1, blocking collectives, layer_backward(): lax.all_to_all(grad_send.reshape(n_exp, capacity, -1), 'ep', 0, 1, tiled=...  94.5 us
    gather x2, local copies, waits for them, and re-layouts, layer_backward(): jnp.take(grad_y, row_tok, axis=0, mode='fill', fill_value=0)  67.1 us
    gather x2, local copies, waits for them, and re-layouts, dispatch(): jnp.take(mixed, row_tok, axis=0, mode='fill', fill_value=0)  67.1 us
    scatter x4, local copies, waits for them, and re-layouts, row_fill(): jnp.full((n_rows,), empty, values.dtype).at[flat_pos.reshape(-1)]  62.5 us
    scatter-add x2, other arithmetic, copy_rows(): counts = jnp.zeros((n_exp,), jnp.int32).at[flat_exp].add(1)  57.8 us
  transfers between devices with their start and end apart: 14, of which 5 were waited for; matrix products, arithmetic and copies ran while one was open for 53% of the time, Pallas kernels for 0%

commit v1 on v0

v1 whole, which is shorter than its diff:
```python
import jax
import jax.numpy as jnp
from jax import lax
from jax.experimental import pallas as pl
from jax.experimental.pallas import tpu as pltpu
from jax.sharding import Mesh, PartitionSpec as P

F32 = jnp.float32
BF16 = jnp.bfloat16
CAP = 64
GROUP = 4
CORES = 2
CHIPS = 2
ALL = ('x', 'c', 'y')


def matmul(lhs, rhs, lhs_dim=1, rhs_dim=0):
    return lax.dot_general(lhs, rhs, (((lhs_dim,), (rhs_dim,)), ((), ())), preferred_element_type=F32)


def gate_hidden(x_rows, w_gate, w_up):
    a_pre = matmul(x_rows, w_gate)
    b_pre = matmul(x_rows, w_up)
    return a_pre, b_pre, jax.nn.sigmoid(a_pre)


def select_rows(rank_ref, gate_ref, src, n_src):
    n_tok = rank_ref.shape[-1]
    slot = lax.broadcasted_iota(jnp.int32, (CAP, n_tok), 0)
    picks, gates = [], []
    for exp in range(GROUP):
        row = pl.ds(exp * n_src + src, 1)
        hit = slot == rank_ref[row, :]
        picks.append(jnp.where(hit, 1.0, 0.0).astype(BF16))
        gates.append(jnp.sum(jnp.where(hit, gate_ref[row, :], 0.0), axis=1, keepdims=True))
    return jnp.concatenate(picks, axis=0), jnp.concatenate(gates, axis=0)


def forward_kernel(where_ref, u_ref, rank_ref, gate_ref, wg_ref, wu_ref, wd_ref, out_ref, pick_ref, row_ref, x_ref, part_ref):
    n_src = u_ref.shape[0]
    own = n_src // CHIPS
    first = where_ref[1] * own

    @pl.when(pl.program_id(0) == 0)
    def _():
        out_ref[...] = jnp.zeros_like(out_ref)

    @pl.loop(0, own)
    def _(src):
        pick, gate = select_rows(rank_ref, gate_ref, first + src, n_src)
        pick_ref[src] = pick
        rows = matmul(pick, u_ref[first + src]).astype(BF16)
        at = pl.ds(pl.multiple_of(src * CAP, CAP), CAP)
        for exp in range(GROUP):
            x_ref[exp, at, :] = rows[exp * CAP:(exp + 1) * CAP]
            row_ref[exp, at, :] = jnp.broadcast_to(gate[exp * CAP:(exp + 1) * CAP], (CAP, 128))

    @pl.loop(0, GROUP)
    def _(exp):
        a_pre, b_pre, sigma = gate_hidden(x_ref[exp], wg_ref[exp], wu_ref[exp])
        hidden = (a_pre * sigma * b_pre).astype(BF16)
        out = matmul(hidden, wd_ref[exp]).astype(BF16).astype(F32) * row_ref[exp][:, :1]
        high = out.astype(BF16)
        rest = out - high.astype(F32)
        mid = rest.astype(BF16)
        low = (rest - mid.astype(F32)).astype(BF16)
        at = pl.ds(pl.multiple_of(exp * CAP, CAP), CAP)
        for src in range(own):
            here = slice(src * CAP, (src + 1) * CAP)
            part_ref[src, 0, at, :] = high[here]
            part_ref[src, 1, at, :] = mid[here]
            part_ref[src, 2, at, :] = low[here]

    @pl.loop(0, own)
    def _(src):
        pick = pick_ref[src]
        total = matmul(pick, part_ref[src, 0], 0, 0)
        total += matmul(pick, part_ref[src, 1], 0, 0) + matmul(pick, part_ref[src, 2], 0, 0)
        out_ref[src] += total


def backward_kernel(where_ref, u_ref, dy_ref, rank_ref, gate_ref, wg_ref, wu_ref, wd_ref,
                    out_ref, gg_ref, gu_ref, gd_ref, pick_ref, x_ref, d_ref, gx_ref):
    n_src, _, dim = u_ref.shape
    own = n_src // CHIPS
    first = where_ref[1] * own
    half = dim // CHIPS
    piece = half // CORES
    cols = pl.ds(pl.multiple_of(where_ref[1] * half, half), half)

    @pl.when(pl.program_id(0) == 0)
    def _():
        out_ref[...] = jnp.zeros_like(out_ref)

    @pl.loop(0, n_src)
    def _(step):
        src = lax.rem(first + step, n_src)
        pick, gate = select_rows(rank_ref, gate_ref, src, n_src)
        pick_ref[step] = pick
        x_rows = matmul(pick, u_ref[src]).astype(BF16)
        d_rows = (matmul(pick, dy_ref[src]) * gate).astype(BF16)
        at = pl.ds(pl.multiple_of(step * CAP, CAP), CAP)
        for exp in range(GROUP):
            x_ref[exp, at, :] = x_rows[exp * CAP:(exp + 1) * CAP]
            d_ref[exp, at, :] = d_rows[exp * CAP:(exp + 1) * CAP]

    @pl.loop(0, GROUP)
    def _(exp):
        w_gate, w_up = wg_ref[exp], wu_ref[exp]
        a_pre, b_pre, sigma = gate_hidden(x_ref[exp], w_gate, w_up)
        silu = a_pre * sigma
        hidden = (silu * b_pre).astype(BF16)
        grad_hidden = matmul(d_ref[exp], wd_ref[exp], 1, 1).astype(BF16).astype(F32)
        grad_a = (grad_hidden * b_pre * sigma * (1.0 + a_pre * (1.0 - sigma))).astype(BF16)
        grad_b = (grad_hidden * silu).astype(BF16)
        x_half = x_ref[exp, :, cols]
        grad_gate = matmul(x_half, grad_a, 0, 0).astype(BF16)
        grad_up = matmul(x_half, grad_b, 0, 0).astype(BF16)
        grad_down = matmul(hidden, d_ref[exp, :, cols], 0, 0).astype(BF16)
        for core in range(CORES):
            here = slice(core * piece, (core + 1) * piece)
            gg_ref[core, exp] = grad_gate[here]
            gu_ref[core, exp] = grad_up[here]
            gd_ref[core, exp] = grad_down[:, here]
        kept = own * CAP
        grad_x = (matmul(grad_a[:kept], w_gate, 1, 1) + matmul(grad_b[:kept], w_up, 1, 1)).astype(BF16)
        at = pl.ds(pl.multiple_of(exp * CAP, CAP), CAP)
        for src in range(own):
            gx_ref[src, at, :] = grad_x[src * CAP:(src + 1) * CAP]

    @pl.loop(0, own)
    def _(src):
        out_ref[src] += matmul(pick_ref[src], gx_ref[src], 0, 0)


def call_specs(n_src, n_tok, dim, ff, n_exp):
    groups = n_exp // GROUP
    whole = pl.BlockSpec((n_src, n_tok, dim), lambda g, w: (0, 0, 0), pipeline_mode=pl.Buffered(1))
    table = pl.BlockSpec((GROUP * n_src, n_tok), lambda g, w: (g, 0))
    wide = pl.BlockSpec((GROUP, dim, ff), lambda g, w: (w[0] * groups + g, 0, 0))
    tall = pl.BlockSpec((GROUP, ff, dim), lambda g, w: (w[0] * groups + g, 0, 0))
    total = pl.BlockSpec((n_src // CHIPS, n_tok, dim), lambda g, w: (0, 0, 0), pipeline_mode=pl.Buffered(1))
    return groups, whole, table, wide, tall, total


def expert_forward(where, u_all, rank, gate, w_gate, w_up, w_down):
    n_src, n_tok, dim = u_all.shape
    ff = w_gate.shape[2]
    n_exp = rank.shape[0] // n_src
    own = n_src // CHIPS
    groups, whole, table, wide, tall, total = call_specs(n_src, n_tok, dim, ff, n_exp)
    rows = n_exp * own * CAP
    return pl.pallas_call(
        forward_kernel,
        out_shape=jax.ShapeDtypeStruct((own, n_tok, dim), F32),
        grid_spec=pltpu.PrefetchScalarGridSpec(
            num_scalar_prefetch=1, grid=(groups,), in_specs=[whole, table, table, wide, wide, tall], out_specs=total,
            scratch_shapes=[pltpu.VMEM((own, GROUP * CAP, n_tok), BF16), pltpu.VMEM((GROUP, own * CAP, 128), F32),
                            pltpu.VMEM((GROUP, own * CAP, dim), BF16), pltpu.VMEM((own, 3, GROUP * CAP, dim), BF16)]),
        compiler_params=pltpu.CompilerParams(dimension_semantics=('arbitrary',), vmem_limit_bytes=56 << 20),
        cost_estimate=pl.CostEstimate(flops=rows * dim * (8 * n_tok + 6 * ff), bytes_accessed=40 << 20, transcendentals=0),
    )(where, u_all, rank, gate, w_gate, w_up, w_down)


def expert_backward(where, u_all, dy_all, rank, gate, w_gate, w_up, w_down):
    n_src, n_tok, dim = u_all.shape
    ff = w_gate.shape[2]
    n_exp = rank.shape[0] // n_src
    own = n_src // CHIPS
    piece = dim // (CHIPS * CORES)
    groups, whole, table, wide, tall, total = call_specs(n_src, n_tok, dim, ff, n_exp)
    rows = n_exp * n_src * CAP
    wide_out = pl.BlockSpec((CORES, GROUP, piece, ff), lambda g, w: (0, g, 0, 0))
    tall_out = pl.BlockSpec((CORES, GROUP, ff, piece), lambda g, w: (0, g, 0, 0))
    wide_shape = jax.ShapeDtypeStruct((CORES, n_exp, piece, ff), BF16)
    return pl.pallas_call(
        backward_kernel,
        out_shape=(jax.ShapeDtypeStruct((own, n_tok, dim), F32), wide_shape, wide_shape,
                   jax.ShapeDtypeStruct((CORES, n_exp, ff, piece), BF16)),
        grid_spec=pltpu.PrefetchScalarGridSpec(
            num_scalar_prefetch=1, grid=(groups,), in_specs=[whole, whole, table, table, wide, wide, tall],
            out_specs=(total, wide_out, wide_out, tall_out),
            scratch_shapes=[pltpu.VMEM((n_src, GROUP * CAP, n_tok), BF16), pltpu.VMEM((GROUP, n_src * CAP, dim), BF16),
                            pltpu.VMEM((GROUP, n_src * CAP, dim), BF16), pltpu.VMEM((own, GROUP * CAP, dim), BF16)]),
        compiler_params=pltpu.CompilerParams(dimension_semantics=('arbitrary',), vmem_limit_bytes=56 << 20),
        cost_estimate=pl.CostEstimate(flops=rows * dim * (5 * n_tok + 11 * ff), bytes_accessed=60 << 20, transcendentals=0),
    )(where, u_all, dy_all, rank, gate, w_gate, w_up, w_down)


def route_tables(idx, gate, first_exp, n_exp):
    n_src, _, n_tok = idx.shape
    experts = (first_exp + jnp.arange(n_exp, dtype=jnp.int32)).astype(F32)
    hit = idx[None] == experts[:, None, None, None]
    member = jnp.any(hit, axis=2)
    gates = jnp.sum(jnp.where(hit, gate[None], 0.0), axis=2)
    before = jnp.triu(jnp.ones((n_tok, n_tok), BF16), 1)
    count = jnp.einsum('est,tv->esv', member.astype(BF16), before, preferred_element_type=F32)
    rank = jnp.where(member, count.astype(jnp.int32), -1)
    return rank.reshape(n_exp * n_src, n_tok), gates.reshape(n_exp * n_src, n_tok)


def mix(x, weight):
    return (x.astype(F32) + jnp.einsum('...d,de->...e', x, weight, preferred_element_type=F32)).astype(BF16)


def mix_back(grad, weight):
    return (grad.astype(F32) + jnp.einsum('...e,de->...d', grad, weight, preferred_element_type=F32)).astype(BF16)


def swap_cores(parts):
    moved = lax.all_to_all(parts, 'c', 0, 0, tiled=True)
    return moved.reshape((-1,) + moved.shape[2:])


def solution(mesh):
    fine = Mesh(mesh.devices.reshape(2, CHIPS, CORES), ('y', 'x', 'c'))
    tok_spec = P(ALL, None)
    exp_spec = P('y', None, None)
    layer_specs = (P(None, None), tok_spec, tok_spec, exp_spec, exp_spec, exp_spec)
    grad_specs = (P(ALL, None), P('y', ('x', 'c'), None), P('y', ('x', 'c'), None), P('y', None, ('x', 'c')))

    def local_step(tokens, dy_out, dense_w1, route_idx1, route_gate1, w_gate1, w_up1, w_down1, dense_w2, route_idx2, route_gate2, w_gate2, w_up2, w_down2):
        n_exp = w_gate1.shape[0] // CORES
        ix, ic, iy = (lax.axis_index(name) for name in ALL)
        where = jnp.stack([ic, ix]).astype(jnp.int32)
        first_exp = (iy * CORES + ic) * n_exp
        me = (ix * CORES + ic) * 2 + iy

        def gather(value):
            return lax.all_gather(value, ALL, axis=0, tiled=False)

        def reduce_own(total):
            return lax.psum_scatter(total, ('c', 'y'), scatter_dimension=0, tiled=False)

        routes = jnp.concatenate([route_idx1.astype(F32), route_idx2.astype(F32), route_gate1, route_gate2], axis=1).T
        routes = gather(routes)
        idx1, idx2, gate1, gate2 = jnp.split(routes, 4, axis=1)
        rank1, gates1 = route_tables(idx1, gate1, first_exp, n_exp)
        rank2, gates2 = route_tables(idx2, gate2, first_exp, n_exp)

        tok_all = gather(tokens)
        dy_all = gather(dy_out)
        u_one = mix(tok_all, dense_w1)
        y_sum = reduce_own(expert_forward(where, u_one, rank1, gates1, w_gate1, w_up1, w_down1))
        y_one = (mix(tokens, dense_w1).astype(F32) + y_sum).astype(BF16)
        y_all = gather(y_one)
        u_two = mix(y_all, dense_w2)
        back, gg, gu, gd = expert_backward(where, u_two, dy_all, rank2, gates2, w_gate2, w_up2, w_down2)
        gm_two = (dy_out.astype(F32) + reduce_own(back)).astype(BF16)
        gate_two, up_two, down_two = swap_cores(gg), swap_cores(gu), swap_cores(gd)
        gm_all = gather(gm_two)
        rows = dense_w2.shape[0] // 8
        y_cols = lax.dynamic_slice_in_dim(y_all, me * rows, rows, 2)
        dense_two = jnp.einsum('std,ste->de', y_cols, gm_all, preferred_element_type=F32).astype(BF16)
        grad_mid = mix_back(gm_all, dense_w2)
        back, gg, gu, gd = expert_backward(where, u_one, grad_mid, rank1, gates1, w_gate1, w_up1, w_down1)
        gm_one = (lax.dynamic_index_in_dim(grad_mid, me, 0, keepdims=False).astype(F32) + reduce_own(back)).astype(BF16)
        gate_one, up_one, down_one = swap_cores(gg), swap_cores(gu), swap_cores(gd)
        grad_tok = mix_back(gm_one, dense_w1)
        dense_part = jnp.einsum('td,te->de', tokens, gm_one, preferred_element_type=F32).astype(BF16)
        dense_one = lax.psum_scatter(dense_part, ALL, scatter_dimension=0, tiled=True)
        return (grad_tok, dense_one, gate_one, up_one, down_one, dense_two, gate_two, up_two, down_two)

    return jax.shard_map(local_step, mesh=fine, in_specs=(tok_spec, tok_spec) + layer_specs + layer_specs,
                         out_specs=(tok_spec,) + grad_specs + grad_specs, check_vma=False)
```

time: 1730 us -> 668 us (0.39)
  local copies, waits for them, and re-layouts: 872 us -> 120 us
  Pallas kernels: 0 us -> 248 us
  matrix products: 235 us -> 33 us
  waiting for transfers between devices: 334 us -> 163 us
  other arithmetic: 119 us -> 13.2 us
  starting transfers between devices: 43.6 us -> 0.5 us
  blocking collectives: 94.5 us -> 72.7 us
    all_to_all x6 -> x0, waiting for transfers between devices: 334 us -> none  [the longest x2 165 us: dispatch(): recv = lax.all_to_all(send, 'ep', 0, 1, tiled=True)]
    gather x11 -> x0, local copies, waits for them, and re-layouts: 295 us -> none  [the longest x2 67.1 us: layer_backward(): jnp.take(grad_y, row_tok, axis=0, mode='fill', fill_value=0)]
    unnamed x89 -> x37, local copies, waits for them, and re-layouts: 382 us -> 95.4 us
    pallas_call x0 -> x3, Pallas kernels: none -> 248 us  [the longest x2 193 us: expert_backward(): pl.pallas_call(backward_kernel, out_shape=(jax.ShapeDtypeStruct((own, n_t...]
    dot_general x23 -> x9, matrix products: 235 us -> 33 us  [the longest x3 18.1 us: mix(): jnp.einsum('...d,de->...e', x, weight, preferred_element_type=F32)]
    unnamed x15 -> x12, waiting for transfers between devices: 0.14 us -> 117 us
    scatter x6 -> x0, local copies, waits for them, and re-layouts: 93.6 us -> none  [the longest x4 62.5 us: row_fill(): jnp.full((n_rows,), empty, values.dtype).at[flat_pos.reshape(-1)]]
    all_to_all x7 -> x0, local copies, waits for them, and re-layouts: 65 us -> none  [the longest x2 22.7 us: layer_backward(): grad_back = lax.all_to_all(grad_recv, 'ep', 1, 0, tiled=True)]
  transfers between devices with their start and end apart: 14 -> 8, of which waited for: 5 -> 5; matrix products, arithmetic and copies ran while one was open for 53% -> 19% of each run, Pallas kernels for 0% -> 0%
where the time goes in v1:
time: 668 us; the launch traced here: 665 us
  Pallas kernels  248 us (37%)
  waiting for transfers between devices  163 us (24%)
  local copies, waits for them, and re-layouts  120 us (18%)
  blocking collectives  72.7 us (11%)
  matrix products  33 us (5%)
  between operations  14.2 us (2%)
  other arithmetic  13.2 us (2%)
    pallas_call x2, Pallas kernels, expert_backward(): pl.pallas_call(backward_kernel, out_shape=(jax.ShapeDtypeStruct((own, n_t...  193 us
    unnamed x12, waiting for transfers between devices  117 us
    unnamed x37, local copies, waits for them, and re-layouts  95.4 us
    all_to_all x6, blocking collectives, swap_cores(): moved = lax.all_to_all(parts, 'c', 0, 0, tiled=True)  57.6 us
    pallas_call x1, Pallas kernels, expert_forward(): pl.pallas_call(forward_kernel, out_shape=jax.ShapeDtypeStruct((own, n_tok...  55.7 us
    all_gather x4, waiting for transfers between devices, gather(): return lax.all_gather(value, ALL, axis=0, tiled=False)  46.6 us
    pallas_call x4, local copies, waits for them, and re-layouts, expert_backward(): pl.pallas_call(backward_kernel, out_shape=(jax.ShapeDtypeStruct((own, n_t...  24.4 us
    dot_general x3, matrix products, mix(): jnp.einsum('...d,de->...e', x, weight, preferred_element_type=F32)  18.1 us
  transfers between devices with their start and end apart: 8, of which 5 were waited for; matrix products, arithmetic and copies ran while one was open for 19% of the time, Pallas kernels for 0%

profile of v1, /device:TPU:0, one launch (start us, length us, event | category | flops | bytes accessed | tf_op | source)
XLA Modules:
  0.0 665.1 jit_solution(941803202266979446)
XLA Ops:
  9.4 19.0 %copy.47.wg_ref = bf16[64,512,192]{2,1,0:T(8,128)(2,1)} copy(bf16[64,512,192]{1,2,0:T(8,128)(2,1)} %param.19) | data formatting | bytes 25165824 | tf_op args[5]
  28.4 19.0 %copy.48.wu_ref = bf16[64,512,192]{2,1,0:T(8,128)(2,1)} copy(bf16[64,512,192]{1,2,0:T(8,128)(2,1)} %param.20) | data formatting | bytes 25165824 | tf_op args[6]
  48.1 15.1 %all-gather.1 = f32[256,512]{1,0:T(8,128)S(1)} all-gather(f32[32,512]{1,0:T(8,128)S(1)} %maximum_bitcast_fusion), channel_id=3, replica_groups=mesh['y'=2,'x'=2,'c'=2] {'x','c','y'}, dimensions={0}, use_global_device_ids=true | all-gather | bytes 589824 | tf_op jit(solution)/shard_map/all_gather | solution.py:230
  71.8 7.9 %add_convert_fusion.2.u_ref = bf16[8,512,512]{2,1,0:T(8,128)(2,1)} fusion(bf16[8,512,512]{2,1,0:T(8,128)(2,1)} %bitcast.75, bf16[512,512]{1,0:T(8,128)(2,1)S(1)} %copy-done.10), kind=kOutput, calls=%fused_computation.2 | convolution fusion | flops 2153775104 | bytes 8912896 | tf_op jit(solution)/shard_map/...d,de->...e/dot_general | solution.py:203
  79.7 55.7 %shard_map.205 = f32[4,512,512]{2,1,0:T(8,128)} custom-call(s32[2]{0:T(128)} %pad_add_fusion.where_ref, bf16[8,512,512]{2,1,0:T(8,128)(2,1)} %add_convert_fusion.2.u_ref, s32[256,512]{1,0:T(8,128)} %fusion.10.rank_ref, f32[256,512]{1,0:T(8,128)} %bitcast.70, bf16[64,512,192]{2,1,0:T(8,128)(2,1)} %copy.47.wg_ref, bf16[64,512,192]{2,1,0:T(8,128)(2,1)} %copy.48.wu_ref, ...), custom_call_target="tpu_custom_call" | custom-call | flops 22011707392 | bytes 41943040 | tf_op jit(solution)/shard_map/pallas_call | solution.py:153
  135.5 38.4 %reduce-scatter.15.cloned.1.call-done = f32[1,512,512]{2,1,0:T(8,128)} async-done(((f32[4,512,512]{2,1,0:T(8,128)}), f32[1,512,512]{2,1,0:T(8,128)}) %reduce-scatter.15.cloned.1.call-update) | async-done | bytes 1048592
  177.2 18.9 %copy.49.wg_ref = bf16[64,512,192]{2,1,0:T(8,128)(2,1)} copy(bf16[64,512,192]{1,2,0:T(8,128)(2,1)} %param.25) | data formatting | bytes 25165824 | tf_op args[11]
  196.2 18.9 %copy.50.wu_ref = bf16[64,512,192]{2,1,0:T(8,128)(2,1)} copy(bf16[64,512,192]{1,2,0:T(8,128)(2,1)} %param.26) | data formatting | bytes 25165824 | tf_op args[12]
  216.2 7.8 %add_convert_fusion.1.u_ref = bf16[8,512,512]{2,1,0:T(8,128)(2,1)} fusion(bf16[8,512,512]{2,1,0:T(8,128)(2,1)} %bitcast.73, bf16[512,512]{1,0:T(8,128)(2,1)S(1)} %copy-done), kind=kOutput, calls=%fused_computation.1 | convolution fusion | flops 2153775104 | bytes 8912896 | tf_op jit(solution)/shard_map/...d,de->...e/dot_general | solution.py:203
  224.0 15.7 %all-gather.14.cloned.1.call-done = bf16[4096,512]{1,0:T(8,128)(2,1)} async-done(((bf16[512,512]{1,0:T(8,128)(2,1)}), bf16[4096,512]{1,0:T(8,128)(2,1)}) %all-gather.14.cloned.1.call-update) | async-done | bytes 4194320 | tf_op jit(solution)/shard_map/all_gather | solution.py:230
  239.8 96.3 %shard_map.206 = (f32[4,512,512]{2,1,0:T(8,128)}, bf16[2,32,128,192]{3,2,1,0:T(8,128)(2,1)}, bf16[2,32,128,192]{3,2,1,0:T(8,128)(2,1)}, bf16[2,32,192,128]{3,2,1,0:T(8,128)(2,1)}) custom-call(s32[2]{0:T(128)} %pad_add_fusion.where_ref, bf16[8,512,512]{2,1,0:T(8,128)(2,1)} %add_convert_fusion.1.u_ref, bf16[8,512,512]{2,1,0:T(8,128)(2,1)} %bitcast.76, ...), custom_call_target="tpu_custom_call" | custom-call | flops 39191576576 | bytes 62914560 | tf_op jit(solution)/shard_map/pallas_call | solution.py:176
  336.1 38.5 %reduce-scatter.17.cloned.1.call-done = f32[1,512,512]{2,1,0:T(8,128)} async-done(((f32[4,512,512]{2,1,0:T(8,128)}), f32[1,512,512]{2,1,0:T(8,128)}) %reduce-scatter.17.cloned.1.call-update) | async-done | bytes 1048592
  376.9 30.8 %all-gather.16.cloned.1.call-done = bf16[4096,512]{1,0:T(8,128)(2,1)} async-done(((bf16[512,512]{1,0:T(8,128)(2,1)}), bf16[4096,512]{1,0:T(8,128)(2,1)}) %all-gather.16.cloned.1.call-update) | async-done | bytes 4194320 | tf_op jit(solution)/shard_map/all_gather | solution.py:230
  407.7 7.9 %add_convert_fusion.dy_ref = bf16[8,512,512]{2,1,0:T(8,128)(2,1)} fusion(bf16[8,512,512]{2,1,0:T(8,128)(2,1)} %bitcast.67, bf16[512,512]{1,0:T(8,128)(2,1)S(1)} %copy-done), kind=kOutput, calls=%fused_computation | convolution fusion | flops 2153775104 | bytes 8912896 | tf_op jit(solution)/shard_map/...e,de->...d/dot_general | solution.py:207
  415.6 96.3 %shard_map.207 = (f32[4,512,512]{2,1,0:T(8,128)}, bf16[2,32,128,192]{3,2,1,0:T(8,128)(2,1)}, bf16[2,32,128,192]{3,2,1,0:T(8,128)(2,1)}, bf16[2,32,192,128]{3,2,1,0:T(8,128)(2,1)}) custom-call(s32[2]{0:T(128)} %pad_add_fusion.where_ref, bf16[8,512,512]{2,1,0:T(8,128)(2,1)} %add_convert_fusion.2.u_ref, bf16[8,512,512]{2,1,0:T(8,128)(2,1)} %add_convert_fusion.dy_ref, ...), custom_call_target="tpu_custom_call" | custom-call | flops 39191576576 | bytes 62914560 | tf_op jit(solution)/shard_map/pallas_call | solution.py:176
  512.0 38.5 %reduce-scatter.19.cloned.1.call-done = f32[1,512,512]{2,1,0:T(8,128)} async-done(((f32[4,512,512]{2,1,0:T(8,128)}), f32[1,512,512]{2,1,0:T(8,128)}) %reduce-scatter.19.cloned.1.call-update) | async-done | bytes 1048592
  553.5 10.1 %all_to_all.30 = bf16[2,32,192,128]{3,2,1,0:T(8,128)(2,1)} all-to-all(bf16[2,32,192,128]{3,2,1,0:T(8,128)(2,1)} %get-tuple-element.24), channel_id=1, replica_groups=mesh['y'=2,'x'=2,'c'=2] {'c'}, dimensions={0} | all-to-all | bytes 6291456 | tf_op jit(solution)/shard_map/all_to_all | solution.py:211
  563.6 6.1 copy.56
  569.7 10.0 %all_to_all.31 = bf16[2,32,128,192]{2,3,1,0:T(8,128)(2,1)} all-to-all(bf16[2,32,128,192]{2,3,1,0:T(8,128)(2,1)} %copy.56), channel_id=1, replica_groups=mesh['y'=2,'x'=2,'c'=2] {'c'}, dimensions={0} | all-to-all | bytes 6291456 | tf_op jit(solution)/shard_map/all_to_all | solution.py:211
  585.8 10.2 %all_to_all.32 = bf16[2,32,128,192]{2,3,1,0:T(8,128)(2,1)} all-to-all(bf16[2,32,128,192]{2,3,1,0:T(8,128)(2,1)} %copy.57), channel_id=1, replica_groups=mesh['y'=2,'x'=2,'c'=2] {'c'}, dimensions={0} | all-to-all | bytes 6291456 | tf_op jit(solution)/shard_map/all_to_all | solution.py:211
  596.0 7.1 %all_to_all.33 = bf16[2,32,192,128]{3,2,1,0:T(8,128)(2,1)} all-to-all(bf16[2,32,192,128]{3,2,1,0:T(8,128)(2,1)S(1)} %copy-done.7), channel_id=1, replica_groups=mesh['y'=2,'x'=2,'c'=2] {'c'}, dimensions={0} | all-to-all | bytes 6291456 | tf_op jit(solution)/shard_map/all_to_all | solution.py:211
  609.2 10.0 %all_to_all.34 = bf16[2,32,128,192]{2,3,1,0:T(8,128)(2,1)} all-to-all(bf16[2,32,128,192]{2,3,1,0:T(8,128)(2,1)} %copy.53), channel_id=1, replica_groups=mesh['y'=2,'x'=2,'c'=2] {'c'}, dimensions={0} | all-to-all | bytes 6291456 | tf_op jit(solution)/shard_map/all_to_all | solution.py:211
  619.2 6.1 copy.54
  625.3 10.2 %all_to_all.35 = bf16[2,32,128,192]{2,3,1,0:T(8,128)(2,1)} all-to-all(bf16[2,32,128,192]{2,3,1,0:T(8,128)(2,1)} %copy.54), channel_id=1, replica_groups=mesh['y'=2,'x'=2,'c'=2] {'c'}, dimensions={0} | all-to-all | bytes 6291456 | tf_op jit(solution)/shard_map/all_to_all | solution.py:211
  (70 shorter events, 56.2 us)
Async XLA Ops:
  7.2 209.0 %copy-start = (bf16[512,512]{1,0:T(8,128)(2,1)S(1)}, bf16[512,512]{1,0:T(8,128)(2,1)}, u32[]{:S(2)}) copy-start(bf16[512,512]{1,0:T(8,128)(2,1)} %param.22) | copy-start | bytes 1572868
  7.2 64.6 %all-gather.10.cloned.1.call-start = ((), (), s32[]{:S(2)}) async-start(), calls=%async_computation.10 | async-start | bytes 4718592 | tf_op jit(solution)/shard_map/all_gather | solution.py:230
  7.9 166.0 %reduce-scatter.15.cloned.1.call-start = ((), (), s32[]{:S(2)}) async-start(), calls=%async_computation.15 | async-start | bytes 5242880
  28.4 19.6 %copy-start.11 = (f32[512,8]{0,1:T(8,128)S(1)}, f32[512,8]{0,1:T(8,128)}, u32[]{:S(2)}) copy-start(f32[512,8]{0,1:T(8,128)} %param.24) | copy-start | bytes 49156
  28.4 19.6 %copy-start.12 = (f32[512,8]{0,1:T(8,128)S(1)}, f32[512,8]{0,1:T(8,128)}, u32[]{:S(2)}) copy-start(f32[512,8]{0,1:T(8,128)} %param.18) | copy-start | bytes 49156
  47.5 24.4 %copy-start.10 = (bf16[512,512]{1,0:T(8,128)(2,1)S(1)}, bf16[512,512]{1,0:T(8,128)(2,1)}, u32[]{:S(2)}) copy-start(bf16[512,512]{1,0:T(8,128)(2,1)} %param.16) | copy-start | bytes 1572868
  135.4 38.5 %copy-start.8 = (bf16[512,512]{1,0:T(8,128)(2,1)S(1)}, bf16[512,512]{1,0:T(8,128)(2,1)}, u32[]{:S(2)}) copy-start(bf16[512,512]{1,0:T(8,128)(2,1)} %param.14) | copy-start | bytes 1572868
  135.5 80.8 %all-gather.12.cloned.1.call-start = ((), (), s32[]{:S(2)}) async-start(), calls=%async_computation.11 | async-start | bytes 4718592 | tf_op jit(solution)/shard_map/all_gather | solution.py:230
  176.4 63.4 %all-gather.14.cloned.1.call-start = ((), (), s32[]{:S(2)}) async-start(), calls=%async_computation.12 | async-start | bytes 4718592 | tf_op jit(solution)/shard_map/all_gather | solution.py:230
  177.0 197.7 %reduce-scatter.17.cloned.1.call-start = ((), (), s32[]{:S(2)}) async-start(), calls=%async_computation.16 | async-start | bytes 5242880
  336.1 38.6 %copy-start.9 = (bf16[512,512]{1,0:T(8,128)(2,1)S(1)}, bf16[512,512]{1,0:T(8,128)(2,1)}, u32[]{:S(2)}) copy-start(bf16[512,512]{1,0:T(8,128)(2,1)} %param.15) | copy-start | bytes 1572868
  336.1 71.6 %all-gather.16.cloned.1.call-start = ((), (), s32[]{:S(2)}) async-start(), calls=%async_computation.13 | async-start | bytes 4718592 | tf_op jit(solution)/shard_map/all_gather | solution.py:230
  376.8 173.6 %reduce-scatter.19.cloned.1.call-start = ((), (), s32[]{:S(2)}) async-start(), calls=%async_computation.17 | async-start | bytes 5242880
  511.9 127.9 %reduce-scatter.13.cloned.1.call-start = ((), (), s32[]{:S(2)}) async-start(), calls=%async_computation.14 | async-start | bytes 589824
  585.8 10.2 %copy-start.7 = (bf16[2,32,192,128]{3,2,1,0:T(8,128)(2,1)S(1)}, bf16[2,32,192,128]{3,2,1,0:T(8,128)(2,1)}, u32[]{:S(2)}) copy-start(bf16[2,32,192,128]{3,2,1,0:T(8,128)(2,1)} %get-tuple-element.21) | copy-start | bytes 9437188
  625.3 10.2 %copy-start.6 = (bf16[4096,512]{1,0:T(8,128)(2,1)S(1)}, bf16[4096,512]{1,0:T(8,128)(2,1)}, u32[]{:S(2)}) copy-start(bf16[4096,512]{1,0:T(8,128)(2,1)} %all-gather.16.cloned.1.call-done) | copy-start | bytes 12582916
  643.6 3.9 copy-start.5
  647.5 3.0 copy-start.3
  650.6 3.0 copy-start.4
  653.6 3.0 copy-start.2
  653.6 4.7 copy-start.1
Sparse Core Ops, SparseCore 0:
  9.8 33.5 all-gather.9
  135.6 38.2 reduce-scatter.14
  176.5 30.7 all-gather.11
  209.0 30.7 all-gather.13
  336.2 38.3 reduce-scatter.16
  377.0 30.7 all-gather.15
  512.0 38.3 reduce-scatter.18
  554.0 25.8 reduce-scatter.12

commit v2 on v1

--- a/solution.py
+++ b/solution.py
@@ -19,8 +19,8 @@
 
 
 def gate_hidden(x_rows, w_gate, w_up):
-    a_pre = matmul(x_rows, w_gate)
-    b_pre = matmul(x_rows, w_up)
+    a_pre = matmul(x_rows, w_gate, 1, 1)
+    b_pre = matmul(x_rows, w_up, 1, 1)
     return a_pre, b_pre, jax.nn.sigmoid(a_pre)
 
 
@@ -114,16 +114,16 @@
         grad_a = (grad_hidden * b_pre * sigma * (1.0 + a_pre * (1.0 - sigma))).astype(BF16)
         grad_b = (grad_hidden * silu).astype(BF16)
         x_half = x_ref[exp, :, cols]
-        grad_gate = matmul(x_half, grad_a, 0, 0).astype(BF16)
-        grad_up = matmul(x_half, grad_b, 0, 0).astype(BF16)
+        grad_gate = matmul(grad_a, x_half, 0, 0).astype(BF16)
+        grad_up = matmul(grad_b, x_half, 0, 0).astype(BF16)
         grad_down = matmul(hidden, d_ref[exp, :, cols], 0, 0).astype(BF16)
         for core in range(CORES):
             here = slice(core * piece, (core + 1) * piece)
-            gg_ref[core, exp] = grad_gate[here]
-            gu_ref[core, exp] = grad_up[here]
+            gg_ref[core, exp] = grad_gate[:, here]
+            gu_ref[core, exp] = grad_up[:, here]
             gd_ref[core, exp] = grad_down[:, here]
         kept = own * CAP
-        grad_x = (matmul(grad_a[:kept], w_gate, 1, 1) + matmul(grad_b[:kept], w_up, 1, 1)).astype(BF16)
+        grad_x = (matmul(grad_a[:kept], w_gate) + matmul(grad_b[:kept], w_up)).astype(BF16)
         at = pl.ds(pl.multiple_of(exp * CAP, CAP), CAP)
         for src in range(own):
             gx_ref[src, at, :] = grad_x[src * CAP:(src + 1) * CAP]
@@ -137,24 +137,23 @@
     groups = n_exp // GROUP
     whole = pl.BlockSpec((n_src, n_tok, dim), lambda g, w: (0, 0, 0), pipeline_mode=pl.Buffered(1))
     table = pl.BlockSpec((GROUP * n_src, n_tok), lambda g, w: (g, 0))
-    wide = pl.BlockSpec((GROUP, dim, ff), lambda g, w: (w[0] * groups + g, 0, 0))
     tall = pl.BlockSpec((GROUP, ff, dim), lambda g, w: (w[0] * groups + g, 0, 0))
     total = pl.BlockSpec((n_src // CHIPS, n_tok, dim), lambda g, w: (0, 0, 0), pipeline_mode=pl.Buffered(1))
-    return groups, whole, table, wide, tall, total
+    return groups, whole, table, tall, total
 
 
 def expert_forward(where, u_all, rank, gate, w_gate, w_up, w_down):
     n_src, n_tok, dim = u_all.shape
-    ff = w_gate.shape[2]
+    ff = w_gate.shape[1]
     n_exp = rank.shape[0] // n_src
     own = n_src // CHIPS
-    groups, whole, table, wide, tall, total = call_specs(n_src, n_tok, dim, ff, n_exp)
+    groups, whole, table, tall, total = call_specs(n_src, n_tok, dim, ff, n_exp)
     rows = n_exp * own * CAP
     return pl.pallas_call(
         forward_kernel,
         out_shape=jax.ShapeDtypeStruct((own, n_tok, dim), F32),
         grid_spec=pltpu.PrefetchScalarGridSpec(
-            num_scalar_prefetch=1, grid=(groups,), in_specs=[whole, table, table, wide, wide, tall], out_specs=total,
+            num_scalar_prefetch=1, grid=(groups,), in_specs=[whole, table, table, tall, tall, tall], out_specs=total,
             scratch_shapes=[pltpu.VMEM((own, GROUP * CAP, n_tok), BF16), pltpu.VMEM((GROUP, own * CAP, 128), F32),
                             pltpu.VMEM((GROUP, own * CAP, dim), BF16), pltpu.VMEM((own, 3, GROUP * CAP, dim), BF16)]),
         compiler_params=pltpu.CompilerParams(dimension_semantics=('arbitrary',), vmem_limit_bytes=56 << 20),
@@ -164,22 +163,20 @@
 
 def expert_backward(where, u_all, dy_all, rank, gate, w_gate, w_up, w_down):
     n_src, n_tok, dim = u_all.shape
-    ff = w_gate.shape[2]
+    ff = w_gate.shape[1]
     n_exp = rank.shape[0] // n_src
     own = n_src // CHIPS
     piece = dim // (CHIPS * CORES)
-    groups, whole, table, wide, tall, total = call_specs(n_src, n_tok, dim, ff, n_exp)
+    groups, whole, table, tall, total = call_specs(n_src, n_tok, dim, ff, n_exp)
     rows = n_exp * n_src * CAP
-    wide_out = pl.BlockSpec((CORES, GROUP, piece, ff), lambda g, w: (0, g, 0, 0))
     tall_out = pl.BlockSpec((CORES, GROUP, ff, piece), lambda g, w: (0, g, 0, 0))
-    wide_shape = jax.ShapeDtypeStruct((CORES, n_exp, piece, ff), BF16)
+    tall_shape = jax.ShapeDtypeStruct((CORES, n_exp, ff, piece), BF16)
     return pl.pallas_call(
         backward_kernel,
-        out_shape=(jax.ShapeDtypeStruct((own, n_tok, dim), F32), wide_shape, wide_shape,
-                   jax.ShapeDtypeStruct((CORES, n_exp, ff, piece), BF16)),
+        out_shape=(jax.ShapeDtypeStruct((own, n_tok, dim), F32), tall_shape, tall_shape, tall_shape),
         grid_spec=pltpu.PrefetchScalarGridSpec(
-            num_scalar_prefetch=1, grid=(groups,), in_specs=[whole, whole, table, table, wide, wide, tall],
-            out_specs=(total, wide_out, wide_out, tall_out),
+            num_scalar_prefetch=1, grid=(groups,), in_specs=[whole, whole, table, table, tall, tall, tall],
+            out_specs=(total, tall_out, tall_out, tall_out),
             scratch_shapes=[pltpu.VMEM((n_src, GROUP * CAP, n_tok), BF16), pltpu.VMEM((GROUP, n_src * CAP, dim), BF16),
                             pltpu.VMEM((GROUP, n_src * CAP, dim), BF16), pltpu.VMEM((own, GROUP * CAP, dim), BF16)]),
         compiler_params=pltpu.CompilerParams(dimension_semantics=('arbitrary',), vmem_limit_bytes=56 << 20),
@@ -221,6 +218,7 @@
 
     def local_step(tokens, dy_out, dense_w1, route_idx1, route_gate1, w_gate1, w_up1, w_down1, dense_w2, route_idx2, route_gate2, w_gate2, w_up2, w_down2):
         n_exp = w_gate1.shape[0] // CORES
+        w_gate1, w_up1, w_gate2, w_up2 = (jnp.swapaxes(w, 1, 2) for w in (w_gate1, w_up1, w_gate2, w_up2))
         ix, ic, iy = (lax.axis_index(name) for name in ALL)
         where = jnp.stack([ic, ix]).astype(jnp.int32)
         first_exp = (iy * CORES + ic) * n_exp
@@ -247,7 +245,7 @@
         u_two = mix(y_all, dense_w2)
         back, gg, gu, gd = expert_backward(where, u_two, dy_all, rank2, gates2, w_gate2, w_up2, w_down2)
         gm_two = (dy_out.astype(F32) + reduce_own(back)).astype(BF16)
-        gate_two, up_two, down_two = swap_cores(gg), swap_cores(gu), swap_cores(gd)
+        gate_two, up_two, down_two = jnp.swapaxes(swap_cores(gg), 1, 2), jnp.swapaxes(swap_cores(gu), 1, 2), swap_cores(gd)
         gm_all = gather(gm_two)
         rows = dense_w2.shape[0] // 8
         y_cols = lax.dynamic_slice_in_dim(y_all, me * rows, rows, 2)
@@ -255,7 +253,7 @@
         grad_mid = mix_back(gm_all, dense_w2)
         back, gg, gu, gd = expert_backward(where, u_one, grad_mid, rank1, gates1, w_gate1, w_up1, w_down1)
         gm_one = (lax.dynamic_index_in_dim(grad_mid, me, 0, keepdims=False).astype(F32) + reduce_own(back)).astype(BF16)
-        gate_one, up_one, down_one = swap_cores(gg), swap_cores(gu), swap_cores(gd)
+        gate_one, up_one, down_one = jnp.swapaxes(swap_cores(gg), 1, 2), jnp.swapaxes(swap_cores(gu), 1, 2), swap_cores(gd)
         grad_tok = mix_back(gm_one, dense_w1)
         dense_part = jnp.einsum('td,te->de', tokens, gm_one, preferred_element_type=F32).astype(BF16)
         dense_one = lax.psum_scatter(dense_part, ALL, scatter_dimension=0, tiled=True)

time: 668 us -> 598 us (0.90)
  local copies, waits for them, and re-layouts: 120 us -> 18.2 us
  waiting for transfers between devices: 163 us -> 211 us
  blocking collectives: 72.7 us -> 64.6 us
    unnamed x37 -> x41, local copies, waits for them, and re-layouts: 95.4 us -> 18.2 us
    all_gather x4, waiting for transfers between devices: 46.6 us -> 93.2 us  [gather(): return lax.all_gather(value, ALL, axis=0, tiled=False)]
    pallas_call x4 -> x0, local copies, waits for them, and re-layouts: 24.4 us -> none  [expert_backward(): pl.pallas_call(backward_kernel, out_shape=(jax.ShapeDtypeStruct((own, n_t...]
    all_to_all x6, blocking collectives: 57.6 us -> 47.1 us  [swap_cores(): moved = lax.all_to_all(parts, 'c', 0, 0, tiled=True)]
  transfers between devices with their start and end apart: 8 -> 8, of which waited for: 5 -> 7; matrix products, arithmetic and copies ran while one was open for 19% -> 4% of each run, Pallas kernels for 0% -> 0%
where the time goes in v2:
time: 598 us; the launch traced here: 597 us
  Pallas kernels  242 us (40%)
  waiting for transfers between devices  211 us (35%)
  blocking collectives  64.6 us (11%)
  matrix products  32.9 us (6%)
  local copies, waits for them, and re-layouts  18.2 us (3%)
  between operations  14.3 us (2%)
  other arithmetic  14 us (2%)
    pallas_call x2, Pallas kernels, expert_backward(): pl.pallas_call(backward_kernel, out_shape=(jax.ShapeDtypeStruct((own, n_t...  186 us
    unnamed x12, waiting for transfers between devices  118 us
    all_gather x4, waiting for transfers between devices, gather(): return lax.all_gather(value, ALL, axis=0, tiled=False)  93.2 us
    pallas_call x1, Pallas kernels, expert_forward(): pl.pallas_call(forward_kernel, out_shape=jax.ShapeDtypeStruct((own, n_tok...  55.8 us
    all_to_all x6, blocking collectives, swap_cores(): moved = lax.all_to_all(parts, 'c', 0, 0, tiled=True)  47.1 us
    unnamed x41, local copies, waits for them, and re-layouts  18.2 us
    dot_general x3, matrix products, mix(): jnp.einsum('...d,de->...e', x, weight, preferred_element_type=F32)  18 us
    all_gather x1, blocking collectives, gather(): return lax.all_gather(value, ALL, axis=0, tiled=False)  17.5 us
  transfers between devices with their start and end apart: 8, of which 7 were waited for; matrix products, arithmetic and copies ran while one was open for 4% of the time, Pallas kernels for 0%

profile of v2, /device:TPU:0, one launch (start us, length us, event | category | flops | bytes accessed | tf_op | source)
XLA Modules:
  0.0 597.4 jit_solution(7124976318306892417)
XLA Ops:
  10.8 17.5 %all-gather.1 = f32[256,512]{1,0:T(8,128)S(1)} all-gather(f32[32,512]{1,0:T(8,128)S(1)} %maximum_bitcast_fusion), channel_id=3, replica_groups=mesh['y'=2,'x'=2,'c'=2] {'x','c','y'}, dimensions={0}, use_global_device_ids=true | all-gather | bytes 589824 | tf_op jit(solution)/shard_map/all_gather | solution.py:228
  28.4 3.8 compare_reduce_fusion
  33.3 3.7 fusion.1
  37.0 8.7 %all-gather.10.cloned.1.call-done = bf16[4096,512]{1,0:T(8,128)(2,1)} async-done(((bf16[512,512]{1,0:T(8,128)(2,1)}), bf16[4096,512]{1,0:T(8,128)(2,1)}) %all-gather.10.cloned.1.call-update) | async-done | bytes 4194320 | tf_op jit(solution)/shard_map/all_gather | solution.py:228
  45.6 7.8 %add_convert_fusion.2.u_ref = bf16[8,512,512]{2,1,0:T(8,128)(2,1)} fusion(bf16[8,512,512]{2,1,0:T(8,128)(2,1)} %bitcast.93, bf16[512,512]{1,0:T(8,128)(2,1)S(1)} %copy-done.13), kind=kOutput, calls=%fused_computation.2 | convolution fusion | flops 2153775104 | bytes 8912896 | tf_op jit(solution)/shard_map/...d,de->...e/dot_general | solution.py:200
  53.5 55.8 %shard_map.205 = f32[4,512,512]{2,1,0:T(8,128)} custom-call(s32[2]{0:T(128)} %pad_add_fusion.where_ref, bf16[8,512,512]{2,1,0:T(8,128)(2,1)} %add_convert_fusion.2.u_ref, s32[256,512]{1,0:T(8,128)} %fusion.10.rank_ref, f32[256,512]{1,0:T(8,128)} %bitcast.82, bf16[64,192,512]{2,1,0:T(8,128)(2,1)} %bitcast.89, bf16[64,192,512]{2,1,0:T(8,128)(2,1)} %bitcast.91, ...), custom_call_target="tpu_custom_call" | custom-call | flops 22011707392 | bytes 41943040 | tf_op jit(solution)/shard_map/pallas_call | solution.py:152
  109.3 38.4 %reduce-scatter.15.cloned.1.call-done = f32[1,512,512]{2,1,0:T(8,128)} async-done(((f32[4,512,512]{2,1,0:T(8,128)}), f32[1,512,512]{2,1,0:T(8,128)}) %reduce-scatter.15.cloned.1.call-update) | async-done | bytes 1048592
  152.1 29.0 %all-gather.12.cloned.1.call-done = bf16[4096,512]{1,0:T(8,128)(2,1)} async-done(((bf16[512,512]{1,0:T(8,128)(2,1)}), bf16[4096,512]{1,0:T(8,128)(2,1)}) %all-gather.12.cloned.1.call-update) | async-done | bytes 4194320 | tf_op jit(solution)/shard_map/all_gather | solution.py:228
  181.1 7.7 %add_convert_fusion.1.u_ref = bf16[8,512,512]{2,1,0:T(8,128)(2,1)} fusion(bf16[8,512,512]{2,1,0:T(8,128)(2,1)} %bitcast.85, bf16[512,512]{1,0:T(8,128)(2,1)S(1)} %copy-done), kind=kOutput, calls=%fused_computation.1 | convolution fusion | flops 2153775104 | bytes 8912896 | tf_op jit(solution)/shard_map/...d,de->...e/dot_general | solution.py:200
  188.9 24.7 %all-gather.14.cloned.1.call-done = bf16[4096,512]{1,0:T(8,128)(2,1)} async-done(((bf16[512,512]{1,0:T(8,128)(2,1)}), bf16[4096,512]{1,0:T(8,128)(2,1)}) %all-gather.14.cloned.1.call-update) | async-done | bytes 4194320 | tf_op jit(solution)/shard_map/all_gather | solution.py:228
  213.6 93.2 %shard_map.206 = (f32[4,512,512]{2,1,0:T(8,128)}, bf16[2,32,192,128]{3,2,1,0:T(8,128)(2,1)}, bf16[2,32,192,128]{3,2,1,0:T(8,128)(2,1)}, bf16[2,32,192,128]{3,2,1,0:T(8,128)(2,1)}) custom-call(s32[2]{0:T(128)} %pad_add_fusion.where_ref, bf16[8,512,512]{2,1,0:T(8,128)(2,1)} %add_convert_fusion.1.u_ref, bf16[8,512,512]{2,1,0:T(8,128)(2,1)} %bitcast.94, ...), custom_call_target="tpu_custom_call" | custom-call | flops 39191576576 | bytes 62914560 | tf_op jit(solution)/shard_map/pallas_call | solution.py:174
  306.8 38.9 %reduce-scatter.17.cloned.1.call-done = f32[1,512,512]{2,1,0:T(8,128)} async-done(((f32[4,512,512]{2,1,0:T(8,128)}), f32[1,512,512]{2,1,0:T(8,128)}) %reduce-scatter.17.cloned.1.call-update) | async-done | bytes 1048592
  348.0 30.8 %all-gather.16.cloned.1.call-done = bf16[4096,512]{1,0:T(8,128)(2,1)} async-done(((bf16[512,512]{1,0:T(8,128)(2,1)}), bf16[4096,512]{1,0:T(8,128)(2,1)}) %all-gather.16.cloned.1.call-update) | async-done | bytes 4194320 | tf_op jit(solution)/shard_map/all_gather | solution.py:228
  378.9 7.8 %add_convert_fusion.dy_ref = bf16[8,512,512]{2,1,0:T(8,128)(2,1)} fusion(bf16[8,512,512]{2,1,0:T(8,128)(2,1)} %bitcast.79, bf16[512,512]{1,0:T(8,128)(2,1)S(1)} %copy-done), kind=kOutput, calls=%fused_computation | convolution fusion | flops 2153775104 | bytes 8912896 | tf_op jit(solution)/shard_map/...e,de->...d/dot_general | solution.py:204
  386.6 93.2 %shard_map.207 = (f32[4,512,512]{2,1,0:T(8,128)}, bf16[2,32,192,128]{3,2,1,0:T(8,128)(2,1)}, bf16[2,32,192,128]{3,2,1,0:T(8,128)(2,1)}, bf16[2,32,192,128]{3,2,1,0:T(8,128)(2,1)}) custom-call(s32[2]{0:T(128)} %pad_add_fusion.where_ref, bf16[8,512,512]{2,1,0:T(8,128)(2,1)} %add_convert_fusion.2.u_ref, bf16[8,512,512]{2,1,0:T(8,128)(2,1)} %add_convert_fusion.dy_ref, ...), custom_call_target="tpu_custom_call" | custom-call | flops 39191576576 | bytes 62914560 | tf_op jit(solution)/shard_map/pallas_call | solution.py:174
  479.9 39.0 %reduce-scatter.19.cloned.1.call-done = f32[1,512,512]{2,1,0:T(8,128)} async-done(((f32[4,512,512]{2,1,0:T(8,128)}), f32[1,512,512]{2,1,0:T(8,128)}) %reduce-scatter.19.cloned.1.call-update) | async-done | bytes 1048592
  522.7 7.5 %all_to_all.30 = bf16[2,32,192,128]{3,2,1,0:T(8,128)(2,1)S(1)} all-to-all(bf16[2,32,192,128]{3,2,1,0:T(8,128)(2,1)} %get-tuple-element.22), channel_id=1, replica_groups=mesh['y'=2,'x'=2,'c'=2] {'c'}, dimensions={0} | all-to-all | bytes 6291456 | tf_op jit(solution)/shard_map/all_to_all | solution.py:208
  530.2 10.2 %all_to_all.31 = bf16[2,32,192,128]{3,2,1,0:T(8,128)(2,1)} all-to-all(bf16[2,32,192,128]{3,2,1,0:T(8,128)(2,1)} %get-tuple-element.23), channel_id=1, replica_groups=mesh['y'=2,'x'=2,'c'=2] {'c'}, dimensions={0} | all-to-all | bytes 6291456 | tf_op jit(solution)/shard_map/all_to_all | solution.py:208
  540.4 7.3 %all_to_all.32 = bf16[2,32,192,128]{3,2,1,0:T(8,128)(2,1)} all-to-all(bf16[2,32,192,128]{3,2,1,0:T(8,128)(2,1)S(1)} %copy-done.7), channel_id=1, replica_groups=mesh['y'=2,'x'=2,'c'=2] {'c'}, dimensions={0} | all-to-all | bytes 6291456 | tf_op jit(solution)/shard_map/all_to_all | solution.py:208
  547.8 7.3 %all_to_all.33 = bf16[2,32,192,128]{3,2,1,0:T(8,128)(2,1)} all-to-all(bf16[2,32,192,128]{3,2,1,0:T(8,128)(2,1)S(1)} %copy-done.10), channel_id=1, replica_groups=mesh['y'=2,'x'=2,'c'=2] {'c'}, dimensions={0} | all-to-all | bytes 6291456 | tf_op jit(solution)/shard_map/all_to_all | solution.py:208
  555.1 7.3 %all_to_all.34 = bf16[2,32,192,128]{3,2,1,0:T(8,128)(2,1)} all-to-all(bf16[2,32,192,128]{3,2,1,0:T(8,128)(2,1)S(1)} %copy-done.9), channel_id=1, replica_groups=mesh['y'=2,'x'=2,'c'=2] {'c'}, dimensions={0} | all-to-all | bytes 6291456 | tf_op jit(solution)/shard_map/all_to_all | solution.py:208
  562.4 7.3 %all_to_all.35 = bf16[2,32,192,128]{3,2,1,0:T(8,128)(2,1)} all-to-all(bf16[2,32,192,128]{3,2,1,0:T(8,128)(2,1)S(1)} %copy-done.8), channel_id=1, replica_groups=mesh['y'=2,'x'=2,'c'=2] {'c'}, dimensions={0} | all-to-all | bytes 6291456 | tf_op jit(solution)/shard_map/all_to_all | solution.py:208
  569.8 3.2 fusion.12
  574.2 3.9 copy.38
  (70 shorter events, 29.0 us)
Async XLA Ops:
  7.2 173.9 %copy-start = (bf16[512,512]{1,0:T(8,128)(2,1)S(1)}, bf16[512,512]{1,0:T(8,128)(2,1)}, u32[]{:S(2)}) copy-start(bf16[512,512]{1,0:T(8,128)(2,1)} %param.22) | copy-start | bytes 1572868
  7.2 38.5 %copy-start.13 = (bf16[512,512]{1,0:T(8,128)(2,1)S(1)}, bf16[512,512]{1,0:T(8,128)(2,1)}, u32[]{:S(2)}) copy-start(bf16[512,512]{1,0:T(8,128)(2,1)} %param.16) | copy-start | bytes 1572868
  7.2 38.4 %all-gather.10.cloned.1.call-start = ((), (), s32[]{:S(2)}) async-start(), calls=%async_computation.10 | async-start | bytes 4718592 | tf_op jit(solution)/shard_map/all_gather | solution.py:228
  7.9 139.8 %reduce-scatter.15.cloned.1.call-start = ((), (), s32[]{:S(2)}) async-start(), calls=%async_computation.15 | async-start | bytes 5242880
  109.2 38.5 %copy-start.11 = (bf16[512,512]{1,0:T(8,128)(2,1)S(1)}, bf16[512,512]{1,0:T(8,128)(2,1)}, u32[]{:S(2)}) copy-start(bf16[512,512]{1,0:T(8,128)(2,1)} %param.14) | copy-start | bytes 1572868
  109.3 71.8 %all-gather.12.cloned.1.call-start = ((), (), s32[]{:S(2)}) async-start(), calls=%async_computation.11 | async-start | bytes 4718592 | tf_op jit(solution)/shard_map/all_gather | solution.py:228
  150.2 63.4 %all-gather.14.cloned.1.call-start = ((), (), s32[]{:S(2)}) async-start(), calls=%async_computation.12 | async-start | bytes 4718592 | tf_op jit(solution)/shard_map/all_gather | solution.py:228
  150.8 195.0 %reduce-scatter.17.cloned.1.call-start = ((), (), s32[]{:S(2)}) async-start(), calls=%async_computation.16 | async-start | bytes 5242880
  306.7 39.0 %copy-start.12 = (bf16[512,512]{1,0:T(8,128)(2,1)S(1)}, bf16[512,512]{1,0:T(8,128)(2,1)}, u32[]{:S(2)}) copy-start(bf16[512,512]{1,0:T(8,128)(2,1)} %param.15) | copy-start | bytes 1572868
  306.8 72.1 %all-gather.16.cloned.1.call-start = ((), (), s32[]{:S(2)}) async-start(), calls=%async_computation.13 | async-start | bytes 4718592 | tf_op jit(solution)/shard_map/all_gather | solution.py:228
  348.0 170.9 %reduce-scatter.19.cloned.1.call-start = ((), (), s32[]{:S(2)}) async-start(), calls=%async_computation.17 | async-start | bytes 5242880
  479.8 94.4 %reduce-scatter.13.cloned.1.call-start = ((), (), s32[]{:S(2)}) async-start(), calls=%async_computation.14 | async-start | bytes 589824
  530.2 10.2 %copy-start.7 = (bf16[2,32,192,128]{3,2,1,0:T(8,128)(2,1)S(1)}, bf16[2,32,192,128]{3,2,1,0:T(8,128)(2,1)}, u32[]{:S(2)}) copy-start(bf16[2,32,192,128]{3,2,1,0:T(8,128)(2,1)} %get-tuple-element.24) | copy-start | bytes 9437188
  540.4 7.4 %copy-start.10 = (bf16[2,32,192,128]{3,2,1,0:T(8,128)(2,1)S(1)}, bf16[2,32,192,128]{3,2,1,0:T(8,128)(2,1)}, u32[]{:S(2)}) copy-start(bf16[2,32,192,128]{3,2,1,0:T(8,128)(2,1)} %get-tuple-element.19) | copy-start | bytes 9437188
  547.8 7.3 %copy-start.9 = (bf16[2,32,192,128]{3,2,1,0:T(8,128)(2,1)S(1)}, bf16[2,32,192,128]{3,2,1,0:T(8,128)(2,1)}, u32[]{:S(2)}) copy-start(bf16[2,32,192,128]{3,2,1,0:T(8,128)(2,1)} %get-tuple-element.20) | copy-start | bytes 9437188
  555.1 7.3 %copy-start.8 = (bf16[2,32,192,128]{3,2,1,0:T(8,128)(2,1)S(1)}, bf16[2,32,192,128]{3,2,1,0:T(8,128)(2,1)}, u32[]{:S(2)}) copy-start(bf16[2,32,192,128]{3,2,1,0:T(8,128)(2,1)} %get-tuple-element.21) | copy-start | bytes 9437188
  562.4 7.3 %copy-start.6 = (bf16[4096,512]{1,0:T(8,128)(2,1)S(1)}, bf16[4096,512]{1,0:T(8,128)(2,1)}, u32[]{:S(2)}) copy-start(bf16[4096,512]{1,0:T(8,128)(2,1)} %all-gather.16.cloned.1.call-done) | copy-start | bytes 12582916
  569.8 3.2 copy-start.14
  569.8 3.2 copy-start.16
  574.2 3.9 copy-start.4
  578.1 3.0 copy-start.5
  582.8 3.0 copy-start.2
  585.8 3.0 copy-start.3
  585.9 4.7 copy-start.1
  (1 other events, 0.8 us)
Sparse Core Ops, SparseCore 0:
  9.8 35.7 all-gather.9
  109.4 38.2 reduce-scatter.14
  150.3 30.7 all-gather.11
  182.8 30.7 all-gather.13
  306.9 38.8 reduce-scatter.16
  348.1 30.7 all-gather.15
  480.0 38.8 reduce-scatter.18
  522.8 25.8 reduce-scatter.12

commit v3 on v2

v3 whole, which is shorter than its diff:
```python
import functools

import jax
import jax.numpy as jnp
from jax import lax
from jax.experimental import pallas as pl
from jax.experimental.pallas import tpu as pltpu
from jax.sharding import Mesh, PartitionSpec as P

F32 = jnp.float32
BF16 = jnp.bfloat16
CAP = 64
GROUP = 4
CORES = 2
CHIPS = 2
ALL = ('x', 'c', 'y')


def matmul(lhs, rhs, lhs_dim=1, rhs_dim=0):
    return lax.dot_general(lhs, rhs, (((lhs_dim,), (rhs_dim,)), ((), ())), preferred_element_type=F32)


def gate_hidden(x_rows, w_gate, w_up):
    a_pre = matmul(x_rows, w_gate, 1, 1)
    b_pre = matmul(x_rows, w_up, 1, 1)
    return a_pre, b_pre, jax.nn.sigmoid(a_pre)


def select_rows(rank_ref, gate_ref, group, src):
    n_tok = rank_ref.shape[-1]
    slot = lax.broadcasted_iota(jnp.int32, (CAP, n_tok), 0)
    picks, gates = [], []
    for exp in range(GROUP):
        row = pl.ds(group * GROUP + exp, 1)
        hit = slot == rank_ref[src, row, :]
        picks.append(jnp.where(hit, 1.0, 0.0).astype(BF16))
        gates.append(jnp.sum(jnp.where(hit, gate_ref[src, row, :], 0.0), axis=1, keepdims=True))
    return jnp.concatenate(picks, axis=0), jnp.concatenate(gates, axis=0)


def forward_kernel(where_ref, u_ref, rank_ref, gate_ref, wg_ref, wu_ref, wd_ref, out_ref, pick_ref, row_ref, x_ref, part_ref):
    n_src = u_ref.shape[0]
    own = n_src // CHIPS
    first = where_ref[1] * own

    @pl.when(pl.program_id(0) == 0)
    def _():
        out_ref[...] = jnp.zeros_like(out_ref)

    @pl.loop(0, own)
    def _(src):
        pick, gate = select_rows(rank_ref, gate_ref, pl.program_id(0), first + src)
        pick_ref[src] = pick
        rows = matmul(pick, u_ref[first + src]).astype(BF16)
        at = pl.ds(pl.multiple_of(src * CAP, CAP), CAP)
        for exp in range(GROUP):
            x_ref[exp, at, :] = rows[exp * CAP:(exp + 1) * CAP]
            row_ref[exp, at, :] = jnp.broadcast_to(gate[exp * CAP:(exp + 1) * CAP], (CAP, 128))

    @pl.loop(0, GROUP)
    def _(exp):
        a_pre, b_pre, sigma = gate_hidden(x_ref[exp], wg_ref[exp], wu_ref[exp])
        hidden = (a_pre * sigma * b_pre).astype(BF16)
        out = matmul(hidden, wd_ref[exp]).astype(BF16).astype(F32) * row_ref[exp][:, :1]
        high = out.astype(BF16)
        rest = out - high.astype(F32)
        mid = rest.astype(BF16)
        low = (rest - mid.astype(F32)).astype(BF16)
        at = pl.ds(pl.multiple_of(exp * CAP, CAP), CAP)
        for src in range(own):
            here = slice(src * CAP, (src + 1) * CAP)
            part_ref[src, 0, at, :] = high[here]
            part_ref[src, 1, at, :] = mid[here]
            part_ref[src, 2, at, :] = low[here]

    @pl.loop(0, own)
    def _(src):
        pick = pick_ref[src]
        total = matmul(pick, part_ref[src, 0], 0, 0)
        total += matmul(pick, part_ref[src, 1], 0, 0) + matmul(pick, part_ref[src, 2], 0, 0)
        out_ref[src] += total


def layer_kernel(gather_input, whole_ref, mine_ref, rank_ref, gate_ref, wg_ref, wu_ref, wd_ref,
                 total_ref, gg_ref, gu_ref, gd_ref,
                 peer_ref, xo_ref, do_ref, h_ref, ga_ref, gb_ref, pick_ref, gx_ref, p_ref, rs_ref, x_ref, d_ref, stage_ref,
                 ag_send, ag_recv, rs_send, rs_recv, keep_sem, give_send, give_recv):
    n_src, _, dim = whole_ref.shape
    own = n_src // CHIPS
    n_group = xo_ref.shape[0] // GROUP
    half = dim // CHIPS
    piece = half // CORES
    step = pl.program_id(0)
    ix, ic, iy = (lax.axis_index(name) for name in ALL)
    cols = pl.ds(pl.multiple_of(ix * half, half), half)
    u_ref, dy_ref = (peer_ref, whole_ref) if gather_input else (whole_ref, peer_ref)
    outs = (gg_ref, gu_ref, gd_ref)

    def slot(flip_x=False, flip_y=False):
        x = 1 - ix if flip_x else ix
        y = 1 - iy if flip_y else iy
        return (x * CORES + ic) * 2 + y

    def send(src, dst, sems, at, axis):
        other = 1 - lax.axis_index(axis)
        return pltpu.make_async_remote_copy(src, dst, sems[0].at[at], sems[1].at[at], device_id={axis: other},
                                            device_id_type=pl.DeviceIdType.MESH)

    def spread(at):
        flips = ((0, 0), (0, 0), (0, 1), (0, 0), (0, 1), (1, 0), (1, 1))[at]
        block = peer_ref.at[slot(*flips)]
        return send(block if any(flips) else mine_ref, block, (ag_send, ag_recv), at, 'yxxcccc'[at])

    def add_up(at):
        part = ((1 - ic) * 2 + 1 - iy, (1 - ic) * 2 + iy, ic * 2 + 1 - iy)[at]
        return send(p_ref.at[part], rs_ref.at[at], (rs_send, rs_recv), at, 'ccy'[at])

    def store_copies(group):
        buf = lax.rem(group, 2)
        rows = pl.ds(ic * n_group * GROUP + group * GROUP, GROUP)
        pairs = []
        for kind in range(3):
            dst = outs[kind].at[rows]
            pairs.append(pltpu.make_async_copy(stage_ref.at[buf, ic, kind], dst, keep_sem.at[buf, kind]))
            pairs.append(pltpu.make_async_remote_copy(
                stage_ref.at[buf, 1 - ic, kind], dst, give_send.at[buf, kind], give_recv.at[group, kind],
                device_id={'c': 1 - ic}, device_id_type=pl.DeviceIdType.MESH))
        return pairs

    def store_start(group):
        for copy in store_copies(group):
            copy.start()

    def store_wait(group):
        keep = store_copies(group)
        for at in range(0, len(keep), 2):
            keep[at].wait()
            keep[at + 1].wait_send()

    def pull(first, group, x_dst, d_dst, base, keep_pick):
        @pl.loop(0, own)
        def _(src):
            pick, gate = select_rows(rank_ref, gate_ref, group, first + src)
            if keep_pick:
                pick_ref[src] = pick
            x_rows = matmul(pick, u_ref[first + src]).astype(BF16)
            d_rows = (matmul(pick, dy_ref[first + src]) * gate).astype(BF16)
            at = pl.ds(pl.multiple_of(src * CAP, CAP), CAP)
            for exp in range(GROUP):
                x_dst[base + exp, at, :] = x_rows[exp * CAP:(exp + 1) * CAP]
                d_dst[base + exp, at, :] = d_rows[exp * CAP:(exp + 1) * CAP]

    def hidden_grads(x_rows, d_rows, exp):
        a_pre, b_pre, sigma = gate_hidden(x_rows, wg_ref[exp], wu_ref[exp])
        silu = a_pre * sigma
        grad_hidden = matmul(d_rows, wd_ref[exp], 1, 1).astype(BF16).astype(F32)
        grad_a = (grad_hidden * b_pre * sigma * (1.0 + a_pre * (1.0 - sigma))).astype(BF16)
        return (silu * b_pre).astype(BF16), grad_a, (grad_hidden * silu).astype(BF16)

    @pl.when(step == 0)
    def _():
        barrier = pltpu.get_barrier_semaphore()
        for axis in ALL:
            pl.semaphore_signal(barrier, inc=1, device_id={axis: 1 - lax.axis_index(axis)}, device_id_type=pl.DeviceIdType.MESH)
        pl.semaphore_wait(barrier, len(ALL))
        for at in (0, 1, 3):
            spread(at).start()
        peer_ref[slot()] = mine_ref[...]
        p_ref[...] = jnp.zeros_like(p_ref)
        spread(0).wait_recv()
        spread(4).start()
        spread(2).start()
        spread(3).wait_recv()
        spread(4).wait_recv()

    @pl.when(step == n_group // 2)
    def _():
        spread(1).wait_recv()
        spread(5).start()

    @pl.when(step == n_group - 1)
    def _():
        spread(2).wait_recv()
        spread(6).start()

    @pl.when(step < n_group)
    def _():
        base = step * GROUP
        pull(ix * own, step, xo_ref, do_ref, base, True)

        @pl.loop(0, GROUP)
        def _(exp):
            hidden, grad_a, grad_b = hidden_grads(xo_ref[base + exp], do_ref[base + exp], exp)
            h_ref[base + exp] = hidden
            ga_ref[base + exp] = grad_a
            gb_ref[base + exp] = grad_b
            grad_x = (matmul(grad_a, wg_ref[exp]) + matmul(grad_b, wu_ref[exp])).astype(BF16)
            at = pl.ds(pl.multiple_of(exp * CAP, CAP), CAP)
            for src in range(own):
                gx_ref[src, at, :] = grad_x[src * CAP:(src + 1) * CAP]

        @pl.loop(0, own)
        def _(src):
            p_ref[src] += matmul(pick_ref[src], gx_ref[src], 0, 0)

    @pl.when(step == n_group)
    def _():
        add_up(0).start()
        add_up(1).start()
        spread(5).wait_recv()
        spread(6).wait_recv()

    @pl.when(step == n_group + 1)
    def _():
        add_up(0).wait_recv()
        p_ref[ic * 2 + 1 - iy] += rs_ref[0]

    @pl.when(step == n_group + 2)
    def _():
        add_up(2).start()

    @pl.when(step >= n_group)
    def _():
        group = step - n_group

        @pl.when(group >= 1)
        def _():
            store_start(group - 1)

        pull((1 - ix) * own, group, x_ref, d_ref, 0, False)

        @pl.when(group >= 2)
        def _():
            store_wait(group - 2)

        buf = lax.rem(group, 2)

        @pl.loop(0, GROUP)
        def _(exp):
            base = group * GROUP + exp
            hidden, grad_a, grad_b = hidden_grads(x_ref[exp], d_ref[exp], exp)
            x_own, x_far = xo_ref[base, :, cols], x_ref[exp, :, cols]
            d_own, d_far = do_ref[base, :, cols], d_ref[exp, :, cols]
            grads = (matmul(ga_ref[base], x_own, 0, 0) + matmul(grad_a, x_far, 0, 0),
                     matmul(gb_ref[base], x_own, 0, 0) + matmul(grad_b, x_far, 0, 0),
                     matmul(h_ref[base], d_own, 0, 0) + matmul(hidden, d_far, 0, 0))
            for kind in range(3):
                for core in range(CORES):
                    stage_ref[buf, core, kind, exp] = grads[kind][:, core * piece:(core + 1) * piece].astype(BF16)

    @pl.when(step == 2 * n_group - 1)
    def _():
        last = n_group - 1
        store_wait(last - 1)
        add_up(1).wait_recv()
        add_up(2).wait_recv()
        total_ref[...] = p_ref[ic * 2 + iy] + rs_ref[1] + rs_ref[2]
        store_start(last)
        for at in range(7):
            spread(at).wait_send()
        for at in range(3):
            add_up(at).wait_send()
        store_wait(last)
        for group in range(n_group):
            for copy in store_copies(group)[1::2]:
                copy.wait_recv()


def expert_forward(where, u_all, rank, gate, w_gate, w_up, w_down):
    n_src, n_tok, dim = u_all.shape
    ff = w_gate.shape[1]
    n_exp = rank.shape[1]
    own = n_src // CHIPS
    groups = n_exp // GROUP
    rows = n_exp * own * CAP
    whole = pl.BlockSpec((n_src, n_tok, dim), lambda g, w: (0, 0, 0), pipeline_mode=pl.Buffered(1))
    table = pl.BlockSpec((n_src, n_exp, n_tok), lambda g, w: (0, 0, 0), pipeline_mode=pl.Buffered(1))
    tall = pl.BlockSpec((GROUP, ff, dim), lambda g, w: (w[0] * groups + g, 0, 0))
    total = pl.BlockSpec((own, n_tok, dim), lambda g, w: (0, 0, 0), pipeline_mode=pl.Buffered(1))
    return pl.pallas_call(
        forward_kernel,
        out_shape=jax.ShapeDtypeStruct((own, n_tok, dim), F32),
        grid_spec=pltpu.PrefetchScalarGridSpec(
            num_scalar_prefetch=1, grid=(groups,), in_specs=[whole, table, table, tall, tall, tall], out_specs=total,
            scratch_shapes=[pltpu.VMEM((own, GROUP * CAP, n_tok), BF16), pltpu.VMEM((GROUP, own * CAP, 128), F32),
                            pltpu.VMEM((GROUP, own * CAP, dim), BF16), pltpu.VMEM((own, 3, GROUP * CAP, dim), BF16)]),
        compiler_params=pltpu.CompilerParams(dimension_semantics=('arbitrary',), vmem_limit_bytes=56 << 20),
        cost_estimate=pl.CostEstimate(flops=rows * dim * (8 * n_tok + 6 * ff), bytes_accessed=40 << 20, transcendentals=0),
    )(where, u_all, rank, gate, w_gate, w_up, w_down)


def layer_backward(gather_input, whole, mine, rank, gate, w_gate, w_up, w_down):
    n_src, n_tok, dim = whole.shape
    n_all, ff, _ = w_gate.shape
    n_exp = rank.shape[1]
    own = n_src // CHIPS
    piece = dim // (CHIPS * CORES)
    groups = n_exp // GROUP
    rows = n_exp * n_src * CAP

    def fixed(*shape):
        return pl.BlockSpec(shape, lambda s: (0,) * len(shape), pipeline_mode=pl.Buffered(1))

    tall = pl.BlockSpec((GROUP, ff, dim), lambda s: (lax.axis_index('c') * groups + lax.rem(s, groups), 0, 0))
    grad_shape = jax.ShapeDtypeStruct((n_all, ff, piece), BF16)
    kept = own * CAP
    return pl.pallas_call(
        functools.partial(layer_kernel, gather_input),
        out_shape=(jax.ShapeDtypeStruct((n_tok, dim), F32), grad_shape, grad_shape, grad_shape),
        grid_spec=pltpu.PrefetchScalarGridSpec(
            num_scalar_prefetch=0, grid=(2 * groups,),
            in_specs=[fixed(n_src, n_tok, dim), fixed(n_tok, dim), fixed(n_src, n_exp, n_tok), fixed(n_src, n_exp, n_tok), tall, tall, tall],
            out_specs=(fixed(n_tok, dim),) + (pl.BlockSpec(memory_space=pl.ANY),) * 3,
            scratch_shapes=[pltpu.VMEM((n_src, n_tok, dim), BF16), pltpu.VMEM((n_exp, kept, dim), BF16),
                            pltpu.VMEM((n_exp, kept, dim), BF16), pltpu.VMEM((n_exp, kept, ff), BF16),
                            pltpu.VMEM((n_exp, kept, ff), BF16), pltpu.VMEM((n_exp, kept, ff), BF16),
                            pltpu.VMEM((own, GROUP * CAP, n_tok), BF16), pltpu.VMEM((own, GROUP * CAP, dim), BF16),
                            pltpu.VMEM((own, n_tok, dim), F32), pltpu.VMEM((3, n_tok, dim), F32),
                            pltpu.VMEM((GROUP, kept, dim), BF16), pltpu.VMEM((GROUP, kept, dim), BF16),
                            pltpu.VMEM((2, CORES, 3, GROUP, ff, piece), BF16),
                            pltpu.SemaphoreType.DMA((7,)), pltpu.SemaphoreType.DMA((7,)),
                            pltpu.SemaphoreType.DMA((3,)), pltpu.SemaphoreType.DMA((3,)),
                            pltpu.SemaphoreType.DMA((2, 3)), pltpu.SemaphoreType.DMA((2, 3)), pltpu.SemaphoreType.DMA((groups, 3))]),
        compiler_params=pltpu.CompilerParams(dimension_semantics=('arbitrary',), vmem_limit_bytes=62 << 20,
                                             collective_id=int(gather_input), has_side_effects=True),
        cost_estimate=pl.CostEstimate(flops=rows * dim * (5 * n_tok + 11 * ff), bytes_accessed=60 << 20, transcendentals=0),
    )(whole, mine, rank, gate, w_gate, w_up, w_down)


def route_tables(idx, gate, first_exp, n_exp):
    n_src, _, n_tok = idx.shape
    experts = (first_exp + jnp.arange(n_exp, dtype=jnp.int32)).astype(F32)
    hit = idx[:, None] == experts[None, :, None, None]
    member = jnp.any(hit, axis=2)
    gates = jnp.sum(jnp.where(hit, gate[:, None], 0.0), axis=2)
    before = jnp.triu(jnp.ones((n_tok, n_tok), BF16), 1)
    count = jnp.einsum('set,tv->sev', member.astype(BF16), before, preferred_element_type=F32)
    return jnp.where(member, count.astype(jnp.int32), -1), gates


def mix(x, weight):
    return (x.astype(F32) + jnp.einsum('...d,de->...e', x, weight, preferred_element_type=F32)).astype(BF16)


def mix_back(grad, weight):
    return (grad.astype(F32) + jnp.einsum('...e,de->...d', grad, weight, preferred_element_type=F32)).astype(BF16)


def solution(mesh):
    fine = Mesh(mesh.devices.reshape(2, CHIPS, CORES), ('y', 'x', 'c'))
    tok_spec = P(ALL, None)
    exp_spec = P('y', None, None)
    layer_specs = (P(None, None), tok_spec, tok_spec, exp_spec, exp_spec, exp_spec)
    grad_specs = (P(ALL, None), P('y', ('x', 'c'), None), P('y', ('x', 'c'), None), P('y', None, ('x', 'c')))

    def local_step(tokens, dy_out, dense_w1, route_idx1, route_gate1, w_gate1, w_up1, w_down1, dense_w2, route_idx2, route_gate2, w_gate2, w_up2, w_down2):
        n_exp = w_gate1.shape[0] // CORES
        w_gate1, w_up1, w_gate2, w_up2 = (jnp.swapaxes(w, 1, 2) for w in (w_gate1, w_up1, w_gate2, w_up2))
        ix, ic, iy = (lax.axis_index(name) for name in ALL)
        where = jnp.stack([ic, ix]).astype(jnp.int32)
        first_exp = (iy * CORES + ic) * n_exp

        def gather(value):
            return lax.all_gather(value, ALL, axis=0, tiled=False)

        def reduce_own(total):
            return lax.psum_scatter(total, ('c', 'y'), scatter_dimension=0, tiled=False)

        def dense_grad(x, grad):
            part = jnp.einsum('td,te->de', x, grad, preferred_element_type=F32).astype(BF16)
            return lax.psum_scatter(part, ALL, scatter_dimension=0, tiled=True)

        routes = jnp.concatenate([route_idx1.astype(F32), route_idx2.astype(F32), route_gate1, route_gate2], axis=1).T
        routes = gather(routes)
        idx1, idx2, gate1, gate2 = jnp.split(routes, 4, axis=1)
        rank1, gates1 = route_tables(idx1, gate1, first_exp, n_exp)
        rank2, gates2 = route_tables(idx2, gate2, first_exp, n_exp)

        tok_all = gather(tokens)
        dy_all = gather(dy_out)
        u_one = mix(tok_all, dense_w1)
        y_sum = reduce_own(expert_forward(where, u_one, rank1, gates1, w_gate1, w_up1, w_down1))
        y_one = (mix(tokens, dense_w1).astype(F32) + y_sum).astype(BF16)
        u_two = mix(y_one, dense_w2)
        back, gg, gu, gd = layer_backward(True, dy_all, u_two, rank2, gates2, w_gate2, w_up2, w_down2)
        gate_two, up_two, down_two = jnp.swapaxes(gg, 1, 2), jnp.swapaxes(gu, 1, 2), gd
        gm_two = (dy_out.astype(F32) + back).astype(BF16)
        dense_two = dense_grad(y_one, gm_two)
        grad_mid = mix_back(gm_two, dense_w2)
        back, gg, gu, gd = layer_backward(False, u_one, grad_mid, rank1, gates1, w_gate1, w_up1, w_down1)
        gate_one, up_one, down_one = jnp.swapaxes(gg, 1, 2), jnp.swapaxes(gu, 1, 2), gd
        gm_one = (grad_mid.astype(F32) + back).astype(BF16)
        dense_one = dense_grad(tokens, gm_one)
        grad_tok = mix_back(gm_one, dense_w1)
        return (grad_tok, dense_one, gate_one, up_one, down_one, dense_two, gate_two, up_two, down_two)

    return jax.shard_map(local_step, mesh=fine, in_specs=(tok_spec, tok_spec) + layer_specs + layer_specs,
                         out_specs=(tok_spec,) + grad_specs + grad_specs, check_vma=False)
```

time: 598 us -> 486 us (0.81)
  waiting for transfers between devices: 211 us -> 100 us
  Pallas kernels: 242 us -> 301 us
  blocking collectives: 64.6 us -> 17.5 us
  matrix products: 32.9 us -> 23.4 us
    pallas_call x2, Pallas kernels: 186 us -> 245 us  [layer_backward(): pl.pallas_call(functools.partial(layer_kernel, gather_input), out_shape=(...]
    unnamed x12 -> x7, waiting for transfers between devices: 118 us -> 61.4 us
    all_gather x4 -> x2, waiting for transfers between devices: 93.2 us -> 38.7 us  [gather(): return lax.all_gather(value, ALL, axis=0, tiled=False)]
    all_to_all x6 -> x0, blocking collectives: 47.1 us -> none  [swap_cores(): moved = lax.all_to_all(parts, 'c', 0, 0, tiled=True)]
    dot_general x3, matrix products: 18 us -> 10.6 us  [mix(): jnp.einsum('...d,de->...e', x, weight, preferred_element_type=F32)]
    unnamed x41 -> x25, local copies, waits for them, and re-layouts: 18.2 us -> 18.7 us
  transfers between devices with their start and end apart: 8 -> 5, of which waited for: 7 -> 4; matrix products, arithmetic and copies ran while one was open for 4% -> 4% of each run, Pallas kernels for 0% -> 25%
where the time goes in v3:
time: 486 us; the launch traced here: 485 us
  Pallas kernels  301 us (62%)
  waiting for transfers between devices  100 us (21%)
  matrix products  23.4 us (5%)
  local copies, waits for them, and re-layouts  18.7 us (4%)
  blocking collectives  17.5 us (4%)
  between operations  13.9 us (3%)
  other arithmetic  9.94 us (2%)
    pallas_call x2, Pallas kernels, layer_backward(): pl.pallas_call(functools.partial(layer_kernel, gather_input), out_shape=(...  245 us
    unnamed x7, waiting for transfers between devices  61.4 us
    pallas_call x1, Pallas kernels, expert_forward(): pl.pallas_call(forward_kernel, out_shape=jax.ShapeDtypeStruct((own, n_tok...  56 us
    all_gather x2, waiting for transfers between devices, gather(): return lax.all_gather(value, ALL, axis=0, tiled=False)  38.7 us
    unnamed x25, local copies, waits for them, and re-layouts  18.7 us
    all_gather x1, blocking collectives, gather(): return lax.all_gather(value, ALL, axis=0, tiled=False)  17.5 us
    dot_general x3, matrix products, mix(): jnp.einsum('...d,de->...e', x, weight, preferred_element_type=F32)  10.6 us
  transfers between devices with their start and end apart: 5, of which 4 were waited for; matrix products, arithmetic and copies ran while one was open for 4% of the time, Pallas kernels for 25%

profile of v3, /device:TPU:0, one launch (start us, length us, event | category | flops | bytes accessed | tf_op | source)
XLA Modules:
  0.0 485.1 jit_solution(14658253853162170185)
XLA Ops:
  10.8 17.5 %all-gather.2 = f32[256,512]{1,0:T(8,128)S(1)} all-gather(f32[32,512]{1,0:T(8,128)S(1)} %maximum_bitcast_fusion), channel_id=4, replica_groups=mesh['y'=2,'x'=2,'c'=2] {'x','c','y'}, dimensions={0}, use_global_device_ids=true | all-gather | bytes 589824 | tf_op jit(solution)/shard_map/all_gather | solution.py:364
  28.3 3.6 compare_reduce_fusion
  33.0 3.6 fusion.1
  36.6 9.0 %all-gather.8.cloned.1.call-done = bf16[4096,512]{1,0:T(8,128)(2,1)} async-done(((bf16[512,512]{1,0:T(8,128)(2,1)}), bf16[4096,512]{1,0:T(8,128)(2,1)}) %all-gather.8.cloned.1.call-update) | async-done | bytes 4194320 | tf_op jit(solution)/shard_map/all_gather | solution.py:364
  45.6 7.7 %add_convert_fusion.u_ref.whole_ref = bf16[8,512,512]{2,1,0:T(8,128)(2,1)} fusion(bf16[8,512,512]{2,1,0:T(8,128)(2,1)} %bitcast.50, bf16[512,512]{1,0:T(8,128)(2,1)S(1)} %copy-done), kind=kOutput, calls=%fused_computation | convolution fusion | flops 2153775104 | bytes 8912896 | tf_op jit(solution)/shard_map/...d,de->...e/dot_general | solution.py:342
  53.4 56.0 %shard_map.205 = f32[4,512,512]{2,1,0:T(8,128)} custom-call(s32[2]{0:T(128)} %pad_add_fusion.where_ref, bf16[8,512,512]{2,1,0:T(8,128)(2,1)} %add_convert_fusion.u_ref.whole_ref, s32[8,32,512]{2,1,0:T(8,128)} %fusion.10.rank_ref, f32[8,32,512]{2,1,0:T(8,128)} %get-tuple-element.53.gate_ref, bf16[64,192,512]{2,1,0:T(8,128)(2,1)} %bitcast.46, ...), custom_call_target="tpu_custom_call" | custom-call | flops 22011707392 | bytes 41943040 | tf_op jit(solution)/shard_map/pallas_call | solution.py:280
  111.5 36.4 %reduce-scatter.12.cloned.1.call-done = f32[1,512,512]{2,1,0:T(8,128)} async-done(((f32[4,512,512]{2,1,0:T(8,128)}), f32[1,512,512]{2,1,0:T(8,128)}) %reduce-scatter.12.cloned.1.call-update) | async-done | bytes 1048592
  147.8 1.7 fusion.5
  150.7 29.7 %all-gather.6.cloned.1.call-done = bf16[4096,512]{1,0:T(8,128)(2,1)} async-done(((bf16[512,512]{1,0:T(8,128)(2,1)}), bf16[4096,512]{1,0:T(8,128)(2,1)}) %all-gather.6.cloned.1.call-update) | async-done | bytes 4194320 | tf_op jit(solution)/shard_map/all_gather | solution.py:364
  180.4 121.5 %shard_map.206 = (f32[512,512]{1,0:T(8,128)}, bf16[64,192,128]{2,1,0:T(8,128)(2,1)}, bf16[64,192,128]{2,1,0:T(8,128)(2,1)}, bf16[64,192,128]{2,1,0:T(8,128)(2,1)}) custom-call(bf16[8,512,512]{2,1,0:T(8,128)(2,1)} %bitcast.51, bf16[512,512]{1,0:T(8,128)(2,1)} %fusion.6.mine_ref, s32[8,32,512]{2,1,0:T(8,128)} %fusion.9.rank_ref, ...), custom_call_target="tpu_custom_call" | custom-call | flops 39191576576 | bytes 62914560 | tf_op jit(solution)/shard_map/pallas_call | solution.py:307
  302.0 2.6 convolution_convert_fusion
  304.6 3.4 fusion.7.mine_ref
  308.1 123.6 %shard_map.207 = (f32[512,512]{1,0:T(8,128)}, bf16[64,192,128]{2,1,0:T(8,128)(2,1)}, bf16[64,192,128]{2,1,0:T(8,128)(2,1)}, bf16[64,192,128]{2,1,0:T(8,128)(2,1)}) custom-call(bf16[8,512,512]{2,1,0:T(8,128)(2,1)} %add_convert_fusion.u_ref.whole_ref, bf16[512,512]{1,0:T(8,128)(2,1)} %fusion.7.mine_ref, s32[8,32,512]{2,1,0:T(8,128)} %fusion.10.rank_ref, ...), custom_call_target="tpu_custom_call" | custom-call | flops 39191576576 | bytes 62914560 | tf_op jit(solution)/shard_map/pallas_call | solution.py:307
  431.7 1.7 fusion.11
  434.4 2.8 fusion.8
  437.2 23.6 %reduce-scatter.10.cloned.1.call-done = bf16[64,512]{1,0:T(8,128)(2,1)} async-done(((bf16[512,512]{1,0:T(8,128)(2,1)}), bf16[64,512]{1,0:T(8,128)(2,1)}) %reduce-scatter.10.cloned.1.call-update) | async-done | bytes 65552
  460.9 3.9 copy.34
  464.8 1.7 copy.35
  466.5 1.4 copy-done.5
  467.8 1.7 copy.36
  470.9 1.7 copy.37
  472.5 1.4 copy-done.3
  473.9 1.7 copy.38
  476.9 1.7 copy.39
  (37 shorter events, 11.8 us)
Async XLA Ops:
  7.2 38.4 %copy-start = (bf16[512,512]{1,0:T(8,128)(2,1)S(1)}, bf16[512,512]{1,0:T(8,128)(2,1)}, u32[]{:S(2)}) copy-start(bf16[512,512]{1,0:T(8,128)(2,1)} %param.16) | copy-start | bytes 1572868
  7.2 38.4 %all-gather.8.cloned.1.call-start = ((), (), s32[]{:S(2)}) async-start(), calls=%async_computation.5 | async-start | bytes 4718592 | tf_op jit(solution)/shard_map/all_gather | solution.py:364
  7.9 139.9 %reduce-scatter.12.cloned.1.call-start = ((), (), s32[]{:S(2)}) async-start(), calls=%async_computation.7 | async-start | bytes 5242880
  109.4 38.5 %copy-start.1 = (bf16[512,512]{1,0:T(8,128)(2,1)S(1)}, bf16[512,512]{1,0:T(8,128)(2,1)}, u32[]{:S(2)}) copy-start(bf16[512,512]{1,0:T(8,128)(2,1)} %param.14) | copy-start | bytes 1572868
  109.4 40.1 %copy-start.8 = (bf16[512,512]{1,0:T(8,128)(2,1)S(1)}, bf16[512,512]{1,0:T(8,128)(2,1)}, u32[]{:S(2)}) copy-start(bf16[512,512]{1,0:T(8,128)(2,1)} %param.22) | copy-start | bytes 1572868
  109.4 71.0 %all-gather.6.cloned.1.call-start = ((), (), s32[]{:S(2)}) async-start(), calls=%async_computation.4 | async-start | bytes 4718592 | tf_op jit(solution)/shard_map/all_gather | solution.py:364
  110.1 327.1 %reduce-scatter.8.cloned.1.call-start = ((), (), s32[]{:S(2)}) async-start(), calls=%async_computation.3 | async-start | bytes 589824 | tf_op jit(solution)/shard_map/reduce_scatter | solution.py:371
  308.0 123.6 %copy-start.7 = (bf16[512,512]{1,0:T(8,128)(2,1)S(1)}, bf16[512,512]{1,0:T(8,128)(2,1)}, u32[]{:S(2)}) copy-start(bf16[512,512]{1,0:T(8,128)(2,1)} %fusion.7.mine_ref) | copy-start | bytes 1572868
  308.1 152.8 %reduce-scatter.10.cloned.1.call-start = ((), (), s32[]{:S(2)}) async-start(), calls=%async_computation.6 | async-start | bytes 589824
  460.9 3.9 copy-start.6
  464.8 3.0 copy-start.5
  467.8 3.0 copy-start.4
  470.9 3.0 copy-start.3
  473.9 3.0 copy-start.2
Sparse Core Ops, SparseCore 0:
  9.8 35.7 all-gather.7
  109.5 38.2 reduce-scatter.11
  149.7 30.7 all-gather.5
  308.2 27.6 reduce-scatter.7
  434.6 26.2 reduce-scatter.9

commit v4 on v3

v4 whole, which is shorter than its diff:
```python
import functools

import jax
import jax.numpy as jnp
from jax import lax
from jax.experimental import pallas as pl
from jax.experimental.pallas import tpu as pltpu
from jax.sharding import Mesh, PartitionSpec as P

F32 = jnp.float32
BF16 = jnp.bfloat16
CAP = 64
GROUP = 4
CORES = 2
CHIPS = 2
ALL = ('x', 'c', 'y')
MESH = pl.DeviceIdType.MESH
FLIPS = ((0, 0), (0, 0), (0, 1), (0, 0), (0, 1), (1, 0), (1, 1))
ROUTE = 'yxxcccc'


def matmul(lhs, rhs, lhs_dim=1, rhs_dim=0):
    return lax.dot_general(lhs, rhs, (((lhs_dim,), (rhs_dim,)), ((), ())), preferred_element_type=F32)


def position():
    return tuple(lax.axis_index(name) for name in ALL)


def send(src, dst, sems, at, axis):
    return pltpu.make_async_remote_copy(src, dst, sems[0].at[at], sems[1].at[at],
                                        device_id={axis: 1 - lax.axis_index(axis)}, device_id_type=MESH)


def spreader(mine_ref, peer_ref, sems):
    ix, ic, iy = position()

    def copy(at):
        flip_x, flip_y = FLIPS[at]
        x = 1 - ix if flip_x else ix
        y = 1 - iy if flip_y else iy
        block = peer_ref.at[(x * CORES + ic) * 2 + y]
        return send(block if flip_x or flip_y else mine_ref, block, sems, at, ROUTE[at])

    return copy


def adder(p_ref, rs_ref, sems):
    ix, ic, iy = position()

    def copy(at):
        part = ((1 - ic) * 2 + 1 - iy, (1 - ic) * 2 + iy, ic * 2 + 1 - iy)[at]
        return send(p_ref.at[part], rs_ref.at[at], sems, at, 'ccy'[at])

    return copy


def greet(everyone):
    barrier = pltpu.get_barrier_semaphore()
    if everyone:
        others = [target(hop) for hop in range(1, 8)]
    else:
        others = [{axis: 1 - lax.axis_index(axis)} for axis in ALL]
    for other in others:
        pl.semaphore_signal(barrier, inc=1, device_id=other, device_id_type=MESH)
    pl.semaphore_wait(barrier, len(others))


def rank_of(x, c, y):
    return (x * CORES + c) * 2 + y


def target(hop):
    goal = lax.rem(rank_of(*position()) + hop, 8)
    return {'x': lax.div(goal, 4), 'c': lax.rem(lax.div(goal, 2), 2), 'y': lax.rem(goal, 2)}


def at_step(number):
    return pl.when(pl.program_id(0) == number)


def gate_hidden(x_rows, w_gate, w_up):
    a_pre = matmul(x_rows, w_gate, 1, 1)
    b_pre = matmul(x_rows, w_up, 1, 1)
    return a_pre, b_pre, jax.nn.sigmoid(a_pre)


def select_rows(rank_ref, gate_ref, group, src):
    n_tok = rank_ref.shape[-1]
    slot = lax.broadcasted_iota(jnp.int32, (CAP, n_tok), 0)
    picks, gates = [], []
    for exp in range(GROUP):
        row = pl.ds(group * GROUP + exp, 1)
        hit = slot == rank_ref[src, row, :]
        picks.append(jnp.where(hit, 1.0, 0.0).astype(BF16))
        gates.append(jnp.sum(jnp.where(hit, gate_ref[src, row, :], 0.0), axis=1, keepdims=True))
    return jnp.concatenate(picks, axis=0), jnp.concatenate(gates, axis=0)


def route_table(route_ref, before_ref, src, layer, rank_ref, gate_ref, n_exp):
    _, ic, iy = position()
    n_tok = route_ref.shape[-1]
    experts = ((iy * CORES + ic) * n_exp + lax.broadcasted_iota(jnp.int32, (n_exp, n_tok), 0)).astype(F32)
    member = jnp.zeros((n_exp, n_tok), F32)
    gates = jnp.zeros((n_exp, n_tok), F32)
    for top in range(8):
        hit = experts == route_ref[src, layer * 8 + top:layer * 8 + top + 1, :]
        member = jnp.where(hit, 1.0, member)
        gates = jnp.where(hit, route_ref[src, 16 + layer * 8 + top:17 + layer * 8 + top, :], gates)
    count = matmul(member.astype(BF16), before_ref[...])
    rank_ref[src] = jnp.where(member > 0.0, count, -1.0).astype(jnp.int32)
    gate_ref[src] = gates


def forward_kernel(mine_ref, grad_ref, routes_ref, dense_ref, wg_ref, wu_ref, wd_ref,
                   y_ref, u_ref, uall_ref, dall_ref, rank1_ref, gate1_ref, rank2_ref, gate2_ref,
                   us_ref, ds_ref, route_ref, before_ref, pick_ref, row_ref, x_ref, part_ref, p_ref, rs_ref,
                   u_send, u_recv, d_send, d_recv, t_send, t_recv, rs_send, rs_recv, out_sem):
    n_exp, n_tok = rank1_ref.shape[1:]
    n_group = n_exp // GROUP
    step = pl.program_id(0)
    ix, ic, iy = position()
    me = rank_of(ix, ic, iy)
    spread_u = spreader(mine_ref, us_ref, (u_send, u_recv))
    spread_d = spreader(grad_ref, ds_ref, (d_send, d_recv))
    spread_t = spreader(routes_ref, route_ref, (t_send, t_recv))
    add_up = adder(p_ref, rs_ref, (rs_send, rs_recv))
    stores = ((us_ref, uall_ref), (ds_ref, dall_ref))

    def pass_on(copy, arrived, onward):
        copy(arrived).wait_recv()
        for at in onward:
            copy(at).start()

    @at_step(0)
    def _():
        greet(False)
        for copy in (spread_t, spread_u):
            for at in (0, 3, 1):
                copy(at).start()
        us_ref[me] = mine_ref[...]
        ds_ref[me] = grad_ref[...]
        route_ref[me] = routes_ref[...]
        p_ref[...] = jnp.zeros_like(p_ref)
        before_ref[...] = jnp.where(lax.broadcasted_iota(jnp.int32, (n_tok, n_tok), 0)
                                    < lax.broadcasted_iota(jnp.int32, (n_tok, n_tok), 1), 1.0, 0.0).astype(BF16)
        pass_on(spread_t, 0, (4, 2))
        spread_t(3).wait_recv()
        spread_t(4).wait_recv()

        @pl.loop(0, 4)
        def _(src):
            route_table(route_ref, before_ref, ix * 4 + src, 0, rank1_ref, gate1_ref, n_exp)

        pass_on(spread_u, 0, (4, 2))
        for at in (0, 3, 1):
            spread_d(at).start()
        spread_u(3).wait_recv()
        spread_u(4).wait_recv()

    @at_step(n_group // 4)
    def _():
        pass_on(spread_t, 1, (5,))
        pass_on(spread_u, 1, (5,))

    @at_step(n_group // 2)
    def _():
        pass_on(spread_t, 2, (6,))
        pass_on(spread_u, 2, (6,))
        pass_on(spread_d, 0, (4, 2))

    @at_step(n_group - 1)
    def _():
        spread_t(5).wait_recv()
        spread_t(6).wait_recv()

        @pl.loop(0, 4)
        def _(src):
            route_table(route_ref, before_ref, (1 - ix) * 4 + src, 0, rank1_ref, gate1_ref, n_exp)

        @pl.loop(0, 8)
        def _(src):
            route_table(route_ref, before_ref, src, 1, rank2_ref, gate2_ref, n_exp)

    @at_step(n_group)
    def _():
        add_up(0).start()

    @at_step(n_group + 1)
    def _():
        add_up(2).start()

    @at_step(n_group + n_group // 2)
    def _():
        pass_on(spread_d, 1, (5,))

    @at_step(2 * n_group - 1)
    def _():
        pass_on(spread_d, 2, (6,))
        spread_u(5).wait_recv()
        spread_u(6).wait_recv()
        pltpu.make_async_copy(us_ref, uall_ref, out_sem.at[0]).start()

    group = lax.rem(step, n_group)
    far = 1 - lax.div(step, n_group)
    y_now = jnp.where(far == 1, 1 - iy, iy)

    @pl.loop(0, CORES)
    def _(core):
        src = rank_of(ix, core, y_now)
        pick, gate = select_rows(rank1_ref, gate1_ref, group, src)
        pick_ref[core] = pick
        rows = matmul(pick, us_ref[src]).astype(BF16)
        at = pl.ds(pl.multiple_of(core * CAP, CAP), CAP)
        for exp in range(GROUP):
            x_ref[exp, at, :] = rows[exp * CAP:(exp + 1) * CAP]
            row_ref[exp, at, :] = jnp.broadcast_to(gate[exp * CAP:(exp + 1) * CAP], (CAP, 128))

    @pl.loop(0, GROUP)
    def _(exp):
        a_pre, b_pre, sigma = gate_hidden(x_ref[exp], wg_ref[exp], wu_ref[exp])
        hidden = (a_pre * sigma * b_pre).astype(BF16)
        out = matmul(hidden, wd_ref[exp]).astype(BF16).astype(F32) * row_ref[exp][:, :1]
        high = out.astype(BF16)
        rest = out - high.astype(F32)
        mid = rest.astype(BF16)
        low = (rest - mid.astype(F32)).astype(BF16)
        at = pl.ds(pl.multiple_of(exp * CAP, CAP), CAP)
        for core in range(CORES):
            here = slice(core * CAP, (core + 1) * CAP)
            part_ref[core, 0, at, :] = high[here]
            part_ref[core, 1, at, :] = mid[here]
            part_ref[core, 2, at, :] = low[here]

    @pl.loop(0, CORES)
    def _(core):
        pick = pick_ref[core]
        total = matmul(pick, part_ref[core, 0], 0, 0)
        total += matmul(pick, part_ref[core, 1], 0, 0) + matmul(pick, part_ref[core, 2], 0, 0)
        p_ref[core * 2 + y_now] += total

    @at_step(n_group)
    def _():
        add_up(0).wait_recv()
        p_ref[ic * 2 + 1 - iy] += rs_ref[0]

    @at_step(2 * n_group - 1)
    def _():
        for at in (3, 4, 5, 6):
            spread_d(at).wait_recv()
        pltpu.make_async_copy(ds_ref, dall_ref, out_sem.at[1]).start()
        add_up(1).start()
        add_up(1).wait_recv()
        add_up(2).wait_recv()
        y_own = (mine_ref[...].astype(F32) + (p_ref[ic * 2 + iy] + rs_ref[1] + rs_ref[2])).astype(BF16)
        y_ref[...] = y_own
        u_ref[...] = (y_own.astype(F32) + matmul(y_own, dense_ref[...])).astype(BF16)
        for copy in (spread_u, spread_d, spread_t):
            for at in range(7):
                copy(at).wait_send()
        for at in range(3):
            add_up(at).wait_send()
        for at in range(2):
            pltpu.make_async_copy(*stores[at], out_sem.at[at]).wait()


def layer_kernel(last_layer, *refs):
    refs = list(refs)
    whole_ref, mine_ref, rank_ref, gate_ref, x_own_ref, grad_own_ref, dense_ref, wg_ref, wu_ref, wd_ref = refs[:10]
    del refs[:10]
    if last_layer:
        other_ref = refs.pop(0)
        one_ref, two_ref = refs[1:3]
        del refs[1:3]
    else:
        part_ref = refs.pop(1)
    gx_out_ref, gg_ref, gu_ref, gd_ref = refs[:4]
    (peer_ref, xo_ref, do_ref, h_ref, ga_ref, gb_ref, pick_ref, gx_ref, p_ref, rs_ref, x_ref, d_ref, stage_ref,
     ag_send, ag_recv, rs_send, rs_recv, keep_sem, give_send, give_recv) = refs[4:24]
    if last_layer:
        part_ref, land_ref, land_send, land_recv = refs[24:]
    n_src, _, dim = whole_ref.shape
    own = n_src // CHIPS
    n_group = xo_ref.shape[0] // GROUP
    n_first = 2 * n_group
    n_step = 3 * n_group
    half = dim // CHIPS
    piece = half // CORES
    step = pl.program_id(0)
    ix, ic, iy = position()
    cols = pl.ds(pl.multiple_of(ix * half, half), half)
    u_ref, dy_ref = (whole_ref, peer_ref) if last_layer else (peer_ref, whole_ref)
    outs = (gg_ref, gu_ref, gd_ref)
    spread = spreader(mine_ref, peer_ref, (ag_send, ag_recv))
    add_up = adder(p_ref, rs_ref, (rs_send, rs_recv))

    def land_copy(layer, hop):
        goal = target(hop)
        rows = dim // 8
        src = (part_ref, other_ref)[layer]
        at = pl.ds(pl.multiple_of(rank_of(goal['x'], goal['c'], goal['y']) * rows, rows), rows)
        return pltpu.make_async_remote_copy(src.at[at, :], land_ref.at[layer, hop], land_send.at[layer, hop],
                                            land_recv.at[layer, hop], device_id=goal, device_id_type=MESH)

    def land_sum(layer, out_ref):
        rows = dim // 8
        at = pl.ds(pl.multiple_of(rank_of(ix, ic, iy) * rows, rows), rows)
        total = (part_ref, other_ref)[layer][at, :].astype(F32)
        for hop in range(1, 8):
            land_copy(layer, hop).wait_recv()
            total += land_ref[layer, hop].astype(F32)
        out_ref[...] = total.astype(BF16)

    def store_copies(group, moved):
        buf = lax.rem(group, 2)
        rows = pl.ds(ic * n_group * GROUP + group * GROUP, GROUP)
        for kind in range(3):
            dst = outs[kind].at[rows]
            if moved:
                yield pltpu.make_async_remote_copy(
                    stage_ref.at[buf, 1 - ic, kind], dst, give_send.at[buf, kind], give_recv.at[group, kind],
                    device_id={'c': 1 - ic}, device_id_type=MESH)
            else:
                yield pltpu.make_async_copy(stage_ref.at[buf, ic, kind], dst, keep_sem.at[buf, kind])

    def store_start(group):
        for moved in (True, False):
            for copy in store_copies(group, moved):
                copy.start()

    def store_wait(group):
        for copy in store_copies(group, True):
            copy.wait_send()
        for copy in store_copies(group, False):
            copy.wait()

    def pull(src, group, x_dst, d_dst, base, at, keep):
        pick, gate = select_rows(rank_ref, gate_ref, group, src)
        if keep is not None:
            pick_ref[keep] = pick
        x_rows = matmul(pick, u_ref[src]).astype(BF16)
        d_rows = (matmul(pick, dy_ref[src]) * gate).astype(BF16)
        rows = pl.ds(pl.multiple_of(at * CAP, CAP), CAP)
        for exp in range(GROUP):
            x_dst[base + exp, rows, :] = x_rows[exp * CAP:(exp + 1) * CAP]
            d_dst[base + exp, rows, :] = d_rows[exp * CAP:(exp + 1) * CAP]

    def hidden_grads(x_rows, d_rows, exp):
        a_pre, b_pre, sigma = gate_hidden(x_rows, wg_ref[exp], wu_ref[exp])
        silu = a_pre * sigma
        grad_hidden = matmul(d_rows, wd_ref[exp], 1, 1).astype(BF16).astype(F32)
        grad_a = (grad_hidden * b_pre * sigma * (1.0 + a_pre * (1.0 - sigma))).astype(BF16)
        return (silu * b_pre).astype(BF16), grad_a, (grad_hidden * silu).astype(BF16)

    @at_step(0)
    def _():
        greet(last_layer)
        for at in (0, 3, 1):
            spread(at).start()
        if last_layer:
            for hop in range(1, 8):
                land_copy(1, hop).start()
        peer_ref[rank_of(ix, ic, iy)] = mine_ref[...]
        p_ref[...] = jnp.zeros_like(p_ref)
        spread(3).wait_recv()

    @at_step(n_group // 2)
    def _():
        spread(0).wait_recv()
        spread(4).start()
        spread(2).start()

    @at_step(n_group)
    def _():
        spread(4).wait_recv()

    @at_step(n_group + n_group // 2)
    def _():
        spread(1).wait_recv()
        spread(5).start()

    @at_step(n_first - 1)
    def _():
        spread(2).wait_recv()
        spread(6).start()

    @pl.when(step < n_first)
    def _():
        group = lax.rem(step, n_group)
        late = lax.div(step, n_group)
        y_now = jnp.where(late == 1, 1 - iy, iy)
        base = group * GROUP
        rows = pl.ds(pl.multiple_of(late * CORES * CAP, CORES * CAP), CORES * CAP)

        @pl.loop(0, CORES)
        def _(core):
            pull(rank_of(ix, core, y_now), group, xo_ref, do_ref, base, late * CORES + core, core)

        @pl.loop(0, GROUP)
        def _(exp):
            hidden, grad_a, grad_b = hidden_grads(xo_ref[base + exp, rows, :], do_ref[base + exp, rows, :], exp)
            h_ref[base + exp, rows, :] = hidden
            ga_ref[base + exp, rows, :] = grad_a
            gb_ref[base + exp, rows, :] = grad_b
            grad_x = (matmul(grad_a, wg_ref[exp]) + matmul(grad_b, wu_ref[exp])).astype(BF16)
            at = pl.ds(pl.multiple_of(exp * CAP, CAP), CAP)
            for core in range(CORES):
                gx_ref[core, at, :] = grad_x[core * CAP:(core + 1) * CAP]

        @pl.loop(0, CORES)
        def _(core):
            p_ref[core * 2 + y_now] += matmul(pick_ref[core], gx_ref[core], 0, 0)

    @at_step(n_first)
    def _():
        add_up(0).start()
        add_up(1).start()
        spread(5).wait_recv()
        spread(6).wait_recv()

    @at_step(n_first + 1)
    def _():
        add_up(2).start()

    @at_step(n_step - 1)
    def _():
        add_up(1).wait_recv()
        add_up(2).wait_recv()
        total = p_ref[ic * 2 + iy] + rs_ref[1] + rs_ref[2]
        grad = (grad_own_ref[...].astype(F32) + total).astype(BF16)
        part_ref[...] = matmul(x_own_ref[...], grad, 0, 0).astype(BF16)
        gx_out_ref[...] = (grad.astype(F32) + matmul(grad, dense_ref[...], 1, 1)).astype(BF16)
        if last_layer:
            for hop in range(1, 8):
                land_copy(0, hop).start()

    @pl.when(step >= n_first)
    def _():
        group = step - n_first

        @pl.when(group >= 1)
        def _():
            store_start(group - 1)

        @pl.loop(0, own)
        def _(src):
            pull((1 - ix) * own + src, group, x_ref, d_ref, 0, src, None)

        @pl.when(group >= 2)
        def _():
            store_wait(group - 2)

        buf = lax.rem(group, 2)

        @pl.loop(0, GROUP)
        def _(exp):
            base = group * GROUP + exp
            hidden, grad_a, grad_b = hidden_grads(x_ref[exp], d_ref[exp], exp)
            x_own, x_far = xo_ref[base, :, cols], x_ref[exp, :, cols]
            d_own, d_far = do_ref[base, :, cols], d_ref[exp, :, cols]
            grads = (matmul(ga_ref[base], x_own, 0, 0) + matmul(grad_a, x_far, 0, 0),
                     matmul(gb_ref[base], x_own, 0, 0) + matmul(grad_b, x_far, 0, 0),
                     matmul(h_ref[base], d_own, 0, 0) + matmul(hidden, d_far, 0, 0))
            for kind in range(3):
                for core in range(CORES):
                    stage_ref[buf, core, kind, exp] = grads[kind][:, core * piece:(core + 1) * piece].astype(BF16)

    @at_step(n_first)
    def _():
        add_up(0).wait_recv()
        p_ref[ic * 2 + 1 - iy] += rs_ref[0]

    @at_step(n_step - 1)
    def _():
        last = n_group - 1
        store_wait(last - 1)
        store_start(last)
        if last_layer:
            land_sum(1, two_ref)
            land_sum(0, one_ref)
            for layer in range(2):
                for hop in range(1, 8):
                    land_copy(layer, hop).wait_send()
        for at in range(7):
            spread(at).wait_send()
        for at in range(3):
            add_up(at).wait_send()
        store_wait(last)
        for group in range(n_group):
            for copy in store_copies(group, True):
                copy.wait_recv()


def fixed(*shape):
    return pl.BlockSpec(shape, lambda s: (0,) * len(shape), pipeline_mode=pl.Buffered(1))


def weight_spec(groups, ff, dim):
    return pl.BlockSpec((GROUP, ff, dim), lambda s: (lax.axis_index('c') * groups + lax.rem(s, groups), 0, 0))


def dma_sems(*shape):
    return pltpu.SemaphoreType.DMA(shape)


def sums_scratch(own, n_tok, dim):
    return [pltpu.VMEM((own, n_tok, dim), F32), pltpu.VMEM((3, n_tok, dim), F32)]


def layer_forward(mine, grad, routes, dense, w_gate, w_up, w_down):
    n_tok, dim = mine.shape
    n_all, ff, _ = w_gate.shape
    n_exp = n_all // CORES
    n_src = 8
    own = n_src // CHIPS
    groups = n_exp // GROUP
    tall = weight_spec(groups, ff, dim)
    table = fixed(n_src, n_exp, n_tok)
    block = jax.ShapeDtypeStruct((n_tok, dim), BF16)
    every = jax.ShapeDtypeStruct((n_src, n_tok, dim), BF16)
    ranks = jax.ShapeDtypeStruct((n_src, n_exp, n_tok), jnp.int32)
    gates = jax.ShapeDtypeStruct((n_src, n_exp, n_tok), F32)
    anywhere = pl.BlockSpec(memory_space=pl.ANY)
    rows = CORES * CAP
    return pl.pallas_call(
        forward_kernel,
        out_shape=(block, block, every, every, ranks, gates, ranks, gates),
        grid_spec=pltpu.PrefetchScalarGridSpec(
            num_scalar_prefetch=0, grid=(2 * groups,),
            in_specs=[fixed(n_tok, dim), fixed(n_tok, dim), fixed(*routes.shape), fixed(dim, dim), tall, tall, tall],
            out_specs=(fixed(n_tok, dim), fixed(n_tok, dim), anywhere, anywhere, table, table, table, table),
            scratch_shapes=[pltpu.VMEM((n_src, n_tok, dim), BF16), pltpu.VMEM((n_src, n_tok, dim), BF16),
                            pltpu.VMEM((n_src,) + routes.shape, F32), pltpu.VMEM((n_tok, n_tok), BF16),
                            pltpu.VMEM((CORES, GROUP * CAP, n_tok), BF16), pltpu.VMEM((GROUP, rows, 128), F32),
                            pltpu.VMEM((GROUP, rows, dim), BF16), pltpu.VMEM((CORES, 3, GROUP * CAP, dim), BF16)]
            + sums_scratch(own, n_tok, dim)
            + [dma_sems(7)] * 6 + [dma_sems(3)] * 2 + [dma_sems(2)]),
        compiler_params=pltpu.CompilerParams(dimension_semantics=('arbitrary',), vmem_limit_bytes=62 << 20,
                                             collective_id=0, has_side_effects=True),
    )(mine, grad, routes, dense, w_gate, w_up, w_down)


def layer_backward(whole, mine, rank, gate, x_own, grad_own, dense, w_gate, w_up, w_down, other=None):
    n_src, n_tok, dim = whole.shape
    n_all, ff, _ = w_gate.shape
    n_exp = rank.shape[1]
    own = n_src // CHIPS
    piece = dim // (CHIPS * CORES)
    groups = n_exp // GROUP
    kept = own * CAP
    last_layer = other is not None
    tall = weight_spec(groups, ff, dim)
    table = fixed(n_src, n_exp, n_tok)
    block = fixed(n_tok, dim)
    square = fixed(dim, dim)
    slab = fixed(dim // 8, dim)
    grad_shape = jax.ShapeDtypeStruct((n_all, ff, piece), BF16)
    part_shape = jax.ShapeDtypeStruct((dim, dim), BF16)
    slab_shape = jax.ShapeDtypeStruct((dim // 8, dim), BF16)
    extra_shapes = (slab_shape, slab_shape) if last_layer else (part_shape,)
    extra_specs = (slab, slab) if last_layer else (square,)
    scratch = [pltpu.VMEM((n_src, n_tok, dim), BF16), pltpu.VMEM((n_exp, kept, dim), BF16),
               pltpu.VMEM((n_exp, kept, dim), BF16), pltpu.VMEM((n_exp, kept, ff), BF16),
               pltpu.VMEM((n_exp, kept, ff), BF16), pltpu.VMEM((n_exp, kept, ff), BF16),
               pltpu.VMEM((CORES, GROUP * CAP, n_tok), BF16), pltpu.VMEM((CORES, GROUP * CAP, dim), BF16)]
    scratch += sums_scratch(own, n_tok, dim)
    scratch += [pltpu.VMEM((GROUP, kept, dim), BF16), pltpu.VMEM((GROUP, kept, dim), BF16),
                pltpu.VMEM((2, CORES, 3, GROUP, ff, piece), BF16),
                dma_sems(7), dma_sems(7), dma_sems(3), dma_sems(3), dma_sems(2, 3), dma_sems(2, 3), dma_sems(groups, 3)]
    if last_layer:
        scratch += [pltpu.VMEM((dim, dim), BF16), pltpu.VMEM((2, 8, dim // 8, dim), BF16), dma_sems(2, 8), dma_sems(2, 8)]
    operands = (whole, mine, rank, gate, x_own, grad_own, dense, w_gate, w_up, w_down) + ((other,) if last_layer else ())
    return pl.pallas_call(
        functools.partial(layer_kernel, last_layer),
        out_shape=(jax.ShapeDtypeStruct((n_tok, dim), BF16),) + extra_shapes + (grad_shape,) * 3,
        grid_spec=pltpu.PrefetchScalarGridSpec(
            num_scalar_prefetch=0, grid=(3 * groups,),
            in_specs=[fixed(n_src, n_tok, dim), block, table, table, block, block, square, tall, tall, tall]
            + ([square] if last_layer else []),
            out_specs=(block,) + extra_specs + (pl.BlockSpec(memory_space=pl.ANY),) * 3,
            scratch_shapes=scratch),
        compiler_params=pltpu.CompilerParams(dimension_semantics=('arbitrary',), vmem_limit_bytes=67043328,
                                             collective_id=1 + int(last_layer), has_side_effects=True),
    )(*operands)


def mix(x, weight):
    return (x.astype(F32) + jnp.dot(x, weight, preferred_element_type=F32)).astype(BF16)


def solution(mesh):
    fine = Mesh(mesh.devices.reshape(2, CHIPS, CORES), ('y', 'x', 'c'))
    tok_spec = P(ALL, None)
    exp_spec = P('y', None, None)
    layer_specs = (P(None, None), tok_spec, tok_spec, exp_spec, exp_spec, exp_spec)
    grad_specs = (P(ALL, None), P('y', ('x', 'c'), None), P('y', ('x', 'c'), None), P('y', None, ('x', 'c')))

    def local_step(tokens, dy_out, dense_w1, route_idx1, route_gate1, w_gate1, w_up1, w_down1, dense_w2, route_idx2, route_gate2, w_gate2, w_up2, w_down2):
        w_gate1, w_up1, w_gate2, w_up2 = (jnp.swapaxes(w, 1, 2) for w in (w_gate1, w_up1, w_gate2, w_up2))
        routes = jnp.concatenate([route_idx1.astype(F32).T, route_idx2.astype(F32).T, route_gate1.T, route_gate2.T], axis=0)
        u_one = mix(tokens, dense_w1)
        y_one, u_two, u_all, dy_all, rank1, gate1, rank2, gate2 = layer_forward(
            u_one, dy_out, routes, dense_w2, w_gate1, w_up1, w_down1)
        grad_mid, part_two, gg, gu, gd = layer_backward(
            dy_all, u_two, rank2, gate2, y_one, dy_out, dense_w2, w_gate2, w_up2, w_down2)
        gate_two, up_two, down_two = jnp.swapaxes(gg, 1, 2), jnp.swapaxes(gu, 1, 2), gd
        grad_tok, dense_one, dense_two, gg, gu, gd = layer_backward(
            u_all, grad_mid, rank1, gate1, tokens, grad_mid, dense_w1, w_gate1, w_up1, w_down1, part_two)
        gate_one, up_one, down_one = jnp.swapaxes(gg, 1, 2), jnp.swapaxes(gu, 1, 2), gd
        return (grad_tok, dense_one, gate_one, up_one, down_one, dense_two, gate_two, up_two, down_two)

    return jax.shard_map(local_step, mesh=fine, in_specs=(tok_spec, tok_spec) + layer_specs + layer_specs,
                         out_specs=(tok_spec,) + grad_specs + grad_specs, check_vma=False)
```

time: 486 us -> 369 us (0.76)
  waiting for transfers between devices: 100 us -> 0 us
  Pallas kernels: 301 us -> 342 us
  matrix products: 23.4 us -> 2.59 us
  blocking collectives: 17.5 us -> 0 us
  between operations: 13.9 us -> 0.68 us
  other arithmetic: 9.94 us -> 2.11 us
    unnamed x7 -> x0, waiting for transfers between devices: 61.4 us -> none
    pallas_call x3, Pallas kernels: 301 us -> 342 us  [the longest x2 249 us: layer_backward(): pl.pallas_call(functools.partial(layer_kernel, last_layer), out_shape=(ja...]
    all_gather x2 -> x0, waiting for transfers between devices: 38.7 us -> none  [gather(): return lax.all_gather(value, ALL, axis=0, tiled=False)]
    dot_general x9 -> x1, matrix products: 23.4 us -> 2.59 us  [mix(): jnp.dot(x, weight, preferred_element_type=F32)]
    all_gather x1 -> x0, blocking collectives: 17.5 us -> none  [gather(): return lax.all_gather(value, ALL, axis=0, tiled=False)]
    unnamed x25 -> x21, local copies, waits for them, and re-layouts: 18.7 us -> 21.1 us
  transfers between devices with their start and end apart: 5 -> 0, of which waited for: 4 -> 0; matrix products, arithmetic and copies ran while one was open for 4% -> 0% of each run, Pallas kernels for 25% -> 0%
where the time goes in v4:
time: 369 us; the launch traced here: 368 us
  Pallas kernels  342 us (93%)
  local copies, waits for them, and re-layouts  21.1 us (6%)
    pallas_call x2, Pallas kernels, layer_backward(): pl.pallas_call(functools.partial(layer_kernel, last_layer), out_shape=(ja...  249 us
    pallas_call x1, Pallas kernels, layer_forward(): pl.pallas_call(forward_kernel, out_shape=(block, block, every, every, ran...  92.6 us
    unnamed x21, local copies, waits for them, and re-layouts  21.1 us

profile of v4, /device:TPU:0, one launch (start us, length us, event | category | flops | bytes accessed | tf_op | source)
XLA Modules:
  0.0 368.3 jit_solution(8224947244241810762)
XLA Ops:
  0.6 0.7 convert_bitcast_fusion
  1.4 1.4 pad_maximum_fusion.routes_ref
  2.8 2.6 fusion.mine_ref
  5.3 92.6 %shard_map.205 = (bf16[512,512]{1,0:T(8,128)(2,1)}, bf16[512,512]{1,0:T(8,128)(2,1)}, bf16[8,512,512]{2,1,0:T(8,128)(2,1)}, bf16[8,512,512]{2,1,0:T(8,128)(2,1)}...) custom-call(bf16[512,512]{1,0:T(8,128)(2,1)} %fusion.mine_ref, ...), custom_call_target="tpu_custom_call" | custom-call | tf_op jit(solution)/shard_map/pallas_call | solution.py:525
  97.9 124.4 %shard_map.206 = (bf16[512,512]{1,0:T(8,128)(2,1)}, bf16[512,512]{1,0:T(8,128)(2,1)}, bf16[64,192,128]{2,1,0:T(8,128)(2,1)}, bf16[64,192,128]{2,1,0:T(8,128)(2,1)}, bf16[64,192,128]{2,1,0:T(8,128)(2,1)}) custom-call(bf16[8,512,512]{2,1,0:T(8,128)(2,1)} %get-tuple-element.29.refs_0_, bf16[512,512]{1,0:T(8,128)(2,1)} %get-tuple-element.30.refs_1_, ...), custom_call_target="tpu_custom_call" | custom-call | tf_op jit(solution)/shard_map/pallas_call | solution.py:573
  222.3 124.8 %shard_map.207 = (bf16[512,512]{1,0:T(8,128)(2,1)}, bf16[64,512]{1,0:T(8,128)(2,1)}, bf16[64,512]{1,0:T(8,128)(2,1)}, bf16[64,192,128]{2,1,0:T(8,128)(2,1)}, bf1...) custom-call(bf16[8,512,512]{2,1,0:T(8,128)(2,1)} %get-tuple-element.28.refs_0_, ...), custom_call_target="tpu_custom_call" | custom-call | tf_op jit(solution)/shard_map/pallas_call | solution.py:573
  347.2 1.9 copy.32
  349.1 1.5 copy.33
  350.5 0.0 copy-start.4
  350.5 3.9 %copy.34 = bf16[64,128,192]{1,2,0:T(8,128)(2,1)} copy(bf16[64,128,192]{1,2,0:T(8,128)(2,1)} %bitcast.25) | data formatting | bytes 6291456
  354.4 0.0 copy-done.4
  354.4 0.0 copy-start.3
  354.4 1.7 copy.35
  356.1 1.4 copy-done.3
  357.5 0.0 copy-start.5
  357.5 1.7 copy.36
  359.1 0.0 copy-done.5
  359.1 0.6 copy.37
  359.8 0.8 copy-done.2
  360.6 1.7 copy.38
  362.2 1.4 copy-done.1
  363.6 1.7 copy.39
  365.3 1.4 copy-done
  366.6 1.7 copy.40
  (3 shorter events, 0.0 us)
Async XLA Ops:
  350.5 3.9 %copy-start.4 = (bf16[64,192,128]{2,1,0:T(8,128)(2,1)S(1)}, bf16[64,192,128]{2,1,0:T(8,128)(2,1)}, u32[]{:S(2)}) copy-start(bf16[64,192,128]{2,1,0:T(8,128)(2,1)} %get-tuple-element.41) | copy-start | bytes 9437188
  354.4 3.0 copy-start.3
  357.5 1.7 copy-start.5
  357.5 3.1 copy-start.2
  360.6 3.0 copy-start.1
  363.6 3.0 copy-start

commit v5 on v4

--- a/solution.py
+++ b/solution.py
@@ -205,19 +205,17 @@
     far = 1 - lax.div(step, n_group)
     y_now = jnp.where(far == 1, 1 - iy, iy)
 
-    @pl.loop(0, CORES)
-    def _(core):
+    for core in range(CORES):
         src = rank_of(ix, core, y_now)
         pick, gate = select_rows(rank1_ref, gate1_ref, group, src)
         pick_ref[core] = pick
         rows = matmul(pick, us_ref[src]).astype(BF16)
-        at = pl.ds(pl.multiple_of(core * CAP, CAP), CAP)
+        at = slice(core * CAP, (core + 1) * CAP)
         for exp in range(GROUP):
             x_ref[exp, at, :] = rows[exp * CAP:(exp + 1) * CAP]
             row_ref[exp, at, :] = jnp.broadcast_to(gate[exp * CAP:(exp + 1) * CAP], (CAP, 128))
 
-    @pl.loop(0, GROUP)
-    def _(exp):
+    for exp in range(GROUP):
         a_pre, b_pre, sigma = gate_hidden(x_ref[exp], wg_ref[exp], wu_ref[exp])
         hidden = (a_pre * sigma * b_pre).astype(BF16)
         out = matmul(hidden, wd_ref[exp]).astype(BF16).astype(F32) * row_ref[exp][:, :1]
@@ -225,15 +223,14 @@
         rest = out - high.astype(F32)
         mid = rest.astype(BF16)
         low = (rest - mid.astype(F32)).astype(BF16)
-        at = pl.ds(pl.multiple_of(exp * CAP, CAP), CAP)
+        at = slice(exp * CAP, (exp + 1) * CAP)
         for core in range(CORES):
             here = slice(core * CAP, (core + 1) * CAP)
             part_ref[core, 0, at, :] = high[here]
             part_ref[core, 1, at, :] = mid[here]
             part_ref[core, 2, at, :] = low[here]
 
-    @pl.loop(0, CORES)
-    def _(core):
+    for core in range(CORES):
         pick = pick_ref[core]
         total = matmul(pick, part_ref[core, 0], 0, 0)
         total += matmul(pick, part_ref[core, 1], 0, 0) + matmul(pick, part_ref[core, 2], 0, 0)
@@ -392,23 +389,20 @@
         base = group * GROUP
         rows = pl.ds(pl.multiple_of(late * CORES * CAP, CORES * CAP), CORES * CAP)
 
-        @pl.loop(0, CORES)
-        def _(core):
+        for core in range(CORES):
             pull(rank_of(ix, core, y_now), group, xo_ref, do_ref, base, late * CORES + core, core)
 
-        @pl.loop(0, GROUP)
-        def _(exp):
+        for exp in range(GROUP):
             hidden, grad_a, grad_b = hidden_grads(xo_ref[base + exp, rows, :], do_ref[base + exp, rows, :], exp)
             h_ref[base + exp, rows, :] = hidden
             ga_ref[base + exp, rows, :] = grad_a
             gb_ref[base + exp, rows, :] = grad_b
             grad_x = (matmul(grad_a, wg_ref[exp]) + matmul(grad_b, wu_ref[exp])).astype(BF16)
-            at = pl.ds(pl.multiple_of(exp * CAP, CAP), CAP)
+            at = slice(exp * CAP, (exp + 1) * CAP)
             for core in range(CORES):
                 gx_ref[core, at, :] = grad_x[core * CAP:(core + 1) * CAP]
 
-        @pl.loop(0, CORES)
-        def _(core):
+        for core in range(CORES):
             p_ref[core * 2 + y_now] += matmul(pick_ref[core], gx_ref[core], 0, 0)
 
     @at_step(n_first)
@@ -442,8 +436,7 @@
         def _():
             store_start(group - 1)
 
-        @pl.loop(0, own)
-        def _(src):
+        for src in range(own):
             pull((1 - ix) * own + src, group, x_ref, d_ref, 0, src, None)
 
         @pl.when(group >= 2)
@@ -452,8 +445,7 @@
 
         buf = lax.rem(group, 2)
 
-        @pl.loop(0, GROUP)
-        def _(exp):
+        for exp in range(GROUP):
             base = group * GROUP + exp
             hidden, grad_a, grad_b = hidden_grads(x_ref[exp], d_ref[exp], exp)
             x_own, x_far = xo_ref[base, :, cols], x_ref[exp, :, cols]

time: 369 us -> 294 us (0.80)
  Pallas kernels: 342 us -> 267 us
    pallas_call x2, Pallas kernels: 249 us -> 190 us  [layer_backward(): pl.pallas_call(functools.partial(layer_kernel, last_layer), out_shape=(ja...]
    pallas_call x1, Pallas kernels: 92.6 us -> 76.7 us  [layer_forward(): pl.pallas_call(forward_kernel, out_shape=(block, block, every, every, ran...]
where the time goes in v5:
time: 294 us; the launch traced here: 293 us
  Pallas kernels  267 us (91%)
  local copies, waits for them, and re-layouts  21.1 us (7%)
    pallas_call x2, Pallas kernels, layer_backward(): pl.pallas_call(functools.partial(layer_kernel, last_layer), out_shape=(ja...  190 us
    pallas_call x1, Pallas kernels, layer_forward(): pl.pallas_call(forward_kernel, out_shape=(block, block, every, every, ran...  76.7 us
    unnamed x21, local copies, waits for them, and re-layouts  21.1 us

profile of v5, /device:TPU:0, one launch (start us, length us, event | category | flops | bytes accessed | tf_op | source)
XLA Modules:
  0.0 293.1 jit_solution(8263060807671486015)
XLA Ops:
  0.6 0.7 convert_bitcast_fusion
  1.4 1.4 pad_maximum_fusion.routes_ref
  2.8 2.6 fusion.mine_ref
  5.3 76.7 %shard_map.205 = (bf16[512,512]{1,0:T(8,128)(2,1)}, bf16[512,512]{1,0:T(8,128)(2,1)}, bf16[8,512,512]{2,1,0:T(8,128)(2,1)}, bf16[8,512,512]{2,1,0:T(8,128)(2,1)}...) custom-call(bf16[512,512]{1,0:T(8,128)(2,1)} %fusion.mine_ref, ...), custom_call_target="tpu_custom_call" | custom-call | tf_op jit(solution)/shard_map/pallas_call | solution.py:517
  82.1 93.8 %shard_map.206 = (bf16[512,512]{1,0:T(8,128)(2,1)}, bf16[512,512]{1,0:T(8,128)(2,1)}, bf16[64,192,128]{2,1,0:T(8,128)(2,1)}, bf16[64,192,128]{2,1,0:T(8,128)(2,1)}, bf16[64,192,128]{2,1,0:T(8,128)(2,1)}) custom-call(bf16[8,512,512]{2,1,0:T(8,128)(2,1)} %get-tuple-element.29.refs_0_, bf16[512,512]{1,0:T(8,128)(2,1)} %get-tuple-element.30.refs_1_, ...), custom_call_target="tpu_custom_call" | custom-call | tf_op jit(solution)/shard_map/pallas_call | solution.py:565
  175.9 96.0 %shard_map.207 = (bf16[512,512]{1,0:T(8,128)(2,1)}, bf16[64,512]{1,0:T(8,128)(2,1)}, bf16[64,512]{1,0:T(8,128)(2,1)}, bf16[64,192,128]{2,1,0:T(8,128)(2,1)}, bf1...) custom-call(bf16[8,512,512]{2,1,0:T(8,128)(2,1)} %get-tuple-element.28.refs_0_, ...), custom_call_target="tpu_custom_call" | custom-call | tf_op jit(solution)/shard_map/pallas_call | solution.py:565
  272.0 1.9 copy.32
  273.8 1.5 copy.33
  275.3 0.0 copy-start.4
  275.3 3.9 %copy.34 = bf16[64,128,192]{1,2,0:T(8,128)(2,1)} copy(bf16[64,128,192]{1,2,0:T(8,128)(2,1)} %bitcast.25) | data formatting | bytes 6291456
  279.2 0.0 copy-done.4
  279.2 0.0 copy-start.3
  279.2 1.7 copy.35
  280.9 1.4 copy-done.3
  282.3 0.0 copy-start.5
  282.3 1.7 copy.36
  283.9 0.0 copy-done.5
  283.9 0.6 copy.37
  284.6 0.8 copy-done.2
  285.3 1.7 copy.38
  287.0 1.4 copy-done.1
  288.4 1.7 copy.39
  290.0 1.4 copy-done
  291.4 1.7 copy.40
  (3 shorter events, 0.0 us)
Async XLA Ops:
  275.3 3.9 %copy-start.4 = (bf16[64,192,128]{2,1,0:T(8,128)(2,1)S(1)}, bf16[64,192,128]{2,1,0:T(8,128)(2,1)}, u32[]{:S(2)}) copy-start(bf16[64,192,128]{2,1,0:T(8,128)(2,1)} %get-tuple-element.41) | copy-start | bytes 9437188
  279.2 3.0 %copy-start.3 = (bf16[64,192,128]{2,1,0:T(8,128)(2,1)S(1)}, bf16[64,192,128]{2,1,0:T(8,128)(2,1)}, u32[]{:S(2)}) copy-start(bf16[64,192,128]{2,1,0:T(8,128)(2,1)} %get-tuple-element.62) | copy-start | bytes 9437188
  282.3 1.7 copy-start.5
  282.3 3.1 %copy-start.2 = (bf16[64,192,128]{2,1,0:T(8,128)(2,1)S(1)}, bf16[64,192,128]{2,1,0:T(8,128)(2,1)}, u32[]{:S(2)}) copy-start(bf16[64,192,128]{2,1,0:T(8,128)(2,1)} %get-tuple-element.44) | copy-start | bytes 9437188
  285.3 3.0 %copy-start.1 = (bf16[64,192,128]{2,1,0:T(8,128)(2,1)S(1)}, bf16[64,192,128]{2,1,0:T(8,128)(2,1)}, u32[]{:S(2)}) copy-start(bf16[64,192,128]{2,1,0:T(8,128)(2,1)} %get-tuple-element.45) | copy-start | bytes 9437188
  288.4 3.0 %copy-start = (bf16[64,192,128]{2,1,0:T(8,128)(2,1)S(1)}, bf16[64,192,128]{2,1,0:T(8,128)(2,1)}, u32[]{:S(2)}) copy-start(bf16[64,192,128]{2,1,0:T(8,128)(2,1)} %get-tuple-element.66) | copy-start | bytes 9437188

commit v6 on v5

--- a/solution.py
+++ b/solution.py
@@ -11,6 +11,7 @@
 BF16 = jnp.bfloat16
 CAP = 64
 GROUP = 4
+LANES = 256
 CORES = 2
 CHIPS = 2
 ALL = ('x', 'c', 'y')
@@ -79,10 +80,9 @@
     return pl.when(pl.program_id(0) == number)
 
 
-def gate_hidden(x_rows, w_gate, w_up):
-    a_pre = matmul(x_rows, w_gate, 1, 1)
-    b_pre = matmul(x_rows, w_up, 1, 1)
-    return a_pre, b_pre, jax.nn.sigmoid(a_pre)
+def side_by_side(first, second):
+    pad = jnp.zeros((LANES - first.shape[0], first.shape[1]), first.dtype)
+    return jnp.concatenate([first, pad, second, pad], axis=0)
 
 
 def select_rows(rank_ref, gate_ref, group, src):
@@ -215,20 +215,28 @@
             x_ref[exp, at, :] = rows[exp * CAP:(exp + 1) * CAP]
             row_ref[exp, at, :] = jnp.broadcast_to(gate[exp * CAP:(exp + 1) * CAP], (CAP, 128))
 
-    for exp in range(GROUP):
-        a_pre, b_pre, sigma = gate_hidden(x_ref[exp], wg_ref[exp], wu_ref[exp])
-        hidden = (a_pre * sigma * b_pre).astype(BF16)
-        out = matmul(hidden, wd_ref[exp]).astype(BF16).astype(F32) * row_ref[exp][:, :1]
-        high = out.astype(BF16)
-        rest = out - high.astype(F32)
-        mid = rest.astype(BF16)
-        low = (rest - mid.astype(F32)).astype(BF16)
-        at = slice(exp * CAP, (exp + 1) * CAP)
-        for core in range(CORES):
-            here = slice(core * CAP, (core + 1) * CAP)
-            part_ref[core, 0, at, :] = high[here]
-            part_ref[core, 1, at, :] = mid[here]
-            part_ref[core, 2, at, :] = low[here]
+    ff = wg_ref.shape[1]
+    pre = {}
+    for tick in range(GROUP + 2):
+        if tick < GROUP:
+            pre[tick] = matmul(x_ref[tick], side_by_side(wg_ref[tick], wu_ref[tick]), 1, 1)
+        if 0 < tick <= GROUP:
+            both = pre.pop(tick - 1)
+            a_pre, b_pre = both[:, :ff], both[:, LANES:LANES + ff]
+            pre[tick - 1, 1] = (a_pre * jax.nn.sigmoid(a_pre) * b_pre).astype(BF16)
+        if tick > 1:
+            exp = tick - 2
+            out = matmul(pre.pop((exp, 1)), wd_ref[exp]).astype(BF16).astype(F32) * row_ref[exp][:, :1]
+            high = out.astype(BF16)
+            rest = out - high.astype(F32)
+            mid = rest.astype(BF16)
+            low = (rest - mid.astype(F32)).astype(BF16)
+            at = slice(exp * CAP, (exp + 1) * CAP)
+            for core in range(CORES):
+                here = slice(core * CAP, (core + 1) * CAP)
+                part_ref[core, 0, at, :] = high[here]
+                part_ref[core, 1, at, :] = mid[here]
+                part_ref[core, 2, at, :] = low[here]
 
     for core in range(CORES):
         pick = pick_ref[core]
@@ -331,21 +339,25 @@
         for copy in store_copies(group, False):
             copy.wait()
 
-    def pull(src, group, x_dst, d_dst, base, at, keep):
+    def pull(src, group, at, keep):
         pick, gate = select_rows(rank_ref, gate_ref, group, src)
-        if keep is not None:
-            pick_ref[keep] = pick
+        if keep:
+            pick_ref[at] = pick
         x_rows = matmul(pick, u_ref[src]).astype(BF16)
         d_rows = (matmul(pick, dy_ref[src]) * gate).astype(BF16)
-        rows = pl.ds(pl.multiple_of(at * CAP, CAP), CAP)
         for exp in range(GROUP):
-            x_dst[base + exp, rows, :] = x_rows[exp * CAP:(exp + 1) * CAP]
-            d_dst[base + exp, rows, :] = d_rows[exp * CAP:(exp + 1) * CAP]
-
-    def hidden_grads(x_rows, d_rows, exp):
-        a_pre, b_pre, sigma = gate_hidden(x_rows, wg_ref[exp], wu_ref[exp])
+            x_ref[exp, at * CAP:(at + 1) * CAP, :] = x_rows[exp * CAP:(exp + 1) * CAP]
+            d_ref[exp, at * CAP:(at + 1) * CAP, :] = d_rows[exp * CAP:(exp + 1) * CAP]
+
+    def hidden_pre(x_rows, d_rows, exp):
+        ff = wg_ref.shape[1]
+        both = matmul(x_rows, side_by_side(wg_ref[exp], wu_ref[exp]), 1, 1)
+        return both[:, :ff], both[:, LANES:LANES + ff], matmul(d_rows, wd_ref[exp], 1, 1)
+
+    def hidden_grads(a_pre, b_pre, back):
+        sigma = jax.nn.sigmoid(a_pre)
         silu = a_pre * sigma
-        grad_hidden = matmul(d_rows, wd_ref[exp], 1, 1).astype(BF16).astype(F32)
+        grad_hidden = back.astype(BF16).astype(F32)
         grad_a = (grad_hidden * b_pre * sigma * (1.0 + a_pre * (1.0 - sigma))).astype(BF16)
         return (silu * b_pre).astype(BF16), grad_a, (grad_hidden * silu).astype(BF16)
 
@@ -390,17 +402,28 @@
         rows = pl.ds(pl.multiple_of(late * CORES * CAP, CORES * CAP), CORES * CAP)
 
         for core in range(CORES):
-            pull(rank_of(ix, core, y_now), group, xo_ref, do_ref, base, late * CORES + core, core)
-
-        for exp in range(GROUP):
-            hidden, grad_a, grad_b = hidden_grads(xo_ref[base + exp, rows, :], do_ref[base + exp, rows, :], exp)
-            h_ref[base + exp, rows, :] = hidden
-            ga_ref[base + exp, rows, :] = grad_a
-            gb_ref[base + exp, rows, :] = grad_b
-            grad_x = (matmul(grad_a, wg_ref[exp]) + matmul(grad_b, wu_ref[exp])).astype(BF16)
-            at = slice(exp * CAP, (exp + 1) * CAP)
-            for core in range(CORES):
-                gx_ref[core, at, :] = grad_x[core * CAP:(core + 1) * CAP]
+            pull(rank_of(ix, core, y_now), group, core, True)
+
+        near = CORES * CAP
+        pre = {}
+        for tick in range(GROUP + 2):
+            if tick < GROUP:
+                pre[tick] = hidden_pre(x_ref[tick, :near, :], d_ref[tick, :near, :], tick)
+            if 0 < tick <= GROUP:
+                exp = tick - 1
+                hidden, grad_a, grad_b = hidden_grads(*pre.pop(exp))
+                xo_ref[base + exp, rows, :] = x_ref[exp, :near, cols]
+                do_ref[base + exp, rows, :] = d_ref[exp, :near, cols]
+                h_ref[base + exp, rows, :] = hidden
+                ga_ref[base + exp, rows, :] = grad_a
+                gb_ref[base + exp, rows, :] = grad_b
+                pre[exp, 1] = None
+            if tick > 1:
+                exp = tick - 2
+                grad_x = (matmul(ga_ref[base + exp, rows, :], wg_ref[exp]) + matmul(gb_ref[base + exp, rows, :], wu_ref[exp])).astype(BF16)
+                at = slice(exp * CAP, (exp + 1) * CAP)
+                for core in range(CORES):
+                    gx_ref[core, at, :] = grad_x[core * CAP:(core + 1) * CAP]
 
         for core in range(CORES):
             p_ref[core * 2 + y_now] += matmul(pick_ref[core], gx_ref[core], 0, 0)
@@ -411,9 +434,8 @@
         add_up(1).start()
         spread(5).wait_recv()
         spread(6).wait_recv()
-
-    @at_step(n_first + 1)
-    def _():
+        add_up(0).wait_recv()
+        p_ref[ic * 2 + 1 - iy] += rs_ref[0]
         add_up(2).start()
 
     @at_step(n_step - 1)
@@ -432,35 +454,38 @@
     def _():
         group = step - n_first
 
+        @pl.when(group >= 2)
+        def _():
+            store_wait(group - 2)
+
         @pl.when(group >= 1)
         def _():
             store_start(group - 1)
 
         for src in range(own):
-            pull((1 - ix) * own + src, group, x_ref, d_ref, 0, src, None)
-
-        @pl.when(group >= 2)
-        def _():
-            store_wait(group - 2)
+            pull((1 - ix) * own + src, group, src, False)
 
         buf = lax.rem(group, 2)
 
-        for exp in range(GROUP):
-            base = group * GROUP + exp
-            hidden, grad_a, grad_b = hidden_grads(x_ref[exp], d_ref[exp], exp)
-            x_own, x_far = xo_ref[base, :, cols], x_ref[exp, :, cols]
-            d_own, d_far = do_ref[base, :, cols], d_ref[exp, :, cols]
-            grads = (matmul(ga_ref[base], x_own, 0, 0) + matmul(grad_a, x_far, 0, 0),
-                     matmul(gb_ref[base], x_own, 0, 0) + matmul(grad_b, x_far, 0, 0),
-                     matmul(h_ref[base], d_own, 0, 0) + matmul(hidden, d_far, 0, 0))
-            for kind in range(3):
-                for core in range(CORES):
-                    stage_ref[buf, core, kind, exp] = grads[kind][:, core * piece:(core + 1) * piece].astype(BF16)
-
-    @at_step(n_first)
-    def _():
-        add_up(0).wait_recv()
-        p_ref[ic * 2 + 1 - iy] += rs_ref[0]
+        pre = {}
+        for tick in range(GROUP + 2):
+            if tick < GROUP:
+                pre[tick] = hidden_pre(x_ref[tick], d_ref[tick], tick)
+            if 0 < tick <= GROUP:
+                exp = tick - 1
+                pre[exp, 1] = hidden_grads(*pre.pop(exp))
+            if tick > 1:
+                exp = tick - 2
+                base = group * GROUP + exp
+                hidden, grad_a, grad_b = pre.pop((exp, 1))
+                x_own, x_far = xo_ref[base], x_ref[exp, :, cols]
+                d_own, d_far = do_ref[base], d_ref[exp, :, cols]
+                grads = (matmul(ga_ref[base], x_own, 0, 0) + matmul(grad_a, x_far, 0, 0),
+                         matmul(gb_ref[base], x_own, 0, 0) + matmul(grad_b, x_far, 0, 0),
+                         matmul(h_ref[base], d_own, 0, 0) + matmul(hidden, d_far, 0, 0))
+                for kind in range(3):
+                    for core in range(CORES):
+                        stage_ref[buf, core, kind, exp] = grads[kind][:, core * piece:(core + 1) * piece].astype(BF16)
 
     @at_step(n_step - 1)
     def _():
@@ -551,8 +576,9 @@
     slab_shape = jax.ShapeDtypeStruct((dim // 8, dim), BF16)
     extra_shapes = (slab_shape, slab_shape) if last_layer else (part_shape,)
     extra_specs = (slab, slab) if last_layer else (square,)
-    scratch = [pltpu.VMEM((n_src, n_tok, dim), BF16), pltpu.VMEM((n_exp, kept, dim), BF16),
-               pltpu.VMEM((n_exp, kept, dim), BF16), pltpu.VMEM((n_exp, kept, ff), BF16),
+    half = dim // CHIPS
+    scratch = [pltpu.VMEM((n_src, n_tok, dim), BF16), pltpu.VMEM((n_exp, kept, half), BF16),
+               pltpu.VMEM((n_exp, kept, half), BF16), pltpu.VMEM((n_exp, kept, ff), BF16),
                pltpu.VMEM((n_exp, kept, ff), BF16), pltpu.VMEM((n_exp, kept, ff), BF16),
                pltpu.VMEM((CORES, GROUP * CAP, n_tok), BF16), pltpu.VMEM((CORES, GROUP * CAP, dim), BF16)]
     scratch += sums_scratch(own, n_tok, dim)

time: 294 us -> 269 us (0.915)
  Pallas kernels: 267 us -> 242 us
    pallas_call x2, Pallas kernels: 190 us -> 167 us  [layer_backward(): pl.pallas_call(functools.partial(layer_kernel, last_layer), out_shape=(ja...]
where the time goes in v6:
time: 269 us
  Pallas kernels  242 us (90%)
  local copies, waits for them, and re-layouts  21.1 us (8%)
    pallas_call x2, Pallas kernels, layer_backward(): pl.pallas_call(functools.partial(layer_kernel, last_layer), out_shape=(ja...  167 us
    pallas_call x1, Pallas kernels, layer_forward(): pl.pallas_call(forward_kernel, out_shape=(block, block, every, every, ran...  75.3 us
    unnamed x21, local copies, waits for them, and re-layouts  21.1 us

profile of v6, /device:TPU:0, one launch (start us, length us, event | category | flops | bytes accessed | tf_op | source)
XLA Modules:
  0.0 268.6 jit_solution(7551786511348653377)
XLA Ops:
  0.6 0.7 convert_bitcast_fusion
  1.4 1.4 pad_maximum_fusion.routes_ref
  2.8 2.6 fusion.mine_ref
  5.3 75.3 %shard_map.205 = (bf16[512,512]{1,0:T(8,128)(2,1)}, bf16[512,512]{1,0:T(8,128)(2,1)}, bf16[8,512,512]{2,1,0:T(8,128)(2,1)}, bf16[8,512,512]{2,1,0:T(8,128)(2,1)}...) custom-call(bf16[512,512]{1,0:T(8,128)(2,1)} %fusion.mine_ref, ...), custom_call_target="tpu_custom_call" | custom-call | tf_op jit(solution)/shard_map/pallas_call | solution.py:542
  80.6 82.1 %shard_map.206 = (bf16[512,512]{1,0:T(8,128)(2,1)}, bf16[512,512]{1,0:T(8,128)(2,1)}, bf16[64,192,128]{2,1,0:T(8,128)(2,1)}, bf16[64,192,128]{2,1,0:T(8,128)(2,1)}, bf16[64,192,128]{2,1,0:T(8,128)(2,1)}) custom-call(bf16[8,512,512]{2,1,0:T(8,128)(2,1)} %get-tuple-element.29.refs_0_, bf16[512,512]{1,0:T(8,128)(2,1)} %get-tuple-element.30.refs_1_, ...), custom_call_target="tpu_custom_call" | custom-call | tf_op jit(solution)/shard_map/pallas_call | solution.py:591
  162.7 84.7 %shard_map.207 = (bf16[512,512]{1,0:T(8,128)(2,1)}, bf16[64,512]{1,0:T(8,128)(2,1)}, bf16[64,512]{1,0:T(8,128)(2,1)}, bf16[64,192,128]{2,1,0:T(8,128)(2,1)}, bf1...) custom-call(bf16[8,512,512]{2,1,0:T(8,128)(2,1)} %get-tuple-element.28.refs_0_, ...), custom_call_target="tpu_custom_call" | custom-call | tf_op jit(solution)/shard_map/pallas_call | solution.py:591
  247.5 1.9 copy.32
  249.3 1.5 copy.33
  250.8 0.0 copy-start.4
  250.8 3.9 %copy.34 = bf16[64,128,192]{1,2,0:T(8,128)(2,1)} copy(bf16[64,128,192]{1,2,0:T(8,128)(2,1)} %bitcast.25) | data formatting | bytes 6291456
  254.7 0.0 copy-done.4
  254.7 0.0 copy-start.3
  254.7 1.7 copy.35
  256.4 1.4 copy-done.3
  257.8 0.0 copy-start.5
  257.8 1.7 copy.36
  259.4 0.0 copy-done.5
  259.4 0.6 copy.37
  260.1 0.8 copy-done.2
  260.8 1.7 copy.38
  262.5 1.4 copy-done.1
  263.9 1.7 copy.39
  265.5 1.4 copy-done
  266.9 1.7 copy.40
  (3 shorter events, 0.0 us)
Async XLA Ops:
  250.8 3.9 %copy-start.4 = (bf16[64,192,128]{2,1,0:T(8,128)(2,1)S(1)}, bf16[64,192,128]{2,1,0:T(8,128)(2,1)}, u32[]{:S(2)}) copy-start(bf16[64,192,128]{2,1,0:T(8,128)(2,1)} %get-tuple-element.41) | copy-start | bytes 9437188
  254.7 3.0 %copy-start.3 = (bf16[64,192,128]{2,1,0:T(8,128)(2,1)S(1)}, bf16[64,192,128]{2,1,0:T(8,128)(2,1)}, u32[]{:S(2)}) copy-start(bf16[64,192,128]{2,1,0:T(8,128)(2,1)} %get-tuple-element.62) | copy-start | bytes 9437188
  257.8 1.7 copy-start.5
  257.8 3.1 %copy-start.2 = (bf16[64,192,128]{2,1,0:T(8,128)(2,1)S(1)}, bf16[64,192,128]{2,1,0:T(8,128)(2,1)}, u32[]{:S(2)}) copy-start(bf16[64,192,128]{2,1,0:T(8,128)(2,1)} %get-tuple-element.44) | copy-start | bytes 9437188
  260.8 3.0 %copy-start.1 = (bf16[64,192,128]{2,1,0:T(8,128)(2,1)S(1)}, bf16[64,192,128]{2,1,0:T(8,128)(2,1)}, u32[]{:S(2)}) copy-start(bf16[64,192,128]{2,1,0:T(8,128)(2,1)} %get-tuple-element.45) | copy-start | bytes 9437188
  263.9 3.0 %copy-start = (bf16[64,192,128]{2,1,0:T(8,128)(2,1)S(1)}, bf16[64,192,128]{2,1,0:T(8,128)(2,1)}, u32[]{:S(2)}) copy-start(bf16[64,192,128]{2,1,0:T(8,128)(2,1)} %get-tuple-element.66) | copy-start | bytes 9437188

commit v7 on v6

--- a/solution.py
+++ b/solution.py
@@ -112,21 +112,24 @@
     gate_ref[src] = gates
 
 
-def forward_kernel(mine_ref, grad_ref, routes_ref, dense_ref, wg_ref, wu_ref, wd_ref,
+def forward_kernel(tok_ref, grad_ref, idx1_ref, idx2_ref, top1_ref, top2_ref, mix_ref, dense_ref, wg_ref, wu_ref, wd_ref,
                    y_ref, u_ref, uall_ref, dall_ref, rank1_ref, gate1_ref, rank2_ref, gate2_ref,
-                   us_ref, ds_ref, route_ref, before_ref, pick_ref, row_ref, x_ref, part_ref, p_ref, rs_ref,
+                   raw_ref, us_ref, ds_ref, routes_ref, route_ref, before_ref, pick_ref, row_ref, x_ref, part_ref, p_ref, rs_ref,
                    u_send, u_recv, d_send, d_recv, t_send, t_recv, rs_send, rs_recv, out_sem):
     n_exp, n_tok = rank1_ref.shape[1:]
     n_group = n_exp // GROUP
     step = pl.program_id(0)
     ix, ic, iy = position()
     me = rank_of(ix, ic, iy)
-    spread_u = spreader(mine_ref, us_ref, (u_send, u_recv))
+    spread_u = spreader(tok_ref, raw_ref, (u_send, u_recv))
     spread_d = spreader(grad_ref, ds_ref, (d_send, d_recv))
     spread_t = spreader(routes_ref, route_ref, (t_send, t_recv))
     add_up = adder(p_ref, rs_ref, (rs_send, rs_recv))
     stores = ((us_ref, uall_ref), (ds_ref, dall_ref))
 
+    def mixed(x):
+        return (x.astype(F32) + matmul(x, mix_ref[...])).astype(BF16)
+
     def pass_on(copy, arrived, onward):
         copy(arrived).wait_recv()
         for at in onward:
@@ -134,17 +137,21 @@
 
     @at_step(0)
     def _():
+        for at, part_in in enumerate((idx1_ref, idx2_ref, top1_ref, top2_ref)):
+            routes_ref[at * 8:at * 8 + 8, :] = part_in[...].astype(F32)
         greet(False)
         for copy in (spread_t, spread_u):
             for at in (0, 3, 1):
                 copy(at).start()
-        us_ref[me] = mine_ref[...]
+        us_ref[me] = mixed(tok_ref[...])
         ds_ref[me] = grad_ref[...]
         route_ref[me] = routes_ref[...]
         p_ref[...] = jnp.zeros_like(p_ref)
         before_ref[...] = jnp.where(lax.broadcasted_iota(jnp.int32, (n_tok, n_tok), 0)
                                     < lax.broadcasted_iota(jnp.int32, (n_tok, n_tok), 1), 1.0, 0.0).astype(BF16)
         pass_on(spread_t, 0, (4, 2))
+        spread_u(3).wait_recv()
+        us_ref[rank_of(ix, 1 - ic, iy)] = mixed(raw_ref[rank_of(ix, 1 - ic, iy)])
         spread_t(3).wait_recv()
         spread_t(4).wait_recv()
 
@@ -155,8 +162,9 @@
         pass_on(spread_u, 0, (4, 2))
         for at in (0, 3, 1):
             spread_d(at).start()
-        spread_u(3).wait_recv()
+        us_ref[rank_of(ix, ic, 1 - iy)] = mixed(raw_ref[rank_of(ix, ic, 1 - iy)])
         spread_u(4).wait_recv()
+        us_ref[rank_of(ix, 1 - ic, 1 - iy)] = mixed(raw_ref[rank_of(ix, 1 - ic, 1 - iy)])
 
     @at_step(n_group // 4)
     def _():
@@ -171,11 +179,13 @@
 
     @at_step(n_group - 1)
     def _():
-        spread_t(5).wait_recv()
-        spread_t(6).wait_recv()
+        for copy in (spread_t, spread_u):
+            copy(5).wait_recv()
+            copy(6).wait_recv()
 
         @pl.loop(0, 4)
         def _(src):
+            us_ref[(1 - ix) * 4 + src] = mixed(raw_ref[(1 - ix) * 4 + src])
             route_table(route_ref, before_ref, (1 - ix) * 4 + src, 0, rank1_ref, gate1_ref, n_exp)
 
         @pl.loop(0, 8)
@@ -185,6 +195,7 @@
     @at_step(n_group)
     def _():
         add_up(0).start()
+        pltpu.make_async_copy(us_ref, uall_ref, out_sem.at[0]).start()
 
     @at_step(n_group + 1)
     def _():
@@ -194,12 +205,15 @@
     def _():
         pass_on(spread_d, 1, (5,))
 
+    @at_step(2 * n_group - 2)
+    def _():
+        pass_on(spread_d, 2, (6,))
+
     @at_step(2 * n_group - 1)
     def _():
-        pass_on(spread_d, 2, (6,))
-        spread_u(5).wait_recv()
-        spread_u(6).wait_recv()
-        pltpu.make_async_copy(us_ref, uall_ref, out_sem.at[0]).start()
+        for at in (3, 4, 5, 6):
+            spread_d(at).wait_recv()
+        pltpu.make_async_copy(ds_ref, dall_ref, out_sem.at[1]).start()
 
     group = lax.rem(step, n_group)
     far = 1 - lax.div(step, n_group)
@@ -251,13 +265,10 @@
 
     @at_step(2 * n_group - 1)
     def _():
-        for at in (3, 4, 5, 6):
-            spread_d(at).wait_recv()
-        pltpu.make_async_copy(ds_ref, dall_ref, out_sem.at[1]).start()
         add_up(1).start()
         add_up(1).wait_recv()
         add_up(2).wait_recv()
-        y_own = (mine_ref[...].astype(F32) + (p_ref[ic * 2 + iy] + rs_ref[1] + rs_ref[2])).astype(BF16)
+        y_own = (us_ref[me].astype(F32) + (p_ref[ic * 2 + iy] + rs_ref[1] + rs_ref[2])).astype(BF16)
         y_ref[...] = y_own
         u_ref[...] = (y_own.astype(F32) + matmul(y_own, dense_ref[...])).astype(BF16)
         for copy in (spread_u, spread_d, spread_t):
@@ -434,8 +445,9 @@
         add_up(1).start()
         spread(5).wait_recv()
         spread(6).wait_recv()
-        add_up(0).wait_recv()
-        p_ref[ic * 2 + 1 - iy] += rs_ref[0]
+
+    @at_step(n_first + 1)
+    def _():
         add_up(2).start()
 
     @at_step(n_step - 1)
@@ -487,6 +499,11 @@
                     for core in range(CORES):
                         stage_ref[buf, core, kind, exp] = grads[kind][:, core * piece:(core + 1) * piece].astype(BF16)
 
+    @at_step(n_first)
+    def _():
+        add_up(0).wait_recv()
+        p_ref[ic * 2 + 1 - iy] += rs_ref[0]
+
     @at_step(n_step - 1)
     def _():
         last = n_group - 1
@@ -524,8 +541,9 @@
     return [pltpu.VMEM((own, n_tok, dim), F32), pltpu.VMEM((3, n_tok, dim), F32)]
 
 
-def layer_forward(mine, grad, routes, dense, w_gate, w_up, w_down):
-    n_tok, dim = mine.shape
+def layer_forward(tokens, grad, idx1, idx2, top1, top2, dense1, dense2, w_gate, w_up, w_down):
+    n_tok, dim = tokens.shape
+    top = idx1.shape[0]
     n_all, ff, _ = w_gate.shape
     n_exp = n_all // CORES
     n_src = 8
@@ -544,17 +562,17 @@
         out_shape=(block, block, every, every, ranks, gates, ranks, gates),
         grid_spec=pltpu.PrefetchScalarGridSpec(
             num_scalar_prefetch=0, grid=(2 * groups,),
-            in_specs=[fixed(n_tok, dim), fixed(n_tok, dim), fixed(*routes.shape), fixed(dim, dim), tall, tall, tall],
+            in_specs=[fixed(n_tok, dim)] * 2 + [fixed(top, n_tok)] * 4 + [fixed(dim, dim)] * 2 + [tall] * 3,
             out_specs=(fixed(n_tok, dim), fixed(n_tok, dim), anywhere, anywhere, table, table, table, table),
-            scratch_shapes=[pltpu.VMEM((n_src, n_tok, dim), BF16), pltpu.VMEM((n_src, n_tok, dim), BF16),
-                            pltpu.VMEM((n_src,) + routes.shape, F32), pltpu.VMEM((n_tok, n_tok), BF16),
+            scratch_shapes=[pltpu.VMEM((n_src, n_tok, dim), BF16)] * 3
+            + [pltpu.VMEM((4 * top, n_tok), F32), pltpu.VMEM((n_src, 4 * top, n_tok), F32), pltpu.VMEM((n_tok, n_tok), BF16),
                             pltpu.VMEM((CORES, GROUP * CAP, n_tok), BF16), pltpu.VMEM((GROUP, rows, 128), F32),
                             pltpu.VMEM((GROUP, rows, dim), BF16), pltpu.VMEM((CORES, 3, GROUP * CAP, dim), BF16)]
             + sums_scratch(own, n_tok, dim)
             + [dma_sems(7)] * 6 + [dma_sems(3)] * 2 + [dma_sems(2)]),
         compiler_params=pltpu.CompilerParams(dimension_semantics=('arbitrary',), vmem_limit_bytes=62 << 20,
                                              collective_id=0, has_side_effects=True),
-    )(mine, grad, routes, dense, w_gate, w_up, w_down)
+    )(tokens, grad, idx1, idx2, top1, top2, dense1, dense2, w_gate, w_up, w_down)
 
 
 def layer_backward(whole, mine, rank, gate, x_own, grad_own, dense, w_gate, w_up, w_down, other=None):
@@ -602,8 +620,36 @@
     )(*operands)
 
 
-def mix(x, weight):
-    return (x.astype(F32) + jnp.dot(x, weight, preferred_element_type=F32)).astype(BF16)
+def settle_kernel(chunks, *refs):
+    n = len(chunks)
+    sources, outs, bufs = refs[:n], refs[n:2 * n], refs[2 * n:3 * n]
+    in_sem, out_sem = refs[3 * n:]
+    loads, stores = [], []
+    for src, out, buf, count in zip(sources, outs, bufs, chunks):
+        rows = src.shape[0] // count
+        for at in range(count):
+            here = pl.ds(at * rows, rows)
+            loads.append(pltpu.make_async_copy(src.at[here], buf.at[here], in_sem.at[len(loads)]))
+            stores.append(pltpu.make_async_copy(buf.at[here], out.at[here], out_sem.at[len(stores)]))
+    for load in loads:
+        load.start()
+    for load, store in zip(loads, stores):
+        load.wait()
+        store.start()
+    for store in stores:
+        store.wait()
+
+
+def settle(*arrays):
+    chunks = tuple(8 if array.ndim == 3 else 1 for array in arrays)
+    anywhere = pl.BlockSpec(memory_space=pl.ANY)
+    return pl.pallas_call(
+        functools.partial(settle_kernel, chunks),
+        out_shape=tuple(jax.ShapeDtypeStruct(array.shape, array.dtype) for array in arrays),
+        in_specs=[anywhere] * len(arrays), out_specs=(anywhere,) * len(arrays),
+        scratch_shapes=[pltpu.VMEM(array.shape, array.dtype) for array in arrays] + [dma_sems(sum(chunks))] * 2,
+        compiler_params=pltpu.CompilerParams(vmem_limit_bytes=40 << 20),
+    )(*arrays)
 
 
 def solution(mesh):
@@ -615,16 +661,15 @@
 
     def local_step(tokens, dy_out, dense_w1, route_idx1, route_gate1, w_gate1, w_up1, w_down1, dense_w2, route_idx2, route_gate2, w_gate2, w_up2, w_down2):
         w_gate1, w_up1, w_gate2, w_up2 = (jnp.swapaxes(w, 1, 2) for w in (w_gate1, w_up1, w_gate2, w_up2))
-        routes = jnp.concatenate([route_idx1.astype(F32).T, route_idx2.astype(F32).T, route_gate1.T, route_gate2.T], axis=0)
-        u_one = mix(tokens, dense_w1)
         y_one, u_two, u_all, dy_all, rank1, gate1, rank2, gate2 = layer_forward(
-            u_one, dy_out, routes, dense_w2, w_gate1, w_up1, w_down1)
-        grad_mid, part_two, gg, gu, gd = layer_backward(
+            tokens, dy_out, route_idx1.T, route_idx2.T, route_gate1.T, route_gate2.T, dense_w1, dense_w2, w_gate1, w_up1, w_down1)
+        grad_mid, part_two, *grads_two = layer_backward(
             dy_all, u_two, rank2, gate2, y_one, dy_out, dense_w2, w_gate2, w_up2, w_down2)
-        gate_two, up_two, down_two = jnp.swapaxes(gg, 1, 2), jnp.swapaxes(gu, 1, 2), gd
-        grad_tok, dense_one, dense_two, gg, gu, gd = layer_backward(
+        grad_tok, dense_one, dense_two, *grads_one = layer_backward(
             u_all, grad_mid, rank1, gate1, tokens, grad_mid, dense_w1, w_gate1, w_up1, w_down1, part_two)
-        gate_one, up_one, down_one = jnp.swapaxes(gg, 1, 2), jnp.swapaxes(gu, 1, 2), gd
+        (grad_tok, dense_one, gate_one, up_one, down_one, dense_two, gate_two, up_two, down_two) = settle(
+            grad_tok, dense_one, *grads_one, dense_two, *grads_two)
+        gate_one, up_one, gate_two, up_two = (jnp.swapaxes(g, 1, 2) for g in (gate_one, up_one, gate_two, up_two))
         return (grad_tok, dense_one, gate_one, up_one, down_one, dense_two, gate_two, up_two, down_two)
 
     return jax.shard_map(local_step, mesh=fine, in_specs=(tok_spec, tok_spec) + layer_specs + layer_specs,

time: 269 us -> 274 us (1.019)
  Pallas kernels: 242 us -> 262 us
  local copies, waits for them, and re-layouts: 21.1 us -> 10.3 us
    pallas_call x0 -> x1, Pallas kernels: none -> 15.4 us  [settle(): pl.pallas_call(functools.partial(settle_kernel, chunks), out_shape=tuple(...]
    unnamed x21 -> x14, local copies, waits for them, and re-layouts: 21.1 us -> 10.3 us
    pallas_call x2, Pallas kernels: 167 us -> 170 us  [layer_backward(): pl.pallas_call(functools.partial(layer_kernel, last_layer), out_shape=(ja...]
where the time goes in v7:
time: 274 us; the launch traced here: 273 us
  Pallas kernels  262 us (96%)
  local copies, waits for them, and re-layouts  10.3 us (4%)
    pallas_call x2, Pallas kernels, layer_backward(): pl.pallas_call(functools.partial(layer_kernel, last_layer), out_shape=(ja...  170 us
    pallas_call x1, Pallas kernels, layer_forward(): pl.pallas_call(forward_kernel, out_shape=(block, block, every, every, ran...  76.8 us
    pallas_call x1, Pallas kernels, settle(): pl.pallas_call(functools.partial(settle_kernel, chunks), out_shape=tuple(...  15.4 us
    unnamed x14, local copies, waits for them, and re-layouts  10.3 us

profile of v7, /device:TPU:0, one launch (start us, length us, event | category | flops | bytes accessed | tf_op | source)
XLA Modules:
  0.0 273.4 jit_solution(5841435013684451466)
XLA Ops:
  0.6 76.8 %shard_map.205 = (bf16[512,512]{1,0:T(8,128)(2,1)}, bf16[512,512]{1,0:T(8,128)(2,1)}, bf16[8,512,512]{2,1,0:T(8,128)(2,1)}, bf16[8,512,512]{2,1,0:T(8,128)(2,1)}...) custom-call(bf16[512,512]{1,0:T(8,128)(2,1)} %refs_4_.1, ...), custom_call_target="tpu_custom_call" | custom-call | tf_op jit(solution)/shard_map/pallas_call | solution.py:560
  77.4 83.1 %shard_map.206 = (bf16[512,512]{1,0:T(8,128)(2,1)}, bf16[512,512]{1,0:T(8,128)(2,1)}, bf16[64,192,128]{2,1,0:T(8,128)(2,1)}, bf16[64,192,128]{2,1,0:T(8,128)(2,1)}, bf16[64,192,128]{2,1,0:T(8,128)(2,1)}) custom-call(bf16[8,512,512]{2,1,0:T(8,128)(2,1)} %get-tuple-element.38.refs_0_, bf16[512,512]{1,0:T(8,128)(2,1)} %get-tuple-element.39.refs_1_, ...), custom_call_target="tpu_custom_call" | custom-call | tf_op jit(solution)/shard_map/pallas_call | solution.py:609
  160.5 87.0 %shard_map.207 = (bf16[512,512]{1,0:T(8,128)(2,1)}, bf16[64,512]{1,0:T(8,128)(2,1)}, bf16[64,512]{1,0:T(8,128)(2,1)}, bf16[64,192,128]{2,1,0:T(8,128)(2,1)}, bf1...) custom-call(bf16[8,512,512]{2,1,0:T(8,128)(2,1)} %get-tuple-element.37.refs_0_, ...), custom_call_target="tpu_custom_call" | custom-call | tf_op jit(solution)/shard_map/pallas_call | solution.py:609
  247.5 0.0 copy-start
  247.6 1.9 copy-done
  249.4 0.0 copy-start.1
  249.4 1.9 copy-done.1
  251.3 0.0 copy-start.2
  251.3 1.9 copy-done.2
  253.2 0.0 copy-start.3
  253.2 1.9 copy-done.3
  255.1 0.0 copy-start.4
  255.1 1.0 copy-done.4
  256.2 0.0 copy-start.5
  256.2 0.8 copy-done.5
  257.0 0.0 copy-start.6
  257.0 0.8 copy-done.6
  257.8 15.4 %shard_map.208 = (bf16[512,512]{1,0:T(8,128)(2,1)}, bf16[64,512]{1,0:T(8,128)(2,1)}, bf16[64,192,128]{2,1,0:T(8,128)(2,1)}, bf16[64,192,128]{2,1,0:T(8,128)(2,1)...) custom-call(bf16[512,512]{1,0:T(8,128)(2,1)S(1)} %copy-done.4, ...), custom_call_target="tpu_custom_call" | custom-call | tf_op jit(solution)/shard_map/pallas_call | solution.py:646
Async XLA Ops:
  247.5 1.9 copy-start
  249.4 1.9 copy-start.1
  251.3 1.9 copy-start.2
  253.2 1.9 copy-start.3
  255.1 1.0 copy-start.4
  256.2 0.8 copy-start.5
  257.0 0.8 copy-start.6

commit v8 on v7

--- a/solution.py
+++ b/solution.py
@@ -384,7 +384,7 @@
         p_ref[...] = jnp.zeros_like(p_ref)
         spread(3).wait_recv()
 
-    @at_step(n_group // 2)
+    @at_step(n_group - 2)
     def _():
         spread(0).wait_recv()
         spread(4).start()
@@ -445,9 +445,8 @@
         add_up(1).start()
         spread(5).wait_recv()
         spread(6).wait_recv()
-
-    @at_step(n_first + 1)
-    def _():
+        add_up(0).wait_recv()
+        p_ref[ic * 2 + 1 - iy] += rs_ref[0]
         add_up(2).start()
 
     @at_step(n_step - 1)
@@ -498,11 +497,6 @@
                 for kind in range(3):
                     for core in range(CORES):
                         stage_ref[buf, core, kind, exp] = grads[kind][:, core * piece:(core + 1) * piece].astype(BF16)
-
-    @at_step(n_first)
-    def _():
-        add_up(0).wait_recv()
-        p_ref[ic * 2 + 1 - iy] += rs_ref[0]
 
     @at_step(n_step - 1)
     def _():
@@ -648,7 +642,7 @@
         out_shape=tuple(jax.ShapeDtypeStruct(array.shape, array.dtype) for array in arrays),
         in_specs=[anywhere] * len(arrays), out_specs=(anywhere,) * len(arrays),
         scratch_shapes=[pltpu.VMEM(array.shape, array.dtype) for array in arrays] + [dma_sems(sum(chunks))] * 2,
-        compiler_params=pltpu.CompilerParams(vmem_limit_bytes=40 << 20),
+        compiler_params=pltpu.CompilerParams(vmem_limit_bytes=67043328),
     )(*arrays)
 
 

time: 274 us -> 258 us (0.942)
  local copies, waits for them, and re-layouts: 10.3 us -> 0 us
  Pallas kernels: 262 us -> 257 us
    unnamed x14 -> x0, local copies, waits for them, and re-layouts: 10.3 us -> none
    pallas_call x2, Pallas kernels: 170 us -> 166 us  [layer_backward(): pl.pallas_call(functools.partial(layer_kernel, last_layer), out_shape=(ja...]
where the time goes in v8:
time: 258 us
  Pallas kernels  257 us (100%)
    pallas_call x2, Pallas kernels, layer_backward(): pl.pallas_call(functools.partial(layer_kernel, last_layer), out_shape=(ja...  166 us
    pallas_call x1, Pallas kernels, layer_forward(): pl.pallas_call(forward_kernel, out_shape=(block, block, every, every, ran...  76.8 us
    pallas_call x1, Pallas kernels, settle(): pl.pallas_call(functools.partial(settle_kernel, chunks), out_shape=tuple(...  14.2 us

profile of v8, /device:TPU:0, one launch (start us, length us, event | category | flops | bytes accessed | tf_op | source)
XLA Modules:
  0.0 257.5 jit_solution(11351224041932780382)
XLA Ops:
  0.6 76.8 %shard_map.205 = (bf16[512,512]{1,0:T(8,128)(2,1)}, bf16[512,512]{1,0:T(8,128)(2,1)}, bf16[8,512,512]{2,1,0:T(8,128)(2,1)}, bf16[8,512,512]{2,1,0:T(8,128)(2,1)}...) custom-call(bf16[512,512]{1,0:T(8,128)(2,1)} %refs_4_.1, ...), custom_call_target="tpu_custom_call" | custom-call | tf_op jit(solution)/shard_map/pallas_call | solution.py:554
  77.5 81.1 %shard_map.206 = (bf16[512,512]{1,0:T(8,128)(2,1)}, bf16[512,512]{1,0:T(8,128)(2,1)}, bf16[64,192,128]{2,1,0:T(8,128)(2,1)}, bf16[64,192,128]{2,1,0:T(8,128)(2,1)}, bf16[64,192,128]{2,1,0:T(8,128)(2,1)}) custom-call(bf16[8,512,512]{2,1,0:T(8,128)(2,1)} %get-tuple-element.38.refs_0_, bf16[512,512]{1,0:T(8,128)(2,1)} %get-tuple-element.39.refs_1_, ...), custom_call_target="tpu_custom_call" | custom-call | tf_op jit(solution)/shard_map/pallas_call | solution.py:603
  158.6 84.5 %shard_map.207 = (bf16[512,512]{1,0:T(8,128)(2,1)}, bf16[64,512]{1,0:T(8,128)(2,1)}, bf16[64,512]{1,0:T(8,128)(2,1)}, bf16[64,192,128]{2,1,0:T(8,128)(2,1)}, bf1...) custom-call(bf16[8,512,512]{2,1,0:T(8,128)(2,1)} %get-tuple-element.37.refs_0_, ...), custom_call_target="tpu_custom_call" | custom-call | tf_op jit(solution)/shard_map/pallas_call | solution.py:603
  243.1 14.2 %shard_map.208 = (bf16[512,512]{1,0:T(8,128)(2,1)}, bf16[64,512]{1,0:T(8,128)(2,1)}, bf16[64,192,128]{2,1,0:T(8,128)(2,1)}, bf16[64,192,128]{2,1,0:T(8,128)(2,1)...) custom-call(bf16[512,512]{1,0:T(8,128)(2,1)} %get-tuple-element.47.r, ...), custom_call_target="tpu_custom_call" | custom-call | tf_op jit(solution)/shard_map/pallas_call | solution.py:640

commit v9 on v8

--- a/solution.py
+++ b/solution.py
@@ -10,7 +10,7 @@
 F32 = jnp.float32
 BF16 = jnp.bfloat16
 CAP = 64
-GROUP = 4
+GROUP = 8
 LANES = 256
 CORES = 2
 CHIPS = 2
@@ -197,10 +197,6 @@
         add_up(0).start()
         pltpu.make_async_copy(us_ref, uall_ref, out_sem.at[0]).start()
 
-    @at_step(n_group + 1)
-    def _():
-        add_up(2).start()
-
     @at_step(n_group + n_group // 2)
     def _():
         pass_on(spread_d, 1, (5,))
@@ -228,6 +224,12 @@
         for exp in range(GROUP):
             x_ref[exp, at, :] = rows[exp * CAP:(exp + 1) * CAP]
             row_ref[exp, at, :] = jnp.broadcast_to(gate[exp * CAP:(exp + 1) * CAP], (CAP, 128))
+
+    @at_step(n_group)
+    def _():
+        add_up(0).wait_recv()
+        p_ref[ic * 2 + 1 - iy] += rs_ref[0]
+        add_up(2).start()
 
     ff = wg_ref.shape[1]
     pre = {}
@@ -258,11 +260,6 @@
         total += matmul(pick, part_ref[core, 1], 0, 0) + matmul(pick, part_ref[core, 2], 0, 0)
         p_ref[core * 2 + y_now] += total
 
-    @at_step(n_group)
-    def _():
-        add_up(0).wait_recv()
-        p_ref[ic * 2 + 1 - iy] += rs_ref[0]
-
     @at_step(2 * n_group - 1)
     def _():
         add_up(1).start()
@@ -282,19 +279,21 @@
 
 def layer_kernel(last_layer, *refs):
     refs = list(refs)
-    whole_ref, mine_ref, rank_ref, gate_ref, x_own_ref, grad_own_ref, dense_ref, wg_ref, wu_ref, wd_ref = refs[:10]
+    whole_ref, mine_ref, rank_ref, gate_ref, x_own_ref, dense_ref, wg_ref, wu_ref, wd_ref, other_ref = refs[:10]
     del refs[:10]
+    grad_own_ref = mine_ref if last_layer else other_ref
     if last_layer:
-        other_ref = refs.pop(0)
         one_ref, two_ref = refs[1:3]
         del refs[1:3]
     else:
         part_ref = refs.pop(1)
     gx_out_ref, gg_ref, gu_ref, gd_ref = refs[:4]
     (peer_ref, xo_ref, do_ref, h_ref, ga_ref, gb_ref, pick_ref, gx_ref, p_ref, rs_ref, x_ref, d_ref, stage_ref,
-     ag_send, ag_recv, rs_send, rs_recv, keep_sem, give_send, give_recv) = refs[4:24]
+     ag_send, ag_recv, rs_send, rs_recv, keep_sem, give_send, give_recv, late_sem) = refs[4:25]
+    late_copies = [pltpu.make_async_copy(src, pick_ref.at[at], late_sem.at[at]) for at, src in enumerate((x_own_ref, dense_ref))]
     if last_layer:
-        part_ref, land_ref, land_send, land_recv = refs[24:]
+        part_ref = gx_ref.at[0]
+        land_ref, land_send, land_recv = refs[25:]
     n_src, _, dim = whole_ref.shape
     own = n_src // CHIPS
     n_group = xo_ref.shape[0] // GROUP
@@ -384,7 +383,7 @@
         p_ref[...] = jnp.zeros_like(p_ref)
         spread(3).wait_recv()
 
-    @at_step(n_group - 2)
+    @at_step(n_group - 1)
     def _():
         spread(0).wait_recv()
         spread(4).start()
@@ -445,21 +444,8 @@
         add_up(1).start()
         spread(5).wait_recv()
         spread(6).wait_recv()
-        add_up(0).wait_recv()
-        p_ref[ic * 2 + 1 - iy] += rs_ref[0]
-        add_up(2).start()
-
-    @at_step(n_step - 1)
-    def _():
-        add_up(1).wait_recv()
-        add_up(2).wait_recv()
-        total = p_ref[ic * 2 + iy] + rs_ref[1] + rs_ref[2]
-        grad = (grad_own_ref[...].astype(F32) + total).astype(BF16)
-        part_ref[...] = matmul(x_own_ref[...], grad, 0, 0).astype(BF16)
-        gx_out_ref[...] = (grad.astype(F32) + matmul(grad, dense_ref[...], 1, 1)).astype(BF16)
-        if last_layer:
-            for hop in range(1, 8):
-                land_copy(0, hop).start()
+        for copy in late_copies:
+            copy.start()
 
     @pl.when(step >= n_first)
     def _():
@@ -475,6 +461,26 @@
 
         for src in range(own):
             pull((1 - ix) * own + src, group, src, False)
+
+        @at_step(n_first)
+        def _():
+            add_up(0).wait_recv()
+            p_ref[ic * 2 + 1 - iy] += rs_ref[0]
+            add_up(2).start()
+
+        @at_step(n_step - 1)
+        def _():
+            for copy in late_copies:
+                copy.wait()
+            add_up(1).wait_recv()
+            add_up(2).wait_recv()
+            total = p_ref[ic * 2 + iy] + rs_ref[1] + rs_ref[2]
+            grad = (grad_own_ref[...].astype(F32) + total).astype(BF16)
+            part_ref[...] = matmul(pick_ref[0], grad, 0, 0).astype(BF16)
+            gx_out_ref[...] = (grad.astype(F32) + matmul(grad, pick_ref[1], 1, 1)).astype(BF16)
+            if last_layer:
+                for hop in range(1, 8):
+                    land_copy(0, hop).start()
 
         buf = lax.rem(group, 2)
 
@@ -569,7 +575,7 @@
     )(tokens, grad, idx1, idx2, top1, top2, dense1, dense2, w_gate, w_up, w_down)
 
 
-def layer_backward(whole, mine, rank, gate, x_own, grad_own, dense, w_gate, w_up, w_down, other=None):
+def layer_backward(last_layer, whole, mine, rank, gate, x_own, dense, w_gate, w_up, w_down, other):
     n_src, n_tok, dim = whole.shape
     n_all, ff, _ = w_gate.shape
     n_exp = rank.shape[1]
@@ -577,7 +583,6 @@
     piece = dim // (CHIPS * CORES)
     groups = n_exp // GROUP
     kept = own * CAP
-    last_layer = other is not None
     tall = weight_spec(groups, ff, dim)
     table = fixed(n_src, n_exp, n_tok)
     block = fixed(n_tok, dim)
@@ -596,22 +601,21 @@
     scratch += sums_scratch(own, n_tok, dim)
     scratch += [pltpu.VMEM((GROUP, kept, dim), BF16), pltpu.VMEM((GROUP, kept, dim), BF16),
                 pltpu.VMEM((2, CORES, 3, GROUP, ff, piece), BF16),
-                dma_sems(7), dma_sems(7), dma_sems(3), dma_sems(3), dma_sems(2, 3), dma_sems(2, 3), dma_sems(groups, 3)]
+                dma_sems(7), dma_sems(7), dma_sems(3), dma_sems(3), dma_sems(2, 3), dma_sems(2, 3), dma_sems(groups, 3), dma_sems(2)]
     if last_layer:
-        scratch += [pltpu.VMEM((dim, dim), BF16), pltpu.VMEM((2, 8, dim // 8, dim), BF16), dma_sems(2, 8), dma_sems(2, 8)]
-    operands = (whole, mine, rank, gate, x_own, grad_own, dense, w_gate, w_up, w_down) + ((other,) if last_layer else ())
+        scratch += [pltpu.VMEM((2, 8, dim // 8, dim), BF16), dma_sems(2, 8), dma_sems(2, 8)]
+    anywhere = pl.BlockSpec(memory_space=pl.ANY)
     return pl.pallas_call(
         functools.partial(layer_kernel, last_layer),
         out_shape=(jax.ShapeDtypeStruct((n_tok, dim), BF16),) + extra_shapes + (grad_shape,) * 3,
         grid_spec=pltpu.PrefetchScalarGridSpec(
             num_scalar_prefetch=0, grid=(3 * groups,),
-            in_specs=[fixed(n_src, n_tok, dim), block, table, table, block, block, square, tall, tall, tall]
-            + ([square] if last_layer else []),
-            out_specs=(block,) + extra_specs + (pl.BlockSpec(memory_space=pl.ANY),) * 3,
+            in_specs=[fixed(n_src, n_tok, dim), block, table, table, anywhere, anywhere, tall, tall, tall, square],
+            out_specs=(block,) + extra_specs + (anywhere,) * 3,
             scratch_shapes=scratch),
         compiler_params=pltpu.CompilerParams(dimension_semantics=('arbitrary',), vmem_limit_bytes=67043328,
                                              collective_id=1 + int(last_layer), has_side_effects=True),
-    )(*operands)
+    )(whole, mine, rank, gate, x_own, dense, w_gate, w_up, w_down, other)
 
 
 def settle_kernel(chunks, *refs):
@@ -658,9 +662,9 @@
         y_one, u_two, u_all, dy_all, rank1, gate1, rank2, gate2 = layer_forward(
             tokens, dy_out, route_idx1.T, route_idx2.T, route_gate1.T, route_gate2.T, dense_w1, dense_w2, w_gate1, w_up1, w_down1)
         grad_mid, part_two, *grads_two = layer_backward(
-            dy_all, u_two, rank2, gate2, y_one, dy_out, dense_w2, w_gate2, w_up2, w_down2)
+            False, dy_all, u_two, rank2, gate2, y_one, dense_w2, w_gate2, w_up2, w_down2, dy_out)
         grad_tok, dense_one, dense_two, *grads_one = layer_backward(
-            u_all, grad_mid, rank1, gate1, tokens, grad_mid, dense_w1, w_gate1, w_up1, w_down1, part_two)
+            True, u_all, grad_mid, rank1, gate1, tokens, dense_w1, w_gate1, w_up1, w_down1, part_two)
         (grad_tok, dense_one, gate_one, up_one, down_one, dense_two, gate_two, up_two, down_two) = settle(
             grad_tok, dense_one, *grads_one, dense_two, *grads_two)
         gate_one, up_one, gate_two, up_two = (jnp.swapaxes(g, 1, 2) for g in (gate_one, up_one, gate_two, up_two))

time: 258 us -> 252 us (0.977)
  Pallas kernels: 257 us -> 251 us
    pallas_call x2, Pallas kernels: 166 us -> 162 us  [layer_backward(): pl.pallas_call(functools.partial(layer_kernel, last_layer), out_shape=(ja...]
where the time goes in v9:
time: 252 us; the launch traced here: 251 us
  Pallas kernels  251 us (100%)
    pallas_call x2, Pallas kernels, layer_backward(): pl.pallas_call(functools.partial(layer_kernel, last_layer), out_shape=(ja...  162 us
    pallas_call x1, Pallas kernels, layer_forward(): pl.pallas_call(forward_kernel, out_shape=(block, block, every, every, ran...  74.7 us
    pallas_call x1, Pallas kernels, settle(): pl.pallas_call(functools.partial(settle_kernel, chunks), out_shape=tuple(...  14.2 us

profile of v9, /device:TPU:0, one launch (start us, length us, event | category | flops | bytes accessed | tf_op | source)
XLA Modules:
  0.0 251.5 jit_solution(3658264530342183248)
XLA Ops:
  0.6 74.7 %shard_map.205 = (bf16[512,512]{1,0:T(8,128)(2,1)}, bf16[512,512]{1,0:T(8,128)(2,1)}, bf16[8,512,512]{2,1,0:T(8,128)(2,1)}, bf16[8,512,512]{2,1,0:T(8,128)(2,1)}...) custom-call(bf16[512,512]{1,0:T(8,128)(2,1)} %refs_4_.1, ...), custom_call_target="tpu_custom_call" | custom-call | tf_op jit(solution)/shard_map/pallas_call | solution.py:560
  75.3 79.7 %shard_map.206 = (bf16[512,512]{1,0:T(8,128)(2,1)}, bf16[512,512]{1,0:T(8,128)(2,1)}, bf16[64,192,128]{2,1,0:T(8,128)(2,1)}, bf16[64,192,128]{2,1,0:T(8,128)(2,1)}, bf16[64,192,128]{2,1,0:T(8,128)(2,1)}) custom-call(bf16[8,512,512]{2,1,0:T(8,128)(2,1)} %get-tuple-element.38.refs_0_, bf16[512,512]{1,0:T(8,128)(2,1)} %get-tuple-element.39.refs_1_, ...), custom_call_target="tpu_custom_call" | custom-call | tf_op jit(solution)/shard_map/pallas_call | solution.py:608
  155.1 82.0 %shard_map.207 = (bf16[512,512]{1,0:T(8,128)(2,1)}, bf16[64,512]{1,0:T(8,128)(2,1)}, bf16[64,512]{1,0:T(8,128)(2,1)}, bf16[64,192,128]{2,1,0:T(8,128)(2,1)}, bf1...) custom-call(bf16[8,512,512]{2,1,0:T(8,128)(2,1)} %get-tuple-element.37.refs_0_, ...), custom_call_target="tpu_custom_call" | custom-call | tf_op jit(solution)/shard_map/pallas_call | solution.py:608
  237.0 14.2 %shard_map.208 = (bf16[512,512]{1,0:T(8,128)(2,1)}, bf16[64,512]{1,0:T(8,128)(2,1)}, bf16[64,192,128]{2,1,0:T(8,128)(2,1)}, bf16[64,192,128]{2,1,0:T(8,128)(2,1)...) custom-call(bf16[512,512]{1,0:T(8,128)(2,1)} %get-tuple-element.47.r, ...), custom_call_target="tpu_custom_call" | custom-call | tf_op jit(solution)/shard_map/pallas_call | solution.py:644

commit v10 on v9

--- a/solution.py
+++ b/solution.py
@@ -74,6 +74,24 @@
 def target(hop):
     goal = lax.rem(rank_of(*position()) + hop, 8)
     return {'x': lax.div(goal, 4), 'c': lax.rem(lax.div(goal, 2), 2), 'y': lax.rem(goal, 2)}
+
+
+def weight_copies(sources, w_ref, sems, step, n_group):
+    slot = lax.rem(step, 2)
+    rows = pl.ds((lax.axis_index('c') * n_group + lax.rem(step, n_group)) * GROUP, GROUP)
+    return [pltpu.make_async_copy(src.at[rows], w_ref.at[slot, kind], sems.at[slot, kind]) for kind, src in enumerate(sources)]
+
+
+def next_weights(sources, w_ref, sems, n_group, n_step):
+    step = pl.program_id(0)
+
+    @pl.when(step + 1 < n_step)
+    def _():
+        for copy in weight_copies(sources, w_ref, sems, step + 1, n_group):
+            copy.start()
+
+    for copy in weight_copies(sources, w_ref, sems, step, n_group):
+        copy.wait()
 
 
 def at_step(number):
@@ -112,10 +130,10 @@
     gate_ref[src] = gates
 
 
-def forward_kernel(tok_ref, grad_ref, idx1_ref, idx2_ref, top1_ref, top2_ref, mix_ref, dense_ref, wg_ref, wu_ref, wd_ref,
+def forward_kernel(tok_ref, grad_ref, idx1_ref, idx2_ref, top1_ref, top2_ref, mix_ref, dense_ref, wg_hbm, wu_hbm, wd_hbm,
                    y_ref, u_ref, uall_ref, dall_ref, rank1_ref, gate1_ref, rank2_ref, gate2_ref,
                    raw_ref, us_ref, ds_ref, routes_ref, route_ref, before_ref, pick_ref, row_ref, x_ref, part_ref, p_ref, rs_ref,
-                   u_send, u_recv, d_send, d_recv, t_send, t_recv, rs_send, rs_recv, out_sem):
+                   w_ref, w_sem, u_send, u_recv, d_send, d_recv, t_send, t_recv, rs_send, rs_recv, out_sem):
     n_exp, n_tok = rank1_ref.shape[1:]
     n_group = n_exp // GROUP
     step = pl.program_id(0)
@@ -126,6 +144,8 @@
     spread_t = spreader(routes_ref, route_ref, (t_send, t_recv))
     add_up = adder(p_ref, rs_ref, (rs_send, rs_recv))
     stores = ((us_ref, uall_ref), (ds_ref, dall_ref))
+    weights = (wg_hbm, wu_hbm, wd_hbm)
+    wg_ref, wu_ref, wd_ref = (w_ref.at[lax.rem(step, 2), kind] for kind in range(3))
 
     def mixed(x):
         return (x.astype(F32) + matmul(x, mix_ref[...])).astype(BF16)
@@ -137,6 +157,8 @@
 
     @at_step(0)
     def _():
+        for copy in weight_copies(weights, w_ref, w_sem, 0, n_group):
+            copy.start()
         for at, part_in in enumerate((idx1_ref, idx2_ref, top1_ref, top2_ref)):
             routes_ref[at * 8:at * 8 + 8, :] = part_in[...].astype(F32)
         greet(False)
@@ -211,6 +233,7 @@
             spread_d(at).wait_recv()
         pltpu.make_async_copy(ds_ref, dall_ref, out_sem.at[1]).start()
 
+    next_weights(weights, w_ref, w_sem, n_group, 2 * n_group)
     group = lax.rem(step, n_group)
     far = 1 - lax.div(step, n_group)
     y_now = jnp.where(far == 1, 1 - iy, iy)
@@ -279,7 +302,7 @@
 
 def layer_kernel(last_layer, *refs):
     refs = list(refs)
-    whole_ref, mine_ref, rank_ref, gate_ref, x_own_ref, dense_ref, wg_ref, wu_ref, wd_ref, other_ref = refs[:10]
+    whole_hbm, mine_ref, rank_hbm, gate_hbm, x_own_ref, dense_ref, *weights, other_ref = refs[:10]
     del refs[:10]
     grad_own_ref = mine_ref if last_layer else other_ref
     if last_layer:
@@ -289,11 +312,12 @@
         part_ref = refs.pop(1)
     gx_out_ref, gg_ref, gu_ref, gd_ref = refs[:4]
     (peer_ref, xo_ref, do_ref, h_ref, ga_ref, gb_ref, pick_ref, gx_ref, p_ref, rs_ref, x_ref, d_ref, stage_ref,
-     ag_send, ag_recv, rs_send, rs_recv, keep_sem, give_send, give_recv, late_sem) = refs[4:25]
+     ag_send, ag_recv, rs_send, rs_recv, keep_sem, give_send, give_recv, late_sem,
+     whole_ref, rank_ref, gate_ref, w_ref, w_sem, load_sem) = refs[4:31]
     late_copies = [pltpu.make_async_copy(src, pick_ref.at[at], late_sem.at[at]) for at, src in enumerate((x_own_ref, dense_ref))]
     if last_layer:
         part_ref = gx_ref.at[0]
-        land_ref, land_send, land_recv = refs[25:]
+        land_ref, land_send, land_recv = refs[31:]
     n_src, _, dim = whole_ref.shape
     own = n_src // CHIPS
     n_group = xo_ref.shape[0] // GROUP
@@ -304,6 +328,9 @@
     step = pl.program_id(0)
     ix, ic, iy = position()
     cols = pl.ds(pl.multiple_of(ix * half, half), half)
+    wg_ref, wu_ref, wd_ref = (w_ref.at[lax.rem(step, 2), kind] for kind in range(3))
+    loads = [pltpu.make_async_copy(src, dst, load_sem.at[at]) for at, (src, dst) in enumerate(
+        ((rank_hbm, rank_ref), (gate_hbm, gate_ref), (whole_hbm, whole_ref)))]
     u_ref, dy_ref = (whole_ref, peer_ref) if last_layer else (peer_ref, whole_ref)
     outs = (gg_ref, gu_ref, gd_ref)
     spread = spreader(mine_ref, peer_ref, (ag_send, ag_recv))
@@ -373,6 +400,8 @@
 
     @at_step(0)
     def _():
+        for copy in loads + weight_copies(weights, w_ref, w_sem, 0, n_group):
+            copy.start()
         greet(last_layer)
         for at in (0, 3, 1):
             spread(at).start()
@@ -381,7 +410,11 @@
                 land_copy(1, hop).start()
         peer_ref[rank_of(ix, ic, iy)] = mine_ref[...]
         p_ref[...] = jnp.zeros_like(p_ref)
+        for copy in loads:
+            copy.wait()
         spread(3).wait_recv()
+
+    next_weights(weights, w_ref, w_sem, n_group, n_step)
 
     @at_step(n_group - 1)
     def _():
@@ -529,10 +562,6 @@
     return pl.BlockSpec(shape, lambda s: (0,) * len(shape), pipeline_mode=pl.Buffered(1))
 
 
-def weight_spec(groups, ff, dim):
-    return pl.BlockSpec((GROUP, ff, dim), lambda s: (lax.axis_index('c') * groups + lax.rem(s, groups), 0, 0))
-
-
 def dma_sems(*shape):
     return pltpu.SemaphoreType.DMA(shape)
 
@@ -549,7 +578,6 @@
     n_src = 8
     own = n_src // CHIPS
     groups = n_exp // GROUP
-    tall = weight_spec(groups, ff, dim)
     table = fixed(n_src, n_exp, n_tok)
     block = jax.ShapeDtypeStruct((n_tok, dim), BF16)
     every = jax.ShapeDtypeStruct((n_src, n_tok, dim), BF16)
@@ -562,13 +590,14 @@
         out_shape=(block, block, every, every, ranks, gates, ranks, gates),
         grid_spec=pltpu.PrefetchScalarGridSpec(
             num_scalar_prefetch=0, grid=(2 * groups,),
-            in_specs=[fixed(n_tok, dim)] * 2 + [fixed(top, n_tok)] * 4 + [fixed(dim, dim)] * 2 + [tall] * 3,
+            in_specs=[fixed(n_tok, dim)] * 2 + [fixed(top, n_tok)] * 4 + [fixed(dim, dim)] * 2 + [anywhere] * 3,
             out_specs=(fixed(n_tok, dim), fixed(n_tok, dim), anywhere, anywhere, table, table, table, table),
             scratch_shapes=[pltpu.VMEM((n_src, n_tok, dim), BF16)] * 3
             + [pltpu.VMEM((4 * top, n_tok), F32), pltpu.VMEM((n_src, 4 * top, n_tok), F32), pltpu.VMEM((n_tok, n_tok), BF16),
                             pltpu.VMEM((CORES, GROUP * CAP, n_tok), BF16), pltpu.VMEM((GROUP, rows, 128), F32),
                             pltpu.VMEM((GROUP, rows, dim), BF16), pltpu.VMEM((CORES, 3, GROUP * CAP, dim), BF16)]
             + sums_scratch(own, n_tok, dim)
+            + [pltpu.VMEM((2, 3, GROUP, ff, dim), BF16), dma_sems(2, 3)]
             + [dma_sems(7)] * 6 + [dma_sems(3)] * 2 + [dma_sems(2)]),
         compiler_params=pltpu.CompilerParams(dimension_semantics=('arbitrary',), vmem_limit_bytes=62 << 20,
                                              collective_id=0, has_side_effects=True),
@@ -583,8 +612,6 @@
     piece = dim // (CHIPS * CORES)
     groups = n_exp // GROUP
     kept = own * CAP
-    tall = weight_spec(groups, ff, dim)
-    table = fixed(n_src, n_exp, n_tok)
     block = fixed(n_tok, dim)
     square = fixed(dim, dim)
     slab = fixed(dim // 8, dim)
@@ -601,7 +628,9 @@
     scratch += sums_scratch(own, n_tok, dim)
     scratch += [pltpu.VMEM((GROUP, kept, dim), BF16), pltpu.VMEM((GROUP, kept, dim), BF16),
                 pltpu.VMEM((2, CORES, 3, GROUP, ff, piece), BF16),
-                dma_sems(7), dma_sems(7), dma_sems(3), dma_sems(3), dma_sems(2, 3), dma_sems(2, 3), dma_sems(groups, 3), dma_sems(2)]
+                dma_sems(7), dma_sems(7), dma_sems(3), dma_sems(3), dma_sems(2, 3), dma_sems(2, 3), dma_sems(groups, 3), dma_sems(2),
+                pltpu.VMEM((n_src, n_tok, dim), BF16), pltpu.VMEM(rank.shape, rank.dtype), pltpu.VMEM(gate.shape, gate.dtype),
+                pltpu.VMEM((2, 3, GROUP, ff, dim), BF16), dma_sems(2, 3), dma_sems(3)]
     if last_layer:
         scratch += [pltpu.VMEM((2, 8, dim // 8, dim), BF16), dma_sems(2, 8), dma_sems(2, 8)]
     anywhere = pl.BlockSpec(memory_space=pl.ANY)
@@ -610,7 +639,7 @@
         out_shape=(jax.ShapeDtypeStruct((n_tok, dim), BF16),) + extra_shapes + (grad_shape,) * 3,
         grid_spec=pltpu.PrefetchScalarGridSpec(
             num_scalar_prefetch=0, grid=(3 * groups,),
-            in_specs=[fixed(n_src, n_tok, dim), block, table, table, anywhere, anywhere, tall, tall, tall, square],
+            in_specs=[anywhere, block] + [anywhere] * 7 + [square],
             out_specs=(block,) + extra_specs + (anywhere,) * 3,
             scratch_shapes=scratch),
         compiler_params=pltpu.CompilerParams(dimension_semantics=('arbitrary',), vmem_limit_bytes=67043328,

time: 252 us -> 245 us (0.972)
  Pallas kernels: 251 us -> 244 us
    pallas_call x2, Pallas kernels: 162 us -> 157 us  [layer_backward(): pl.pallas_call(functools.partial(layer_kernel, last_layer), out_shape=(ja...]
where the time goes in v10:
time: 245 us
  Pallas kernels  244 us (100%)
    pallas_call x2, Pallas kernels, layer_backward(): pl.pallas_call(functools.partial(layer_kernel, last_layer), out_shape=(ja...  157 us
    pallas_call x1, Pallas kernels, layer_forward(): pl.pallas_call(forward_kernel, out_shape=(block, block, every, every, ran...  73.3 us
    pallas_call x1, Pallas kernels, settle(): pl.pallas_call(functools.partial(settle_kernel, chunks), out_shape=tuple(...  14.2 us

profile of v10, /device:TPU:0, one launch (start us, length us, event | category | flops | bytes accessed | tf_op | source)
XLA Modules:
  0.0 245.2 jit_solution(8595166269581598826)
XLA Ops:
  0.6 73.3 %shard_map.205 = (bf16[512,512]{1,0:T(8,128)(2,1)}, bf16[512,512]{1,0:T(8,128)(2,1)}, bf16[8,512,512]{2,1,0:T(8,128)(2,1)}, bf16[8,512,512]{2,1,0:T(8,128)(2,1)}...) custom-call(bf16[512,512]{1,0:T(8,128)(2,1)} %refs_4_.1, ...), custom_call_target="tpu_custom_call" | custom-call | tf_op jit(solution)/shard_map/pallas_call | solution.py:588
  73.9 78.0 %shard_map.206 = (bf16[512,512]{1,0:T(8,128)(2,1)}, bf16[512,512]{1,0:T(8,128)(2,1)}, bf16[64,192,128]{2,1,0:T(8,128)(2,1)}, bf16[64,192,128]{2,1,0:T(8,128)(2,1)}, bf16[64,192,128]{2,1,0:T(8,128)(2,1)}) custom-call(bf16[8,512,512]{2,1,0:T(8,128)(2,1)} %get-tuple-element.38.refs_0_, bf16[512,512]{1,0:T(8,128)(2,1)} %get-tuple-element.39.refs_1_, ...), custom_call_target="tpu_custom_call" | custom-call | tf_op jit(solution)/shard_map/pallas_call | solution.py:637
  151.9 78.8 %shard_map.207 = (bf16[512,512]{1,0:T(8,128)(2,1)}, bf16[64,512]{1,0:T(8,128)(2,1)}, bf16[64,512]{1,0:T(8,128)(2,1)}, bf16[64,192,128]{2,1,0:T(8,128)(2,1)}, bf1...) custom-call(bf16[8,512,512]{2,1,0:T(8,128)(2,1)} %get-tuple-element.37.refs_0_, ...), custom_call_target="tpu_custom_call" | custom-call | tf_op jit(solution)/shard_map/pallas_call | solution.py:637
  230.7 14.2 %shard_map.208 = (bf16[512,512]{1,0:T(8,128)(2,1)}, bf16[64,512]{1,0:T(8,128)(2,1)}, bf16[64,192,128]{2,1,0:T(8,128)(2,1)}, bf16[64,192,128]{2,1,0:T(8,128)(2,1)...) custom-call(bf16[512,512]{1,0:T(8,128)(2,1)} %get-tuple-element.47.r, ...), custom_call_target="tpu_custom_call" | custom-call | tf_op jit(solution)/shard_map/pallas_call | solution.py:673

commit v11 on v10

--- a/solution.py
+++ b/solution.py
@@ -199,7 +199,7 @@
         pass_on(spread_u, 2, (6,))
         pass_on(spread_d, 0, (4, 2))
 
-    @at_step(n_group - 1)
+    @at_step(n_group + 1)
     def _():
         for copy in (spread_t, spread_u):
             copy(5).wait_recv()
@@ -217,15 +217,15 @@
     @at_step(n_group)
     def _():
         add_up(0).start()
+
+    @at_step(n_group + n_group // 2)
+    def _():
+        pass_on(spread_d, 1, (5,))
+
+    @at_step(2 * n_group - 2)
+    def _():
+        pass_on(spread_d, 2, (6,))
         pltpu.make_async_copy(us_ref, uall_ref, out_sem.at[0]).start()
-
-    @at_step(n_group + n_group // 2)
-    def _():
-        pass_on(spread_d, 1, (5,))
-
-    @at_step(2 * n_group - 2)
-    def _():
-        pass_on(spread_d, 2, (6,))
 
     @at_step(2 * n_group - 1)
     def _():

time: 245 us -> 242 us (0.988)
  Pallas kernels: 244 us -> 241 us
    pallas_call x1, Pallas kernels: 73.3 us -> 69.8 us  [layer_forward(): pl.pallas_call(forward_kernel, out_shape=(block, block, every, every, ran...]
where the time goes in v11:
time: 242 us
  Pallas kernels  241 us (100%)
    pallas_call x2, Pallas kernels, layer_backward(): pl.pallas_call(functools.partial(layer_kernel, last_layer), out_shape=(ja...  157 us
    pallas_call x1, Pallas kernels, layer_forward(): pl.pallas_call(forward_kernel, out_shape=(block, block, every, every, ran...  69.8 us
    pallas_call x1, Pallas kernels, settle(): pl.pallas_call(functools.partial(settle_kernel, chunks), out_shape=tuple(...  14.2 us

profile of v11, /device:TPU:0, one launch (start us, length us, event | category | flops | bytes accessed | tf_op | source)
XLA Modules:
  0.0 241.6 jit_solution(4972122620232508267)
XLA Ops:
  0.6 69.8 %shard_map.205 = (bf16[512,512]{1,0:T(8,128)(2,1)}, bf16[512,512]{1,0:T(8,128)(2,1)}, bf16[8,512,512]{2,1,0:T(8,128)(2,1)}, bf16[8,512,512]{2,1,0:T(8,128)(2,1)}...) custom-call(bf16[512,512]{1,0:T(8,128)(2,1)} %refs_4_.1, ...), custom_call_target="tpu_custom_call" | custom-call | tf_op jit(solution)/shard_map/pallas_call | solution.py:588
  70.4 78.0 %shard_map.206 = (bf16[512,512]{1,0:T(8,128)(2,1)}, bf16[512,512]{1,0:T(8,128)(2,1)}, bf16[64,192,128]{2,1,0:T(8,128)(2,1)}, bf16[64,192,128]{2,1,0:T(8,128)(2,1)}, bf16[64,192,128]{2,1,0:T(8,128)(2,1)}) custom-call(bf16[8,512,512]{2,1,0:T(8,128)(2,1)} %get-tuple-element.38.refs_0_, bf16[512,512]{1,0:T(8,128)(2,1)} %get-tuple-element.39.refs_1_, ...), custom_call_target="tpu_custom_call" | custom-call | tf_op jit(solution)/shard_map/pallas_call | solution.py:637
  148.4 78.8 %shard_map.207 = (bf16[512,512]{1,0:T(8,128)(2,1)}, bf16[64,512]{1,0:T(8,128)(2,1)}, bf16[64,512]{1,0:T(8,128)(2,1)}, bf16[64,192,128]{2,1,0:T(8,128)(2,1)}, bf1...) custom-call(bf16[8,512,512]{2,1,0:T(8,128)(2,1)} %get-tuple-element.37.refs_0_, ...), custom_call_target="tpu_custom_call" | custom-call | tf_op jit(solution)/shard_map/pallas_call | solution.py:637
  227.2 14.2 %shard_map.208 = (bf16[512,512]{1,0:T(8,128)(2,1)}, bf16[64,512]{1,0:T(8,128)(2,1)}, bf16[64,192,128]{2,1,0:T(8,128)(2,1)}, bf16[64,192,128]{2,1,0:T(8,128)(2,1)...) custom-call(bf16[512,512]{1,0:T(8,128)(2,1)} %get-tuple-element.47.r, ...), custom_call_target="tpu_custom_call" | custom-call | tf_op jit(solution)/shard_map/pallas_call | solution.py:673

commit v12 on v11

--- a/solution.py
+++ b/solution.py
@@ -330,7 +330,9 @@
     cols = pl.ds(pl.multiple_of(ix * half, half), half)
     wg_ref, wu_ref, wd_ref = (w_ref.at[lax.rem(step, 2), kind] for kind in range(3))
     loads = [pltpu.make_async_copy(src, dst, load_sem.at[at]) for at, (src, dst) in enumerate(
-        ((rank_hbm, rank_ref), (gate_hbm, gate_ref), (whole_hbm, whole_ref)))]
+        ((rank_hbm, rank_ref), (gate_hbm, gate_ref), (whole_hbm.at[pl.ds(ix * own, own)], whole_ref.at[pl.ds(ix * own, own)])))]
+    far_rows = pl.ds((1 - ix) * own, own)
+    far_load = pltpu.make_async_copy(whole_hbm.at[far_rows], whole_ref.at[far_rows], load_sem.at[3])
     u_ref, dy_ref = (whole_ref, peer_ref) if last_layer else (peer_ref, whole_ref)
     outs = (gg_ref, gu_ref, gd_ref)
     spread = spreader(mine_ref, peer_ref, (ag_send, ag_recv))
@@ -400,7 +402,7 @@
 
     @at_step(0)
     def _():
-        for copy in loads + weight_copies(weights, w_ref, w_sem, 0, n_group):
+        for copy in loads + weight_copies(weights, w_ref, w_sem, 0, n_group) + [far_load]:
             copy.start()
         greet(last_layer)
         for at in (0, 3, 1):
@@ -475,6 +477,7 @@
     def _():
         add_up(0).start()
         add_up(1).start()
+        far_load.wait()
         spread(5).wait_recv()
         spread(6).wait_recv()
         for copy in late_copies:
@@ -630,7 +633,7 @@
                 pltpu.VMEM((2, CORES, 3, GROUP, ff, piece), BF16),
                 dma_sems(7), dma_sems(7), dma_sems(3), dma_sems(3), dma_sems(2, 3), dma_sems(2, 3), dma_sems(groups, 3), dma_sems(2),
                 pltpu.VMEM((n_src, n_tok, dim), BF16), pltpu.VMEM(rank.shape, rank.dtype), pltpu.VMEM(gate.shape, gate.dtype),
-                pltpu.VMEM((2, 3, GROUP, ff, dim), BF16), dma_sems(2, 3), dma_sems(3)]
+                pltpu.VMEM((2, 3, GROUP, ff, dim), BF16), dma_sems(2, 3), dma_sems(4)]
     if last_layer:
         scratch += [pltpu.VMEM((2, 8, dim // 8, dim), BF16), dma_sems(2, 8), dma_sems(2, 8)]
     anywhere = pl.BlockSpec(memory_space=pl.ANY)

time: 242 us -> 241 us (level)
  no operation moved by 1% of the time
where the time goes in v12:
time: 241 us
  Pallas kernels  240 us (100%)
    pallas_call x2, Pallas kernels, layer_backward(): pl.pallas_call(functools.partial(layer_kernel, last_layer), out_shape=(ja...  156 us
    pallas_call x1, Pallas kernels, layer_forward(): pl.pallas_call(forward_kernel, out_shape=(block, block, every, every, ran...  69.8 us
    pallas_call x1, Pallas kernels, settle(): pl.pallas_call(functools.partial(settle_kernel, chunks), out_shape=tuple(...  14.2 us

profile of v12, /device:TPU:0, one launch (start us, length us, event | category | flops | bytes accessed | tf_op | source)
XLA Modules:
  0.0 240.5 jit_solution(3934990101365269950)
XLA Ops:
  0.6 69.8 %shard_map.205 = (bf16[512,512]{1,0:T(8,128)(2,1)}, bf16[512,512]{1,0:T(8,128)(2,1)}, bf16[8,512,512]{2,1,0:T(8,128)(2,1)}, bf16[8,512,512]{2,1,0:T(8,128)(2,1)}...) custom-call(bf16[512,512]{1,0:T(8,128)(2,1)} %refs_4_.1, ...), custom_call_target="tpu_custom_call" | custom-call | tf_op jit(solution)/shard_map/pallas_call | solution.py:591
  70.4 77.4 %shard_map.206 = (bf16[512,512]{1,0:T(8,128)(2,1)}, bf16[512,512]{1,0:T(8,128)(2,1)}, bf16[64,192,128]{2,1,0:T(8,128)(2,1)}, bf16[64,192,128]{2,1,0:T(8,128)(2,1)}, bf16[64,192,128]{2,1,0:T(8,128)(2,1)}) custom-call(bf16[8,512,512]{2,1,0:T(8,128)(2,1)} %get-tuple-element.38.refs_0_, bf16[512,512]{1,0:T(8,128)(2,1)} %get-tuple-element.39.refs_1_, ...), custom_call_target="tpu_custom_call" | custom-call | tf_op jit(solution)/shard_map/pallas_call | solution.py:640
  147.8 78.3 %shard_map.207 = (bf16[512,512]{1,0:T(8,128)(2,1)}, bf16[64,512]{1,0:T(8,128)(2,1)}, bf16[64,512]{1,0:T(8,128)(2,1)}, bf16[64,192,128]{2,1,0:T(8,128)(2,1)}, bf1...) custom-call(bf16[8,512,512]{2,1,0:T(8,128)(2,1)} %get-tuple-element.37.refs_0_, ...), custom_call_target="tpu_custom_call" | custom-call | tf_op jit(solution)/shard_map/pallas_call | solution.py:640
  226.1 14.2 %shard_map.208 = (bf16[512,512]{1,0:T(8,128)(2,1)}, bf16[64,512]{1,0:T(8,128)(2,1)}, bf16[64,192,128]{2,1,0:T(8,128)(2,1)}, bf16[64,192,128]{2,1,0:T(8,128)(2,1)...) custom-call(bf16[512,512]{1,0:T(8,128)(2,1)} %get-tuple-element.47.r, ...), custom_call_target="tpu_custom_call" | custom-call | tf_op jit(solution)/shard_map/pallas_call | solution.py:676
